TPU v7x, 32 devices: a whole 2x2x4 slice. The times are simulated.
32 devices in a mesh: dp: 4 (over x, core), tensor: 8 (over z, y).
Axes of the slice: x: 2, y: 2, z: 4, core: 2. Of those that a mesh axis runs over, the one named last changes fastest.
Arguments:
- tokens: bfloat16 [2, 4, 1024, 1024], P(None, 'dp', 'tensor'), may hold values from -6 to 6
- resets: int32 [2, 4, 1024], P(None, 'dp', 'tensor'), may hold values from 0 to 1, as said below
- out_grads: bfloat16 [2, 4, 1024, 1024], P(None, 'dp', 'tensor'), may hold values from -6 to 6
- mixer_key: bfloat16 [1024, 1024], P(('dp', 'tensor')), may hold values from -0.1875 to 0.1875
- mixer_value: bfloat16 [1024, 1024], P(('dp', 'tensor')), may hold values from -0.1875 to 0.1875
- mixer_recept: bfloat16 [1024, 1024], P(('dp', 'tensor')), may hold values from -0.1875 to 0.1875
- mixer_output: bfloat16 [1024, 1024], P(('dp', 'tensor')), may hold values from -1.5 to 1.5
- feed_recept: bfloat16 [1024, 1024], P(('dp', 'tensor')), may hold values from -0.1875 to 0.1875
- feed_key: bfloat16 [4096, 1024], P('tensor'), may hold values from -0.1875 to 0.1875
- feed_value: bfloat16 [4096, 1024], P('tensor'), may hold values from -0.09375 to 0.09375
- first_gain: bfloat16 [1024], P(('dp', 'tensor')), may hold values from 0.099609375 to 1.8984375
- first_bias: bfloat16 [1024], P(('dp', 'tensor')), may hold values from -3 to 3
- second_gain: bfloat16 [1024], P(('dp', 'tensor')), may hold values from 0.099609375 to 1.8984375
- second_bias: bfloat16 [1024], P(('dp', 'tensor')), may hold values from -3 to 3
- mixing_key: bfloat16 [1024], P(('dp', 'tensor')), may hold values from 0.049804688 to 0.94921875
- mixing_value: bfloat16 [1024], P(('dp', 'tensor')), may hold values from 0.049804688 to 0.94921875
- mixing_recept: bfloat16 [1024], P(('dp', 'tensor')), may hold values from 0.049804688 to 0.94921875
- time_decay: bfloat16 [1024], P(('dp', 'tensor')), as said below
- time_first: bfloat16 [1024], P(('dp', 'tensor')), may hold values from -0.5 to 1.5
- feeding_key: bfloat16 [1024], P(('dp', 'tensor')), may hold values from 0.049804688 to 0.94921875
- feeding_recept: bfloat16 [1024], P(('dp', 'tensor')), may hold values from 0.049804688 to 0.94921875
Outputs:
- result: float32 [2, 4, 1024, 1024], P(None, 'dp', 'tensor')
- token_grads: float32 [2, 4, 1024, 1024], P(None, 'dp', 'tensor')
- mixer_key_grad: float32 [1024, 1024], P(('dp', 'tensor'))
- mixer_value_grad: float32 [1024, 1024], P(('dp', 'tensor'))
- mixer_recept_grad: float32 [1024, 1024], P(('dp', 'tensor'))
- mixer_output_grad: float32 [1024, 1024], P(('dp', 'tensor'))
- feed_recept_grad: float32 [1024, 1024], P(('dp', 'tensor'))
- feed_key_grad: float32 [4096, 1024], P('tensor')
- feed_value_grad: float32 [4096, 1024], P('tensor')
- first_gain_grad: float32 [1024], P(('dp', 'tensor'))
- first_bias_grad: float32 [1024], P(('dp', 'tensor'))
- second_gain_grad: float32 [1024], P(('dp', 'tensor'))
- second_bias_grad: float32 [1024], P(('dp', 'tensor'))
- mixing_key_grad: float32 [1024], P(('dp', 'tensor'))
- mixing_value_grad: float32 [1024], P(('dp', 'tensor'))
- mixing_recept_grad: float32 [1024], P(('dp', 'tensor'))
- time_decay_grad: float32 [1024], P(('dp', 'tensor'))
- time_first_grad: float32 [1024], P(('dp', 'tensor'))
- feeding_key_grad: float32 [1024], P(('dp', 'tensor'))
- feeding_recept_grad: float32 [1024], P(('dp', 'tensor'))
Inputs may be any that keep to these rules, and one draw needn't show every extreme that they name: `resets`: the first token of every row is 1; further document starts fall anywhere. exp(time_decay) lies between 0.05 / 1024 and 0.25.
All inputs are finite; a program needn't handle non-finite values.
Results may differ from a plain program's by a relative error of at most 0.012.
Values may be sent and summed in bfloat16 or wider, within the bound.
A program may use at most 320 MiB of HBM per device.

v0:
```python
import jax
import jax.numpy as jnp
from jax import lax
from jax.sharding import PartitionSpec as P

EPSILON = 1e-05


def entering(shard, axis, combine, identity, reverse):
    size, here = (lax.axis_size(axis), lax.axis_index(axis))
    everything = jax.tree.map(lambda part: lax.all_gather(part, axis), shard)
    start = jax.tree.map(
        lambda part, zero: jnp.broadcast_to(jnp.asarray(zero, part.dtype), part.shape),
        shard,
        identity,
    )

    def turn(k, before):
        at = size - 1 - k if reverse else k
        reached = at > here if reverse else at < here
        new = combine(before, jax.tree.map(lambda part: part[at], everything))
        return jax.tree.map(lambda a, b: jnp.where(reached, a, b), new, before)

    return lax.fori_loop(0, size, turn, start)


def shifted(block, axis, distance):
    devices = range(lax.axis_size(axis))
    route = [(i - distance, i) for i in devices if i - distance in devices]
    return lax.ppermute(block, axis, route)


def norm_rows(payload_series, gain, bias):
    center = payload_series - jnp.mean(payload_series, axis=-1, keepdims=True)
    inverse = lax.rsqrt(jnp.mean(center * center, axis=-1, keepdims=True) + EPSILON)
    normed = center * inverse
    return (normed * gain + bias, normed, inverse)


def norm_back(grad_out, normed, inverse, gain):
    scaled = grad_out * gain
    centred = scaled - jnp.mean(scaled, axis=-1, keepdims=True)
    grad_in = inverse * (centred - normed * jnp.mean(scaled * normed, axis=-1, keepdims=True))
    return (grad_in, jnp.sum(grad_out * normed, axis=0), jnp.sum(grad_out, axis=0))


def affine(earlier, later):
    return (
        earlier[0] * later[0],
        later[0] * earlier[1] + later[1],
        later[0] * earlier[2] + later[2],
    )


def carry_across(summary, backward):
    width = summary[0].shape[0]
    identity = (
        jnp.ones((width,), jnp.float32),
        jnp.zeros((width,), jnp.float32),
        jnp.zeros((width,), jnp.float32),
    )
    return entering(summary, "tensor", affine, identity, backward)


def matmul(left, right):
    return jnp.dot(left, right, preferred_element_type=jnp.float32)


def matmul_lead(left, right):
    return lax.dot_general(
        left, right, (((0,), (0,)), ((), ())), preferred_element_type=jnp.float32
    )


def matmul_last(left, right):
    return lax.dot_general(
        left, right, (((1,), (1,)), ((), ())), preferred_element_type=jnp.float32
    )


def shards(
    tokens,
    resets,
    out_grads,
    mixer_key,
    mixer_value,
    mixer_recept,
    mixer_output,
    feed_recept,
    feed_key,
    feed_value,
    first_gain,
    first_bias,
    second_gain,
    second_bias,
    mixing_key,
    mixing_value,
    mixing_recept,
    time_decay,
    time_first,
    feeding_key,
    feeding_recept,
):
    gathered = (
        lax.all_gather(mixer_key, ("dp", "tensor"), axis=0, tiled=True),
        lax.all_gather(mixer_value, ("dp", "tensor"), axis=0, tiled=True),
        lax.all_gather(mixer_recept, ("dp", "tensor"), axis=0, tiled=True),
        lax.all_gather(mixer_output, ("dp", "tensor"), axis=0, tiled=True),
        lax.all_gather(feed_recept, ("dp", "tensor"), axis=0, tiled=True),
        lax.all_gather(first_gain, ("dp", "tensor"), axis=0, tiled=True),
        lax.all_gather(first_bias, ("dp", "tensor"), axis=0, tiled=True),
        lax.all_gather(second_gain, ("dp", "tensor"), axis=0, tiled=True),
        lax.all_gather(second_bias, ("dp", "tensor"), axis=0, tiled=True),
        lax.all_gather(mixing_key, ("dp", "tensor"), axis=0, tiled=True),
        lax.all_gather(mixing_value, ("dp", "tensor"), axis=0, tiled=True),
        lax.all_gather(mixing_recept, ("dp", "tensor"), axis=0, tiled=True),
        lax.all_gather(time_decay, ("dp", "tensor"), axis=0, tiled=True),
        lax.all_gather(time_first, ("dp", "tensor"), axis=0, tiled=True),
        lax.all_gather(feeding_key, ("dp", "tensor"), axis=0, tiled=True),
        lax.all_gather(feeding_recept, ("dp", "tensor"), axis=0, tiled=True),
    )
    w_key, w_value, w_recept, w_output, w_feedr = (
        gathered[0],
        gathered[1],
        gathered[2],
        gathered[3],
        gathered[4],
    )
    parameter_vectors = [piece.astype(jnp.float32) for piece in gathered[5:]]
    gain_one, bias_one, gain_two, bias_two = (
        parameter_vectors[0],
        parameter_vectors[1],
        parameter_vectors[2],
        parameter_vectors[3],
    )
    mix_key, mix_value, mix_recept = (
        parameter_vectors[4],
        parameter_vectors[5],
        parameter_vectors[6],
    )
    (
        fading_speed_logarithm,
        opening_premium_logarithm,
        channel_lookup_blend,
        channel_gating_blend,
    ) = (parameter_vectors[7], parameter_vectors[8], parameter_vectors[9], parameter_vectors[10])
    rates = jnp.exp(fading_speed_logarithm)
    fading_multiplier = jnp.exp(-rates)
    micro_count = tokens.shape[0]
    width = tokens.shape[3]
    grad_keyw = jnp.zeros(feed_key.shape, jnp.float32)
    grad_valuew = jnp.zeros(feed_value.shape, jnp.float32)
    square_grads = [jnp.zeros((width, width), jnp.float32) for index_one in range(5)]
    parameter_vector_gradients = [jnp.zeros((width,), jnp.float32) for index_two in range(11)]
    results = []
    input_grads = []
    for micro_index in range(micro_count):
        inputs = tokens[micro_index, 0].astype(jnp.float32)
        restart_retain_flags = (1 - resets[micro_index, 0]).astype(jnp.float32)[:, None]
        cotangent = out_grads[micro_index, 0].astype(jnp.float32)
        normed_one, unit_one, inverse_one = norm_rows(inputs, gain_one, bias_one)
        z_one = normed_one.astype(jnp.bfloat16)
        prior_one = shifted(z_one[-1:], "tensor", 1)
        before_one = (
            jnp.concatenate([prior_one, z_one[:-1]], axis=0).astype(jnp.float32)
            * restart_retain_flags
        )
        z_onef = z_one.astype(jnp.float32)
        in_key = (z_onef * mix_key + before_one * (1.0 - mix_key)).astype(jnp.bfloat16)
        in_value = (z_onef * mix_value + before_one * (1.0 - mix_value)).astype(jnp.bfloat16)
        in_recept = (z_onef * mix_recept + before_one * (1.0 - mix_recept)).astype(jnp.bfloat16)
        lookup_series = matmul(in_key, w_key)
        payload_series = matmul(in_value, w_value)
        recept = jax.nn.sigmoid(matmul(in_recept, w_recept))
        powered_lookup = jnp.exp(lookup_series)
        premium_plus_lookup = jnp.exp(opening_premium_logarithm + lookup_series)
        factor = restart_retain_flags * fading_multiplier
        cum_factor, local_a, local_b = lax.associative_scan(
            affine, (factor, powered_lookup * payload_series, powered_lookup), axis=0
        )
        incoming = carry_across((cum_factor[-1], local_a[-1], local_b[-1]), False)
        upper_running_state = local_a + cum_factor * incoming[1]
        lower_running_state = local_b + cum_factor * incoming[2]
        earlier_upper_state = jnp.concatenate([incoming[1][None], upper_running_state[:-1]], axis=0)
        earlier_lower_state = jnp.concatenate([incoming[2][None], lower_running_state[:-1]], axis=0)
        lower_quotient_part = restart_retain_flags * earlier_lower_state + premium_plus_lookup
        blended = (
            restart_retain_flags * earlier_upper_state + premium_plus_lookup * payload_series
        ) / lower_quotient_part
        weighted = (recept * blended).astype(jnp.bfloat16)
        residual = inputs + matmul(weighted, w_output)
        normed_two, unit_two, inverse_two = norm_rows(residual, gain_two, bias_two)
        z_two = normed_two.astype(jnp.bfloat16)
        prior_two = shifted(z_two[-1:], "tensor", 1)
        before_two = (
            jnp.concatenate([prior_two, z_two[:-1]], axis=0).astype(jnp.float32)
            * restart_retain_flags
        )
        z_twof = z_two.astype(jnp.float32)
        feed_in = (
            z_twof * channel_lookup_blend + before_two * (1.0 - channel_lookup_blend)
        ).astype(jnp.bfloat16)
        feed_rin = (
            z_twof * channel_gating_blend + before_two * (1.0 - channel_gating_blend)
        ).astype(jnp.bfloat16)
        gate = jax.nn.sigmoid(matmul(feed_rin, w_feedr))
        all_in = lax.all_gather(feed_in, "tensor", axis=0, tiled=True)
        hidden_pre = matmul_last(feed_key, all_in)
        hidden = jnp.square(jnp.maximum(hidden_pre, 0.0)).astype(jnp.bfloat16)
        value_out = lax.psum_scatter(
            matmul_lead(hidden, feed_value), "tensor", scatter_dimension=0, tiled=True
        )
        results.append(residual + gate * value_out)
        grad_value = (cotangent * gate).astype(jnp.bfloat16)
        grad_gate = (cotangent * value_out * gate * (1.0 - gate)).astype(jnp.bfloat16)
        square_grads[4] = square_grads[4] + matmul_lead(feed_rin, grad_gate)
        grad_rin = matmul_last(grad_gate, w_feedr)
        relu_twice = 2.0 * jnp.maximum(hidden_pre, 0.0)
        add_piece = lax.all_gather(grad_value, "tensor", axis=0, tiled=True)
        rows_total = matmul(hidden, add_piece)
        block = matmul_last(feed_value, add_piece)
        grad_valuew = grad_valuew + rows_total
        grad_pre = (block * relu_twice).astype(jnp.bfloat16)
        grad_keyw = grad_keyw + matmul(grad_pre, all_in)
        grad_in = lax.psum_scatter(
            matmul_lead(grad_pre, feed_key), "tensor", scatter_dimension=0, tiled=True
        )
        parameter_vector_gradients[9] = parameter_vector_gradients[9] + jnp.sum(
            grad_in * (z_twof - before_two), axis=0
        )
        parameter_vector_gradients[10] = parameter_vector_gradients[10] + jnp.sum(
            grad_rin * (z_twof - before_two), axis=0
        )
        shift_two = restart_retain_flags * (
            grad_in * (1.0 - channel_lookup_blend) + grad_rin * (1.0 - channel_gating_blend)
        )
        after_two = shifted(shift_two[:1], "tensor", -1)
        grad_z_two = (
            grad_in * channel_lookup_blend
            + grad_rin * channel_gating_blend
            + jnp.concatenate([shift_two[1:], after_two], axis=0)
        )
        back_two, gain_part, bias_part = norm_back(grad_z_two, unit_two, inverse_two, gain_two)
        parameter_vector_gradients[2] = parameter_vector_gradients[2] + gain_part
        parameter_vector_gradients[3] = parameter_vector_gradients[3] + bias_part
        grad_residual = cotangent + back_two
        grad_att = grad_residual.astype(jnp.bfloat16)
        square_grads[3] = square_grads[3] + matmul_lead(weighted, grad_att)
        grad_weighted = matmul_last(grad_att, w_output)
        grad_mixed = grad_weighted * recept
        grad_recept = (grad_weighted * blended * recept * (1.0 - recept)).astype(jnp.bfloat16)
        upper_adjoint = grad_mixed / lower_quotient_part
        denominator_gradient = -grad_mixed * blended / lower_quotient_part
        cum_back, local_xa, local_xb = lax.associative_scan(
            affine,
            (
                factor,
                restart_retain_flags * upper_adjoint,
                restart_retain_flags * denominator_gradient,
            ),
            reverse=True,
            axis=0,
        )
        beyond = carry_across((cum_back[0], local_xa[0], local_xb[0]), True)
        adjoint_a = local_xa + cum_back * beyond[1]
        adjoint_b = local_xb + cum_back * beyond[2]
        running_upper_total = jnp.concatenate([adjoint_a[1:], beyond[1][None]], axis=0)
        running_lower_total = jnp.concatenate([adjoint_b[1:], beyond[2][None]], axis=0)
        premium_power = premium_plus_lookup * (
            payload_series * upper_adjoint + denominator_gradient
        )
        adjoint_payloads = (
            premium_plus_lookup * upper_adjoint + powered_lookup * running_upper_total
        ).astype(jnp.bfloat16)
        key_gradient_rows = (
            premium_power
            + powered_lookup * (payload_series * running_upper_total + running_lower_total)
        ).astype(jnp.bfloat16)
        parameter_vector_gradients[8] = parameter_vector_gradients[8] + jnp.sum(
            premium_power, axis=0
        )
        decay_sum = jnp.sum(
            restart_retain_flags
            * (
                running_upper_total * earlier_upper_state
                + running_lower_total * earlier_lower_state
            ),
            axis=0,
        )
        parameter_vector_gradients[7] = (
            parameter_vector_gradients[7] - rates * fading_multiplier * decay_sum
        )
        square_grads[0] = square_grads[0] + matmul_lead(in_key, key_gradient_rows)
        square_grads[1] = square_grads[1] + matmul_lead(in_value, adjoint_payloads)
        square_grads[2] = square_grads[2] + matmul_lead(in_recept, grad_recept)
        grad_inkey = matmul_last(key_gradient_rows, w_key)
        grad_invalue = matmul_last(adjoint_payloads, w_value)
        grad_inrecept = matmul_last(grad_recept, w_recept)
        spread_one = z_onef - before_one
        parameter_vector_gradients[4] = parameter_vector_gradients[4] + jnp.sum(
            grad_inkey * spread_one, axis=0
        )
        parameter_vector_gradients[5] = parameter_vector_gradients[5] + jnp.sum(
            grad_invalue * spread_one, axis=0
        )
        parameter_vector_gradients[6] = parameter_vector_gradients[6] + jnp.sum(
            grad_inrecept * spread_one, axis=0
        )
        shift_one = restart_retain_flags * (
            grad_inkey * (1.0 - mix_key)
            + grad_invalue * (1.0 - mix_value)
            + grad_inrecept * (1.0 - mix_recept)
        )
        after_one = shifted(shift_one[:1], "tensor", -1)
        grad_z_one = (
            grad_inkey * mix_key
            + grad_invalue * mix_value
            + grad_inrecept * mix_recept
            + jnp.concatenate([shift_one[1:], after_one], axis=0)
        )
        back_one, gain_first, bias_first = norm_back(grad_z_one, unit_one, inverse_one, gain_one)
        parameter_vector_gradients[0] = parameter_vector_gradients[0] + gain_first
        parameter_vector_gradients[1] = parameter_vector_gradients[1] + bias_first
        input_grads.append(grad_residual + back_one)
    owned = (
        lax.psum_scatter(square_grads[0], ("dp", "tensor"), scatter_dimension=0, tiled=True),
        lax.psum_scatter(square_grads[1], ("dp", "tensor"), scatter_dimension=0, tiled=True),
        lax.psum_scatter(square_grads[2], ("dp", "tensor"), scatter_dimension=0, tiled=True),
        lax.psum_scatter(square_grads[3], ("dp", "tensor"), scatter_dimension=0, tiled=True),
        lax.psum_scatter(square_grads[4], ("dp", "tensor"), scatter_dimension=0, tiled=True),
        lax.psum_scatter(
            parameter_vector_gradients[0], ("dp", "tensor"), scatter_dimension=0, tiled=True
        ),
        lax.psum_scatter(
            parameter_vector_gradients[1], ("dp", "tensor"), scatter_dimension=0, tiled=True
        ),
        lax.psum_scatter(
            parameter_vector_gradients[2], ("dp", "tensor"), scatter_dimension=0, tiled=True
        ),
        lax.psum_scatter(
            parameter_vector_gradients[3], ("dp", "tensor"), scatter_dimension=0, tiled=True
        ),
        lax.psum_scatter(
            parameter_vector_gradients[4], ("dp", "tensor"), scatter_dimension=0, tiled=True
        ),
        lax.psum_scatter(
            parameter_vector_gradients[5], ("dp", "tensor"), scatter_dimension=0, tiled=True
        ),
        lax.psum_scatter(
            parameter_vector_gradients[6], ("dp", "tensor"), scatter_dimension=0, tiled=True
        ),
        lax.psum_scatter(
            parameter_vector_gradients[7], ("dp", "tensor"), scatter_dimension=0, tiled=True
        ),
        lax.psum_scatter(
            parameter_vector_gradients[8], ("dp", "tensor"), scatter_dimension=0, tiled=True
        ),
        lax.psum_scatter(
            parameter_vector_gradients[9], ("dp", "tensor"), scatter_dimension=0, tiled=True
        ),
        lax.psum_scatter(
            parameter_vector_gradients[10], ("dp", "tensor"), scatter_dimension=0, tiled=True
        ),
    )
    key_rows, value_rows_grad = (grad_keyw, grad_valuew)
    key_total, value_total = (
        lax.psum(key_rows.astype(jnp.bfloat16), "dp").astype(jnp.float32),
        lax.psum(value_rows_grad.astype(jnp.bfloat16), "dp").astype(jnp.float32),
    )
    result_all = jnp.stack(results)[:, None]
    grads_all = jnp.stack(input_grads)[:, None]
    return (
        result_all,
        grads_all,
        owned[0],
        owned[1],
        owned[2],
        owned[3],
        owned[4],
        key_total,
        value_total,
        owned[5],
        owned[6],
        owned[7],
        owned[8],
        owned[9],
        owned[10],
        owned[11],
        owned[12],
        owned[13],
        owned[14],
        owned[15],
    )


def solution(mesh):
    return jax.shard_map(
        shards,
        mesh=mesh,
        in_specs=(
            P(None, "dp", "tensor", None),
            P(None, "dp", "tensor"),
            P(None, "dp", "tensor", None),
            P(("dp", "tensor"), None),
            P(("dp", "tensor"), None),
            P(("dp", "tensor"), None),
            P(("dp", "tensor"), None),
            P(("dp", "tensor"), None),
            P("tensor", None),
            P("tensor", None),
            P(("dp", "tensor")),
            P(("dp", "tensor")),
            P(("dp", "tensor")),
            P(("dp", "tensor")),
            P(("dp", "tensor")),
            P(("dp", "tensor")),
            P(("dp", "tensor")),
            P(("dp", "tensor")),
            P(("dp", "tensor")),
            P(("dp", "tensor")),
            P(("dp", "tensor")),
        ),
        out_specs=(
            P(None, "dp", "tensor", None),
            P(None, "dp", "tensor", None),
            P(("dp", "tensor"), None),
            P(("dp", "tensor"), None),
            P(("dp", "tensor"), None),
            P(("dp", "tensor"), None),
            P(("dp", "tensor"), None),
            P("tensor", None),
            P("tensor", None),
            P(("dp", "tensor")),
            P(("dp", "tensor")),
            P(("dp", "tensor")),
            P(("dp", "tensor")),
            P(("dp", "tensor")),
            P(("dp", "tensor")),
            P(("dp", "tensor")),
            P(("dp", "tensor")),
            P(("dp", "tensor")),
            P(("dp", "tensor")),
            P(("dp", "tensor")),
        ),
        check_vma=False,
    )
```

profile of v0, /device:TPU:0, one launch (start us, length us, event | category | flops | bytes accessed | tf_op | source)
XLA Modules:
  0.0 2240.6 jit_solution(16272673379080011755)
XLA Ops:
  18.7 43.1 %all-reduce.191 = (bf16[1024]{0:T(1024)(128)(2,1)S(1)}, bf16[1024]{0:T(1024)(128)(2,1)S(1)}, bf16[1024]{0:T(1024)(128)(2,1)S(1)}, bf16[1024]{0:T(1024)(128)(2,1)...) all-reduce(bf16[1024]{0:T(1024)(128)(2,1)S(1)} %dynamic-update-slic, ...), channel_id=1, replica_groups=mesh['dp'=4,'tensor'=8] {'dp','tensor'}, use_global_device_ids=true, to_apply=%add.169 | all-reduce | flops 11264 | bytes 45056
  84.3 44.3 %all-gather.26.cloned.1.call-done = bf16[1024,1024]{1,0:T(8,128)(2,1)} async-done(((bf16[32,1024]{1,0:T(8,128)(2,1)}), bf16[1024,1024]{1,0:T(8,128)(2,1)}) %all-gather.26.cloned.1.call-update) | async-done | bytes 2097168 | tf_op jit(solution)/shard_map/all_gather | solution.py:106
  241.6 30.8 %all-gather.3 = f32[8,1,1024]{2,1,0:T(1,128)S(1)} all-gather(f32[1,1,1024]{2,1,0:T(1,128)S(1)} %add_bitcast_fusion.10), channel_id=1, replica_groups=mesh['dp'=4,'tensor'=8] {'tensor'}, dimensions={0}, use_global_device_ids=true | all-gather | bytes 36864 | tf_op jit(solution)/shard_map/all_gather | solution.py:11
  304.7 30.6 %all-gather.4 = f32[8,1,1024]{2,1,0:T(1,128)S(1)} all-gather(f32[1,1,1024]{2,1,0:T(1,128)S(1)} %add_bitcast_fusion.9), channel_id=1, replica_groups=mesh['dp'=4,'tensor'=8] {'tensor'}, dimensions={0}, use_global_device_ids=true | all-gather | bytes 36864 | tf_op jit(solution)/shard_map/all_gather | solution.py:11
  343.7 30.6 %all-gather = f32[8,1,1024]{2,1,0:T(1,128)S(1)} all-gather(f32[1,1,1024]{2,1,0:T(1,128)S(1)} %add_bitcast_fusion.13), channel_id=1, replica_groups=mesh['dp'=4,'tensor'=8] {'tensor'}, dimensions={0}, use_global_device_ids=true | all-gather | bytes 36864 | tf_op jit(solution)/shard_map/all_gather | solution.py:11
  375.1 30.6 %all-gather.2 = f32[8,1,1024]{2,1,0:T(1,128)S(1)} all-gather(f32[1,1,1024]{2,1,0:T(1,128)S(1)} %add_bitcast_fusion.11), channel_id=1, replica_groups=mesh['dp'=4,'tensor'=8] {'tensor'}, dimensions={0}, use_global_device_ids=true | all-gather | bytes 36864 | tf_op jit(solution)/shard_map/all_gather | solution.py:11
  406.5 30.6 %all-gather.1 = f32[8,1,1024]{2,1,0:T(1,128)S(1)} all-gather(f32[1,1,1024]{2,1,0:T(1,128)S(1)} %add_bitcast_fusion.12), channel_id=1, replica_groups=mesh['dp'=4,'tensor'=8] {'tensor'}, dimensions={0}, use_global_device_ids=true | all-gather | bytes 36864 | tf_op jit(solution)/shard_map/all_gather | solution.py:11
  463.5 50.0 %all-gather.32.cloned.1.call-done = bf16[1024,1024]{1,0:T(8,128)(2,1)} async-done(((bf16[128,1024]{1,0:T(8,128)(2,1)}), bf16[1024,1024]{1,0:T(8,128)(2,1)}) %all-gather.32.cloned.1.call-update) | async-done | bytes 2097168 | tf_op jit(solution)/shard_map/all_gather | solution.py:207
  521.3 42.4 %all-gather.34.cloned.1.call-done = bf16[1024,1024]{1,0:T(8,128)(2,1)} async-done(((bf16[128,1024]{1,0:T(8,128)(2,1)}), bf16[1024,1024]{1,0:T(8,128)(2,1)}) %all-gather.34.cloned.1.call-update) | async-done | bytes 2097168 | tf_op jit(solution)/shard_map/all_gather | solution.py:207
  572.1 49.5 %all-gather.30.cloned.1.call-done = bf16[1024,1024]{1,0:T(8,128)(2,1)} async-done(((bf16[32,1024]{1,0:T(8,128)(2,1)}), bf16[1024,1024]{1,0:T(8,128)(2,1)}) %all-gather.30.cloned.1.call-update) | async-done | bytes 2097168 | tf_op jit(solution)/shard_map/all_gather | solution.py:109
  624.8 87.6 %reduce-scatter.10.cloned.1.call-done = f32[128,1024]{1,0:T(8,128)} async-done(((f32[1024,1024]{1,0:T(8,128)}), f32[128,1024]{1,0:T(8,128)}) %reduce-scatter.10.cloned.1.call-update) | async-done | bytes 524304 | tf_op jit(solution)/shard_map/reduce_scatter | solution.py:210
  712.4 91.7 %reduce-scatter.12.cloned.1.call-done = f32[128,1024]{1,0:T(8,128)} async-done(((f32[1024,1024]{1,0:T(8,128)}), f32[128,1024]{1,0:T(8,128)}) %reduce-scatter.12.cloned.1.call-update) | async-done | bytes 524304 | tf_op jit(solution)/shard_map/reduce_scatter | solution.py:210
  809.0 48.1 %all-gather.38.cloned.1.call-done = bf16[1024,1024]{1,0:T(8,128)(2,1)} async-done(((bf16[128,1024]{1,0:T(8,128)(2,1)}), bf16[1024,1024]{1,0:T(8,128)(2,1)}) %all-gather.38.cloned.1.call-update) | async-done | bytes 2097168 | tf_op jit(solution)/shard_map/all_gather | solution.py:219
  865.0 41.9 %all-gather.36.cloned.1.call-done = bf16[1024,1024]{1,0:T(8,128)(2,1)} async-done(((bf16[128,1024]{1,0:T(8,128)(2,1)}), bf16[1024,1024]{1,0:T(8,128)(2,1)}) %all-gather.36.cloned.1.call-update) | async-done | bytes 2097168 | tf_op jit(solution)/shard_map/all_gather | solution.py:219
  956.0 41.2 %reduce-scatter.16.cloned.1.call-done = f32[128,1024]{1,0:T(8,128)} async-done(((f32[1024,1024]{1,0:T(8,128)}), f32[128,1024]{1,0:T(8,128)}) %reduce-scatter.16.cloned.1.call-update) | async-done | bytes 524304 | tf_op jit(solution)/shard_map/reduce_scatter | solution.py:225
  997.2 91.6 %reduce-scatter.14.cloned.1.call-done = f32[128,1024]{1,0:T(8,128)} async-done(((f32[1024,1024]{1,0:T(8,128)}), f32[128,1024]{1,0:T(8,128)}) %reduce-scatter.14.cloned.1.call-update) | async-done | bytes 524304 | tf_op jit(solution)/shard_map/reduce_scatter | solution.py:225
  1346.9 33.6 %all-gather.11 = f32[8,1,1024]{2,1,0:T(1,128)S(1)} all-gather(f32[1,1,1024]{2,1,0:T(1,128)S(1)} %add_bitcast_fusion.2), channel_id=1, replica_groups=mesh['dp'=4,'tensor'=8] {'tensor'}, dimensions={0}, use_global_device_ids=true | all-gather | bytes 36864 | tf_op jit(solution)/shard_map/all_gather | solution.py:11
  1391.4 30.6 %all-gather.9 = f32[8,1,1024]{2,1,0:T(1,128)S(1)} all-gather(f32[1,1,1024]{2,1,0:T(1,128)S(1)} %add_bitcast_fusion.4), channel_id=1, replica_groups=mesh['dp'=4,'tensor'=8] {'tensor'}, dimensions={0}, use_global_device_ids=true | all-gather | bytes 36864 | tf_op jit(solution)/shard_map/all_gather | solution.py:11
  1432.7 30.8 %all-gather.10 = f32[8,1,1024]{2,1,0:T(1,128)S(1)} all-gather(f32[1,1,1024]{2,1,0:T(1,128)S(1)} %add_bitcast_fusion.3), channel_id=1, replica_groups=mesh['dp'=4,'tensor'=8] {'tensor'}, dimensions={0}, use_global_device_ids=true | all-gather | bytes 36864 | tf_op jit(solution)/shard_map/all_gather | solution.py:11
  1709.2 43.9 %all-reduce.190 = (f32[1024]{0:T(1024)S(1)}, f32[1024]{0:T(1024)S(1)}, f32[1024]{0:T(1024)S(1)}, f32[1024]{0:T(1024)S(1)}, f32[1024]{0:T(1024)S(1)}, /*index=5*/...) all-reduce(f32[1024]{0:T(1024)S(1)} %add.1693, ...), channel_id=11, replica_groups=mesh['dp'=4,'tensor'=8] {'dp','tensor'}, use_global_device_ids=true, to_apply=%region_37.38.clone | all-reduce | flops 11264 | bytes 90112
  1762.2 33.7 %reduce-scatter.24.cloned.1.call-done = f32[32,1024]{1,0:T(8,128)} async-done(((f32[1024,1024]{1,0:T(8,128)}), f32[32,1024]{1,0:T(8,128)}) %reduce-scatter.24.cloned.1.call-update) | async-done | bytes 131088 | tf_op jit(solution)/shard_map/reduce_scatter | solution.py:329
  1795.9 146.3 %reduce-scatter.20.cloned.1.call-done = f32[32,1024]{1,0:T(8,128)} async-done(((f32[1024,1024]{1,0:T(8,128)}), f32[32,1024]{1,0:T(8,128)}) %reduce-scatter.20.cloned.1.call-update) | async-done | bytes 131088 | tf_op jit(solution)/shard_map/reduce_scatter | solution.py:327
  1942.1 145.4 %reduce-scatter.22.cloned.1.call-done = f32[32,1024]{1,0:T(8,128)} async-done(((f32[1024,1024]{1,0:T(8,128)}), f32[32,1024]{1,0:T(8,128)}) %reduce-scatter.22.cloned.1.call-update) | async-done | bytes 131088 | tf_op jit(solution)/shard_map/reduce_scatter | solution.py:328
  2087.5 146.1 %reduce-scatter.18.cloned.1.call-done = f32[32,1024]{1,0:T(8,128)} async-done(((f32[1024,1024]{1,0:T(8,128)}), f32[32,1024]{1,0:T(8,128)}) %reduce-scatter.18.cloned.1.call-update) | async-done | bytes 131088 | tf_op jit(solution)/shard_map/reduce_scatter | solution.py:326
  (1450 shorter events, 839.7 us)
Async XLA Ops:
  7.2 74.9 %all-gather.24.cloned.1.call-start = ((), (), s32[]{:S(2)}) async-start(), calls=%async_computation.10 | async-start | bytes 2162688 | tf_op jit(solution)/shard_map/all_gather | solution.py:105
  8.0 120.7 %all-gather.26.cloned.1.call-start = ((), (), s32[]{:S(2)}) async-start(), calls=%async_computation.11 | async-start | bytes 2162688 | tf_op jit(solution)/shard_map/all_gather | solution.py:106
  8.7 436.2 %all-gather.22.cloned.1.call-start = ((), (), s32[]{:S(2)}) async-start(), calls=%async_computation.9 | async-start | bytes 2162688 | tf_op jit(solution)/shard_map/all_gather | solution.py:107
  9.4 442.4 %all-gather.28.cloned.1.call-start = ((), (), s32[]{:S(2)}) async-start(), calls=%async_computation.12 | async-start | bytes 2162688 | tf_op jit(solution)/shard_map/all_gather | solution.py:108
  65.7 16.4 collective-permute-start.2
  70.2 100.2 %collective-permute-start = (bf16[1,1024]{1,0:T(2,128)(2,1)}, bf16[1,1024]{1,0:T(2,128)(2,1)}, u32[]{:S(2)}, u32[]{:S(2)}) collective-permute-start(bf16[1,1024]{1,0:T(2,128)(2,1)} %slice.1824), channel_id=1, source_target_pairs={{0,1},{1,2},{2,3},{3,4},{4,5},{5,6},{6,7},{8,9},{9,10},{10,11},{11... | collective-permute-start | bytes 6152 | tf_op jit(solution)/shard_map/ppermute | solution.py:30
  73.8 439.7 %all-gather.32.cloned.1.call-start = ((), (), s32[]{:S(2)}) async-start(), calls=%async_computation.14 | async-start | bytes 2359296 | tf_op jit(solution)/shard_map/all_gather | solution.py:207
  462.1 101.6 %all-gather.34.cloned.1.call-start = ((), (), s32[]{:S(2)}) async-start(), calls=%async_computation.16 | async-start | bytes 2359296 | tf_op jit(solution)/shard_map/all_gather | solution.py:207
  462.7 158.9 %all-gather.30.cloned.1.call-start = ((), (), s32[]{:S(2)}) async-start(), calls=%async_computation.13 | async-start | bytes 2162688 | tf_op jit(solution)/shard_map/all_gather | solution.py:109
  463.4 248.9 %reduce-scatter.10.cloned.1.call-start = ((), (), s32[]{:S(2)}) async-start(), calls=%async_computation.15 | async-start | bytes 4718592 | tf_op jit(solution)/shard_map/reduce_scatter | solution.py:210
  521.2 282.8 %reduce-scatter.12.cloned.1.call-start = ((), (), s32[]{:S(2)}) async-start(), calls=%async_computation.17 | async-start | bytes 4718592 | tf_op jit(solution)/shard_map/reduce_scatter | solution.py:210
  571.4 285.7 %all-gather.38.cloned.1.call-start = ((), (), s32[]{:S(2)}) async-start(), calls=%async_computation.20 | async-start | bytes 2359296 | tf_op jit(solution)/shard_map/all_gather | solution.py:219
  808.3 98.7 %all-gather.36.cloned.1.call-start = ((), (), s32[]{:S(2)}) async-start(), calls=%async_computation.18 | async-start | bytes 2359296 | tf_op jit(solution)/shard_map/all_gather | solution.py:219
  809.0 188.3 %reduce-scatter.16.cloned.1.call-start = ((), (), s32[]{:S(2)}) async-start(), calls=%async_computation.21 | async-start | bytes 4718592 | tf_op jit(solution)/shard_map/reduce_scatter | solution.py:225
  865.0 223.9 %reduce-scatter.14.cloned.1.call-start = ((), (), s32[]{:S(2)}) async-start(), calls=%async_computation.19 | async-start | bytes 4718592 | tf_op jit(solution)/shard_map/reduce_scatter | solution.py:225
  914.8 771.9 %all-reduce.195.cloned.1.call-start = ((), (), s32[]{:S(2)}) async-start(), calls=%async_computation.27 | async-start | bytes 4194304 | tf_op jit(solution)/shard_map/psum | solution.py:367
  952.6 809.5 %reduce-scatter.26.cloned.1.call-start = ((), (), s32[]{:S(2)}) async-start(), calls=%async_computation.26 | async-start | bytes 4325376 | tf_op jit(solution)/shard_map/reduce_scatter | solution.py:330
  1093.4 8.0 collective-permute-start.6
  1094.7 6.7 collective-permute-start.4
  1098.9 697.0 %reduce-scatter.24.cloned.1.call-start = ((), (), s32[]{:S(2)}) async-start(), calls=%async_computation.25 | async-start | bytes 4325376 | tf_op jit(solution)/shard_map/reduce_scatter | solution.py:329
  1649.5 292.6 %reduce-scatter.20.cloned.1.call-start = ((), (), s32[]{:S(2)}) async-start(), calls=%async_computation.23 | async-start | bytes 4325376 | tf_op jit(solution)/shard_map/reduce_scatter | solution.py:327
  1673.9 413.6 %reduce-scatter.22.cloned.1.call-start = ((), (), s32[]{:S(2)}) async-start(), calls=%async_computation.24 | async-start | bytes 4325376 | tf_op jit(solution)/shard_map/reduce_scatter | solution.py:328
  1679.1 554.5 %reduce-scatter.18.cloned.1.call-start = ((), (), s32[]{:S(2)}) async-start(), calls=%async_computation.22 | async-start | bytes 4325376 | tf_op jit(solution)/shard_map/reduce_scatter | solution.py:326
  1701.3 6.3 collective-permute-start.5
  (235 other events, 5834.9 us)
Sparse Core Ops, SparseCore 0:
  11.0 59.4 all-gather.23
  73.5 55.1 all-gather.25
  131.6 55.2 all-gather.21
  189.8 55.1 all-gather.27
  462.2 51.2 all-gather.31
  516.0 47.6 all-gather.33
  566.7 54.8 all-gather.29
  625.2 87.1 reduce-scatter.9
  716.0 87.9 reduce-scatter.11
  808.4 48.7 all-gather.37
  859.3 47.6 all-gather.35
  910.4 86.8 reduce-scatter.15
  1000.9 87.9 reduce-scatter.13
  1092.3 51.0 all-reduce.194
  1146.1 145.4 reduce-scatter.25
  1649.6 146.2 reduce-scatter.23
  1798.6 143.5 reduce-scatter.19
  1944.8 142.6 reduce-scatter.21
  2090.4 143.1 reduce-scatter.17
where the time goes:
time: 2260 us; the launch traced here: 2240 us
  waiting for transfers between devices  1070 us (47%)
  blocking collectives  458 us (20%)
  local copies, waits for them, and re-layouts  407 us (18%)
  other arithmetic  171 us (8%)
  matrix products  97.2 us (4%)
    all_gather x12, blocking collectives, entering(): everything = jax.tree.map(lambda part: lax.all_gather(part, axis), shard)  371 us
    slice x145, local copies, waits for them, and re-layouts, shards(): lax.associative_scan(affine, (factor, restart_retain_flags * upper_adjoin...  184 us
    reduce_scatter x2, waiting for transfers between devices, shards(): lax.psum_scatter(matmul_lead(hidden, feed_value), 'tensor', scatter_dimen...  179 us
    reduce_scatter x1, waiting for transfers between devices, shards(): lax.psum_scatter(square_grads[1], ('dp', 'tensor'), scatter_dimension=0,...  146 us
    reduce_scatter x1, waiting for transfers between devices, shards(): lax.psum_scatter(square_grads[0], ('dp', 'tensor'), scatter_dimension=0,...  146 us
    reduce_scatter x1, waiting for transfers between devices, shards(): lax.psum_scatter(square_grads[2], ('dp', 'tensor'), scatter_dimension=0,...  145 us
    reduce_scatter x2, waiting for transfers between devices, shards(): lax.psum_scatter(matmul_lead(grad_pre, feed_key), 'tensor', scatter_dimen...  133 us
    all_gather x2, waiting for transfers between devices, shards(): all_in = lax.all_gather(feed_in, 'tensor', axis=0, tiled=True)  92.4 us
  transfers between devices with their start and end apart: 27, of which 17 were waited for; matrix products, arithmetic and copies ran while one was open for 29% of the time, Pallas kernels for 0%

commit v1 on v0

--- a/solution.py
+++ b/solution.py
@@ -1,6 +1,10 @@
+import functools
+
 import jax
 import jax.numpy as jnp
 from jax import lax
+from jax.experimental import pallas as pl
+from jax.experimental.pallas import tpu as pltpu
 from jax.sharding import PartitionSpec as P
 
 EPSILON = 1e-05
@@ -393,9 +397,751 @@
     )
 
 
+BF = jnp.bfloat16
+F32 = jnp.float32
+BOTH = ("dp", "tensor")
+MESH_ID = pl.DeviceIdType.MESH
+DEVICES = [(x, c, z, y) for x in range(2) for c in range(2) for z in range(4) for y in range(2)]
+
+
+def flat(x, c, z, y):
+    return (x * 2 + c) * 8 + z * 2 + y
+
+
+TO_CORE = [(flat(*d), flat(d[0], 1 - d[1], d[2], d[3])) for d in DEVICES]
+TO_X = [(flat(*d), flat(1 - d[0], d[1], d[2], d[3])) for d in DEVICES]
+TO_FIRST = [(flat(x, c, z, y), flat(x, c, z, 1 - y) if c == 0 else flat(1 - x, c, z, y)) for x, c, z, y in DEVICES]
+TO_SECOND = [(flat(x, c, z, y), flat(x, c, z, 1 - y) if c == 1 else flat(1 - x, c, z, y)) for x, c, z, y in DEVICES]
+TO_Z = [[(flat(x, c, z, y), flat(x, c, (z + o) % 4, y)) for x, c, z, y in DEVICES] for o in (1, 2, 3)]
+
+
+def place():
+    dp, t = lax.axis_index("dp"), lax.axis_index("tensor")
+    return dp // 2, dp % 2, t // 2, t % 2
+
+
+def cost(flops, moved):
+    return pl.CostEstimate(flops=flops, bytes_accessed=moved, transcendentals=0)
+
+
+def whole():
+    return pl.BlockSpec(memory_space=pltpu.VMEM)
+
+
+def anywhere():
+    return pl.BlockSpec(memory_space=pl.ANY)
+
+
+def gather_kernel(count, chunks, *refs):
+    ins, outs = refs[:count], refs[count : 2 * count]
+    send, recv, local_sem = refs[2 * count :]
+    dp, t = lax.axis_index("dp"), lax.axis_index("tensor")
+    x, c, z, y = dp // 2, dp % 2, t // 2, t % 2
+    over_x, over_y, over_core = (1 - x) * 2 + c, z * 2 + 1 - y, x * 2 + 1 - c
+    first = (jnp.where(c == 0, dp, over_x), jnp.where(c == 0, over_y, t))
+    second = (jnp.where(c == 0, over_x, dp), jnp.where(c == 0, t, over_y))
+    x_first, y_first = jnp.where(c == 0, x, 1 - x), jnp.where(c == 0, 1 - y, y)
+    along_z = [(dp, lax.rem(z + o, 4) * 2 + y) for o in (1, 2, 3)]
+    barrier = pltpu.get_barrier_semaphore()
+    peers = along_z + [(over_x, t), (dp, over_y), (over_core, t)]
+    for peer in peers:
+        pl.semaphore_signal(barrier, inc=1, device_id=peer, device_id_type=MESH_ID)
+    pl.semaphore_wait(barrier, len(peers))
+
+    def copy(source, target, k, j, device):
+        return pltpu.make_async_remote_copy(
+            src_ref=source,
+            dst_ref=target,
+            send_sem=send.at[k, j],
+            recv_sem=recv.at[k, j],
+            device_id=device,
+            device_id_type=MESH_ID,
+        )
+
+    copies = {}
+
+    def begin(k, j, source, target, device):
+        copies[k, j] = copy(source, target, k, j, device)
+        copies[k, j].start()
+
+    def column(k, xx, yy):
+        i, start, rows = chunks[k]
+        return outs[i].at[xx, c, :, yy, pl.ds(start, rows)]
+
+    own = []
+    for i in range(count):
+        own.append(pltpu.make_async_copy(ins[i], outs[i].at[x, c, z, y], local_sem.at[i]))
+        own[i].start()
+    steps = len(chunks)
+    for k in range(steps):
+        i, start, rows = chunks[k]
+        for o in range(3):
+            begin(k, o, ins[i].at[pl.ds(start, rows)], outs[i].at[x, c, z, y, pl.ds(start, rows)], along_z[o])
+    for i in range(count):
+        own[i].wait()
+    for s in range(steps + 2):
+        if s < steps:
+            for o in range(3):
+                copies[s, o].wait_recv()
+            begin(s, 3, column(s, x, y), column(s, x, y), first)
+            begin(s, 4, column(s, x, y), column(s, x, y), second)
+        if 0 <= s - 1 < steps:
+            k = s - 1
+            copies[k, 3].wait_recv()
+            begin(k, 5, column(k, x_first, y_first), column(k, x_first, y_first), second)
+        if 0 <= s - 2 < steps:
+            k = s - 2
+            i, start, rows = chunks[k]
+            copies[k, 4].wait_recv()
+            copies[k, 5].wait_recv()
+            half = outs[i].at[:, c, :, :, pl.ds(start, rows)]
+            begin(k, 6, half, half, (over_core, t))
+    for k in range(steps):
+        copies[k, 6].wait_recv()
+    for k in range(steps):
+        for j in range(7):
+            copies[k, j].wait_send()
+
+
+def gather(parts):
+    count = len(parts)
+    chunks = []
+    for i, part in enumerate(parts):
+        for start in range(0, part.shape[0], 16):
+            chunks.append((i, start, 16))
+    outs = [jax.ShapeDtypeStruct((2, 2, 4, 2) + p.shape, p.dtype) for p in parts]
+    moved = sum(2 * 32 * p.size for p in parts)
+    return pl.pallas_call(
+        functools.partial(gather_kernel, count, chunks),
+        out_shape=outs,
+        in_specs=[anywhere()] * count,
+        out_specs=[anywhere()] * count,
+        scratch_shapes=[
+            pltpu.SemaphoreType.DMA((len(chunks), 7)),
+            pltpu.SemaphoreType.DMA((len(chunks), 7)),
+            pltpu.SemaphoreType.DMA((count,)),
+        ],
+        compiler_params=pltpu.CompilerParams(collective_id=0, has_side_effects=True),
+        cost_estimate=cost(0, 8 * moved),
+        name="gather",
+    )(*parts)
+
+
+def roll_rows(value, distance, fill, row):
+    size = value.shape[0]
+    moved = pltpu.roll(value, distance % size, 0)
+    outside = row < distance if distance > 0 else row >= size + distance
+    return jnp.where(outside, fill, moved)
+
+
+def doubling(factor, up, low, row, sign):
+    size, step = factor.shape[0], 1
+    while step < size:
+        up = up + factor * roll_rows(up, sign * step, 0.0, row)
+        low = low + factor * roll_rows(low, sign * step, 0.0, row)
+        factor = factor * roll_rows(factor, sign * step, 1.0, row)
+        step *= 2
+    return factor, up, low
+
+
+def greet_row(t, dp, size):
+    barrier = pltpu.get_barrier_semaphore()
+    for o in range(1, size):
+        pl.semaphore_signal(barrier, inc=1, device_id=(dp, lax.rem(t + o, size)), device_id_type=MESH_ID)
+    pl.semaphore_wait(barrier, size - 1)
+
+
+def share_row(summary, arrived, send, recv, t, dp, size):
+    copies = []
+    for o in range(1, size):
+        copies.append(
+            pltpu.make_async_remote_copy(
+                src_ref=summary,
+                dst_ref=arrived.at[o],
+                send_sem=send.at[o],
+                recv_sem=recv.at[o],
+                device_id=(dp, lax.rem(t + o, size)),
+                device_id_type=MESH_ID,
+            )
+        )
+        copies[-1].start()
+    for copy in copies:
+        copy.wait_recv()
+    return copies
+
+
+def lanes(j):
+    return pl.ds(pl.multiple_of(j * 128, 128), 128)
+
+
+def forward_scan_kernel(
+    keys, values, gates, keep, vectors, weighted, denom, mixed, prior_a, prior_b, recept,
+    cum, up, low, summary, arrived, entering_rows, send, recv,
+):
+    dp, t = lax.axis_index("dp"), lax.axis_index("tensor")
+    size = arrived.shape[0]
+    micro, rows = keys.shape[:2]
+    greet_row(t, dp, size)
+    row = lax.broadcasted_iota(jnp.int32, (rows, 128), 0)
+    summary[...] = jnp.zeros_like(summary)
+    for m in range(micro):
+
+        def first_pass(j, carry, m=m):
+            at = lanes(j)
+            power = jnp.exp(keys[m, :, at])
+            factor = keep[m] * vectors[0:1, at]
+            f, a, b = doubling(factor, power * values[m, :, at], power, row, 1)
+            cum[m, :, at] = f
+            up[m, :, at] = a
+            low[m, :, at] = b
+            summary[3 * m : 3 * m + 1, at] = f[rows - 1 :]
+            summary[3 * m + 1 : 3 * m + 2, at] = a[rows - 1 :]
+            summary[3 * m + 2 : 3 * m + 3, at] = b[rows - 1 :]
+            return carry
+
+        lax.fori_loop(0, keys.shape[2] // 128, first_pass, 0)
+    copies = share_row(summary, arrived, send, recv, t, dp, size)
+    for m in range(micro):
+        a = jnp.zeros((1, keys.shape[2]), F32)
+        b = jnp.zeros((1, keys.shape[2]), F32)
+        for o in range(size - 1, 0, -1):
+            f = arrived[o, 3 * m : 3 * m + 1]
+            a = jnp.where(t >= o, f * a + arrived[o, 3 * m + 1 : 3 * m + 2], a)
+            b = jnp.where(t >= o, f * b + arrived[o, 3 * m + 2 : 3 * m + 3], b)
+        entering_rows[2 * m : 2 * m + 1] = a
+        entering_rows[2 * m + 1 : 2 * m + 2] = b
+    for m in range(micro):
+
+        def second_pass(j, carry, m=m):
+            at = lanes(j)
+            enter_a = entering_rows[2 * m : 2 * m + 1, at]
+            enter_b = entering_rows[2 * m + 1 : 2 * m + 2, at]
+            f = cum[m, :, at]
+            before_a = roll_rows(up[m, :, at] + f * enter_a, 1, enter_a, row)
+            before_b = roll_rows(low[m, :, at] + f * enter_b, 1, enter_b, row)
+            bonus = jnp.exp(vectors[1:2, at] + keys[m, :, at])
+            below = keep[m] * before_b + bonus
+            blended = (keep[m] * before_a + bonus * values[m, :, at]) / below
+            gate = jax.nn.sigmoid(gates[m, :, at])
+            weighted[m, :, at] = (gate * blended).astype(BF)
+            denom[m, :, at] = below
+            mixed[m, :, at] = blended
+            prior_a[m, :, at] = before_a
+            prior_b[m, :, at] = before_b
+            recept[m, :, at] = gate
+            return carry
+
+        lax.fori_loop(0, keys.shape[2] // 128, second_pass, 0)
+    for copy in copies:
+        copy.wait_send()
+
+
+def scan_scratch(shape, size):
+    width = shape[-1]
+    return [
+        pltpu.VMEM(shape, F32),
+        pltpu.VMEM(shape, F32),
+        pltpu.VMEM(shape, F32),
+        pltpu.VMEM((8, width), F32),
+        pltpu.VMEM((size, 8, width), F32),
+        pltpu.VMEM((8, width), F32),
+        pltpu.SemaphoreType.DMA((size,)),
+        pltpu.SemaphoreType.DMA((size,)),
+    ]
+
+
+def forward_scan(keys, values, gates, keep, vectors, size):
+    shape = keys.shape
+    full = jax.ShapeDtypeStruct(shape, F32)
+    return pl.pallas_call(
+        forward_scan_kernel,
+        out_shape=[jax.ShapeDtypeStruct(shape, BF)] + [full] * 5,
+        in_specs=[whole()] * 5,
+        out_specs=[whole()] * 6,
+        scratch_shapes=scan_scratch(shape, size),
+        compiler_params=pltpu.CompilerParams(collective_id=1, has_side_effects=True),
+        cost_estimate=cost(100 * keys.size, 36 * keys.size),
+        name="forward_scan",
+    )(keys, values, gates, keep, vectors)
+
+
+def backward_scan_kernel(
+    grads, keys, values, denom, mixed, prior_a, prior_b, recept, keep, vectors,
+    grad_keys, grad_values, grad_recept, sums,
+    cum, up, low, summary, arrived, entering_rows, send, recv,
+):
+    dp, t = lax.axis_index("dp"), lax.axis_index("tensor")
+    size = arrived.shape[0]
+    micro, rows = keys.shape[:2]
+    greet_row(t, dp, size)
+    row = lax.broadcasted_iota(jnp.int32, (rows, 128), 0)
+    summary[...] = jnp.zeros_like(summary)
+    sums[...] = jnp.zeros_like(sums)
+
+    def quotient_grads(m, at):
+        gate = recept[m, :, at]
+        blended = mixed[m, :, at]
+        inner = grads[m, :, at] * gate
+        above = inner / denom[m, :, at]
+        return above, -above * blended, inner * blended * (1.0 - gate)
+
+    for m in range(micro):
+
+        def first_pass(j, carry, m=m):
+            at = lanes(j)
+            above, below, rec = quotient_grads(m, at)
+            grad_recept[m, :, at] = rec.astype(BF)
+            factor = keep[m] * vectors[0:1, at]
+            f, a, b = doubling(factor, keep[m] * above, keep[m] * below, row, -1)
+            cum[m, :, at] = f
+            up[m, :, at] = a
+            low[m, :, at] = b
+            summary[3 * m : 3 * m + 1, at] = f[:1]
+            summary[3 * m + 1 : 3 * m + 2, at] = a[:1]
+            summary[3 * m + 2 : 3 * m + 3, at] = b[:1]
+            return carry
+
+        lax.fori_loop(0, keys.shape[2] // 128, first_pass, 0)
+    copies = share_row(summary, arrived, send, recv, t, dp, size)
+    for m in range(micro):
+        a = jnp.zeros((1, keys.shape[2]), F32)
+        b = jnp.zeros((1, keys.shape[2]), F32)
+        for ahead in range(size - 1, 0, -1):
+            o = size - ahead
+            f = arrived[o, 3 * m : 3 * m + 1]
+            a = jnp.where(t + ahead < size, f * a + arrived[o, 3 * m + 1 : 3 * m + 2], a)
+            b = jnp.where(t + ahead < size, f * b + arrived[o, 3 * m + 2 : 3 * m + 3], b)
+        entering_rows[2 * m : 2 * m + 1] = a
+        entering_rows[2 * m + 1 : 2 * m + 2] = b
+    for m in range(micro):
+
+        def second_pass(j, carry, m=m):
+            at = lanes(j)
+            enter_a = entering_rows[2 * m : 2 * m + 1, at]
+            enter_b = entering_rows[2 * m + 1 : 2 * m + 2, at]
+            f = cum[m, :, at]
+            alpha = roll_rows(up[m, :, at] + f * enter_a, -1, enter_a, row)
+            beta = roll_rows(low[m, :, at] + f * enter_b, -1, enter_b, row)
+            above, below, _ = quotient_grads(m, at)
+            power = jnp.exp(keys[m, :, at])
+            bonus = jnp.exp(vectors[1:2, at] + keys[m, :, at])
+            premium = bonus * (values[m, :, at] * above + below)
+            grad_values[m, :, at] = (bonus * above + power * alpha).astype(BF)
+            grad_keys[m, :, at] = (premium + power * (values[m, :, at] * alpha + beta)).astype(BF)
+            fading = keep[m] * (alpha * prior_a[m, :, at] + beta * prior_b[m, :, at])
+            sums[0:1, at] += jnp.sum(premium, axis=0, keepdims=True)
+            sums[1:2, at] += jnp.sum(fading, axis=0, keepdims=True)
+            return carry
+
+        lax.fori_loop(0, keys.shape[2] // 128, second_pass, 0)
+    for copy in copies:
+        copy.wait_send()
+
+
+def backward_scan(grads, keys, values, denom, mixed, prior_a, prior_b, recept, keep, vectors, size):
+    shape = keys.shape
+    half = jax.ShapeDtypeStruct(shape, BF)
+    return pl.pallas_call(
+        backward_scan_kernel,
+        out_shape=[half, half, half, jax.ShapeDtypeStruct((8, shape[-1]), F32)],
+        in_specs=[whole()] * 10,
+        out_specs=[whole()] * 4,
+        scratch_shapes=scan_scratch(shape, size),
+        compiler_params=pltpu.CompilerParams(collective_id=2, has_side_effects=True),
+        cost_estimate=cost(100 * keys.size, 38 * keys.size),
+        name="backward_scan",
+    )(grads, keys, values, denom, mixed, prior_a, prior_b, recept, keep, vectors)
+
+
+def channel_forward_kernel(feed_in, key_block, value_block, positive, total):
+    rows = 4 * key_block.shape[-2]
+    keys = key_block[...].reshape(rows, key_block.shape[-1])
+    hidden = jnp.maximum(matmul_last(feed_in[...], keys), 0.0)
+    positive[0] = hidden
+    squares = (hidden * hidden).astype(BF)
+    part = matmul(squares, value_block[...].reshape(rows, value_block.shape[-1]))
+
+    @pl.when(pl.program_id(0) == 0)
+    def _():
+        total[...] = part
+
+    @pl.when(pl.program_id(0) > 0)
+    def _():
+        total[...] += part
+
+
+def channel_forward(feed_in, weights):
+    tokens, width = feed_in.shape
+    rows = weights.shape[4]
+    units = 32 * rows
+
+    def block(side):
+        return pl.BlockSpec((1, 1, 4, 1, rows, width), lambda i: (i // 4, (i // 2) % 2, 0, i % 2, 0, side))
+
+    return pl.pallas_call(
+        channel_forward_kernel,
+        grid=(8,),
+        out_shape=[jax.ShapeDtypeStruct((8, tokens, 4 * rows), F32), jax.ShapeDtypeStruct((tokens, width), F32)],
+        in_specs=[pl.BlockSpec((tokens, width), lambda i: (0, 0)), block(0), block(1)],
+        out_specs=[
+            pl.BlockSpec((1, tokens, 4 * rows), lambda i: (i, 0, 0)),
+            pl.BlockSpec((tokens, width), lambda i: (0, 0)),
+        ],
+        cost_estimate=cost(4 * tokens * units * width, 4 * units * width + 4 * tokens * units),
+        name="channel_forward",
+    )(feed_in, weights, weights)
+
+
+def channel_backward_kernel(here, feed_in, grad_value, positive, start, key_block, value_block, key_grad, value_grad, total):
+    rows = key_block.shape[-2]
+    width = key_block.shape[-1]
+    keys = key_block[...].reshape(4 * rows, width)
+    weights = value_block[...].reshape(4 * rows, width)
+    hidden = positive[0]
+    squares = (hidden * hidden).astype(BF)
+    value_part = matmul_lead(squares, grad_value[...]).astype(BF)
+    grad_pre = (matmul_last(grad_value[...], weights) * (2.0 * hidden)).astype(BF)
+    key_part = matmul_lead(grad_pre, feed_in[...]).astype(BF)
+    part = matmul(grad_pre, keys)
+    for k in range(4):
+        at = lax.rem(k + 4 - here[3], 4)
+        value_grad[0, at] = value_part[k * rows : (k + 1) * rows]
+        key_grad[0, at] = key_part[k * rows : (k + 1) * rows]
+
+    @pl.when(pl.program_id(0) == 0)
+    def _():
+        total[...] = start[...] + part
+
+    @pl.when(pl.program_id(0) > 0)
+    def _():
+        total[...] += part
+
+
+def owner(i, here, c):
+    first, second = i // 2, i % 2
+    x, y = here[0], here[2]
+    flip_x = first * c + second * (1 - c)
+    flip_y = first * (1 - c) + second * c
+    return x + flip_x - 2 * x * flip_x, y + flip_y - 2 * y * flip_y
+
+
+def channel_backward(here, feed_in, grad_value, positive, start, weights, own):
+    tokens, width = feed_in.shape
+    rows = weights.shape[4]
+
+    def side_of(here):
+        return here[1] if own else 1 - here[1]
+
+    def block(side):
+        def at(i, here):
+            x, y = owner(i, here, side_of(here))
+            return (x, side_of(here), 0, y, 0, side)
+
+        return pl.BlockSpec((1, 1, 4, 1, rows, width), at)
+
+    def saved(i, here):
+        x, y = owner(i, here, side_of(here))
+        return (x * 4 + side_of(here) * 2 + y, 0, 0)
+
+    full = pl.BlockSpec((tokens, width), lambda i, here: (0, 0))
+    grads = jax.ShapeDtypeStruct((4, 4, rows, width), BF)
+    grads_spec = pl.BlockSpec((1, 4, rows, width), lambda i, here: (i, 0, 0, 0))
+    return pl.pallas_call(
+        channel_backward_kernel,
+        out_shape=[grads, grads, jax.ShapeDtypeStruct((tokens, width), F32)],
+        grid_spec=pltpu.PrefetchScalarGridSpec(
+            num_scalar_prefetch=1,
+            grid=(4,),
+            in_specs=[full, full, pl.BlockSpec((1, tokens, 4 * rows), saved), full, block(0), block(1)],
+            out_specs=[grads_spec, grads_spec, full],
+        ),
+        cost_estimate=cost(8 * tokens * 16 * rows * width, 8 * 16 * rows * width),
+        name="channel_backward_own" if own else "channel_backward_other",
+    )(here, feed_in, grad_value, positive, start, weights, weights)
+
+
+def weight_grad_kernel(here, left, right, other, own, total):
+    width = left.shape[-1]
+    tile = 256
+
+    def turn(j, carry):
+        at = pl.multiple_of(j * tile, tile)
+        total[pl.ds(at, tile), :] = matmul_lead(left[0, :, pl.ds(at, tile)], right[0])
+        return carry
+
+    lax.fori_loop(0, width // tile, turn, 0)
+    rows = width // 32
+    for i in range(4):
+        for target, c in ((own, here[1]), (other, 1 - here[1])):
+            x, y = owner(i, here, c)
+            for o in range(4):
+                z = lax.rem(here[3] + o, 4)
+                at = pl.multiple_of((x * 16 + c * 8 + z * 2 + y) * rows, rows)
+                target[0, i, o] = total[pl.ds(at, rows), :].astype(BF)
+
+
+def weight_grads(here, lefts, rights):
+    count = len(lefts)
+    left, right = jnp.stack(lefts), jnp.stack(rights)
+    tokens, width = left.shape[1:]
+    out = jax.ShapeDtypeStruct((count, 4, 4, width // 32, width), BF)
+    spec = pl.BlockSpec((1, tokens, width), lambda i, here: (i, 0, 0))
+    out_spec = pl.BlockSpec((1, 4, 4, width // 32, width), lambda i, here: (i, 0, 0, 0, 0))
+    return pl.pallas_call(
+        weight_grad_kernel,
+        out_shape=[out, out],
+        grid_spec=pltpu.PrefetchScalarGridSpec(
+            num_scalar_prefetch=1,
+            grid=(count,),
+            in_specs=[spec, spec],
+            out_specs=[out_spec, out_spec],
+            scratch_shapes=[pltpu.VMEM((width, width), F32)],
+        ),
+        cost_estimate=cost(2 * count * tokens * width * width, 2 * count * width * width),
+        name="weight_grads",
+    )(here, left, right)
+
+
+def permute(value, route):
+    return lax.ppermute(value, BOTH, route)
+
+
+def reduce_to_owner(other, own):
+    shape = (own.shape[0], 2, 2) + own.shape[2:]
+    other, own = other.reshape(shape), own.reshape(shape)
+    wide = lambda v: v.astype(F32)
+    from_core = permute(other, TO_CORE)
+    from_first = permute((wide(own[:, 1]) + wide(from_core[:, 1])).astype(BF), TO_FIRST)
+    kept = wide(own[:, 0]) + wide(from_core[:, 0]) + wide(from_first)
+    from_second = permute(kept[:, 1].astype(BF), TO_SECOND)
+    kept = kept[:, 0] + wide(from_second)
+    total = kept[:, 0]
+    for o in (1, 2, 3):
+        total = total + wide(permute(kept[:, o].astype(BF), TO_Z[o - 1]))
+    return total
+
+
+def vector_sum_kernel(part, total, held, send, recv):
+    dp, t = lax.axis_index("dp"), lax.axis_index("tensor")
+    x, c, z, y = dp // 2, dp % 2, t // 2, t % 2
+    stages = [
+        [(x * 2 + 1 - c, t)],
+        [((1 - x) * 2 + c, t)],
+        [(dp, z * 2 + 1 - y)],
+        [(dp, lax.rem(z + o, 4) * 2 + y) for o in (1, 2, 3)],
+    ]
+    barrier = pltpu.get_barrier_semaphore()
+    for stage in stages:
+        for peer in stage:
+            pl.semaphore_signal(barrier, inc=1, device_id=peer, device_id_type=MESH_ID)
+    pl.semaphore_wait(barrier, 6)
+    slot = 0
+    sending = []
+    source = part
+    for s, stage in enumerate(stages):
+        copies = []
+        for peer in stage:
+            copies.append(
+                pltpu.make_async_remote_copy(
+                    src_ref=source,
+                    dst_ref=held.at[slot],
+                    send_sem=send.at[slot],
+                    recv_sem=recv.at[slot],
+                    device_id=peer,
+                    device_id_type=MESH_ID,
+                )
+            )
+            copies[-1].start()
+            slot += 1
+        value = source[...]
+        for i, copy in enumerate(copies):
+            copy.wait_recv()
+            value = value + held[slot - len(copies) + i]
+        sending += copies
+        if s < len(stages) - 1:
+            held[6 + s] = value
+            source = held.at[6 + s]
+        else:
+            total[...] = value
+    for copy in sending:
+        copy.wait_send()
+
+
+def vector_sum(part):
+    return pl.pallas_call(
+        vector_sum_kernel,
+        out_shape=jax.ShapeDtypeStruct(part.shape, F32),
+        in_specs=[whole()],
+        out_specs=whole(),
+        scratch_shapes=[
+            pltpu.VMEM((9,) + part.shape, F32),
+            pltpu.SemaphoreType.DMA((6,)),
+            pltpu.SemaphoreType.DMA((6,)),
+        ],
+        compiler_params=pltpu.CompilerParams(collective_id=3, has_side_effects=True),
+        cost_estimate=cost(0, 4 * 16 * part.size),
+        name="vector_sum",
+    )(part)
+
+
+def along_row(block, distance):
+    return shifted(block, "tensor", distance)
+
+
+def with_prior(value, prior):
+    return jnp.concatenate([prior, value[:, :-1]], axis=1)
+
+
+def with_next(value, following):
+    return jnp.concatenate([value[:, 1:], following], axis=1)
+
+
+def norm_back_rows(grad_out, normed, inverse, gain):
+    scaled = grad_out * gain
+    centred = scaled - jnp.mean(scaled, axis=-1, keepdims=True)
+    grad_in = inverse * (centred - normed * jnp.mean(scaled * normed, axis=-1, keepdims=True))
+    return grad_in, jnp.sum(grad_out * normed, axis=(0, 1)), jnp.sum(grad_out, axis=(0, 1))
+
+
+def local_shards(tokens, resets, out_grads, *weights):
+    (
+        mixer_key, mixer_value, mixer_recept, mixer_output, feed_recept, feed_key, feed_value, *vector_shards
+    ) = weights
+    size = lax.axis_size("tensor")
+    dp, t = lax.axis_index("dp"), lax.axis_index("tensor")
+    x, c, z, y = place()
+    here = jnp.stack([x, c, y, z]).astype(jnp.int32)
+    micro, _, length, width = tokens.shape
+    count = micro * length
+    wide = lambda v: v.astype(F32)
+
+    unit_rows = feed_key.shape[0] // 4
+    feed_shard = jnp.concatenate(
+        [lax.dynamic_slice_in_dim(w, dp * unit_rows, unit_rows, 0) for w in (feed_key, feed_value)], axis=1
+    )
+    feed = lax.all_gather(feed_shard, BOTH, axis=0, tiled=True).reshape(2, 2, 4, 2, unit_rows, 2 * width)
+    share = vector_shards[0].shape[0]
+    vector_pack = jnp.pad(jnp.stack(vector_shards), ((0, 16 - len(vector_shards)), (0, 128 - share)))
+    token_block = tokens[:, 0]
+    last_token = along_row(token_block[:, -1:], 1)
+    packed, *squares = gather([vector_pack, mixer_key, mixer_value, mixer_recept, mixer_output, feed_recept])
+    w_key, w_value, w_recept, w_output, w_feedr = [w.reshape(width, width) for w in squares]
+    vectors = wide(packed.reshape(32, 16, 128)[:, : len(vector_shards), :share].transpose(1, 0, 2).reshape(-1, width))
+    (
+        gain_one, bias_one, gain_two, bias_two, mix_key, mix_value, mix_recept, fading, premium, blend_key, blend_recept
+    ) = [vectors[i] for i in range(len(vector_shards))]
+    rates = jnp.exp(fading)
+    decay = jnp.exp(-rates)
+    scan_vectors = jnp.pad(jnp.stack([decay, premium]), ((0, 6), (0, 0)))
+
+    inputs = wide(token_block)
+    cotangent = wide(out_grads[:, 0])
+    keep = wide(1 - resets[:, 0])[:, :, None]
+    keep_lanes = jnp.broadcast_to(keep, (micro, length, 128))
+    normed_one, unit_one, inverse_one = norm_rows(inputs, gain_one, bias_one)
+    z_one = wide(normed_one.astype(BF))
+    prior_one = wide(norm_rows(wide(last_token), gain_one, bias_one)[0].astype(BF))
+    before_one = with_prior(z_one, prior_one) * keep
+    blend = lambda z, before, mix: (z * mix + before * (1.0 - mix)).astype(BF)
+    in_key, in_value, in_recept = [
+        blend(z_one, before_one, m).reshape(count, width) for m in (mix_key, mix_value, mix_recept)
+    ]
+    cube = (micro, length, width)
+    keys = matmul(in_key, w_key).reshape(cube)
+    values = matmul(in_value, w_value).reshape(cube)
+    gates = matmul(in_recept, w_recept).reshape(cube)
+    weighted, denom, mixed, prior_a, prior_b, recept = forward_scan(keys, values, gates, keep_lanes, scan_vectors, size)
+    weighted = weighted.reshape(count, width)
+    residual = inputs + matmul(weighted, w_output).reshape(cube)
+
+    normed_two, unit_two, inverse_two = norm_rows(residual, gain_two, bias_two)
+    low_two = normed_two.astype(BF)
+    z_two = wide(low_two)
+    before_two = with_prior(z_two, wide(along_row(low_two[:, -1:], 1))) * keep
+    feed_in = blend(z_two, before_two, blend_key).reshape(count, width)
+    feed_rin = blend(z_two, before_two, blend_recept).reshape(count, width)
+    gate = jax.nn.sigmoid(matmul(feed_rin, w_feedr)).reshape(cube)
+    positive, value_out = channel_forward(feed_in, feed)
+    value_out = value_out.reshape(cube)
+    result = residual + gate * value_out
+
+    grad_value = (cotangent * gate).astype(BF).reshape(count, width)
+    grad_gate = (cotangent * value_out * gate * (1.0 - gate)).astype(BF).reshape(count, width)
+    nothing = jnp.zeros((count, width), F32)
+    key_other, value_other, partial = channel_backward(here, feed_in, grad_value, positive, nothing, feed, False)
+    key_own, value_own, grad_in = channel_backward(here, feed_in, grad_value, positive, partial, feed, True)
+    value_total = reduce_to_owner(value_other[None], value_own[None])[0]
+    key_total = reduce_to_owner(key_other[None], key_own[None])[0]
+    grad_in = grad_in.reshape(cube)
+    grad_rin = matmul_last(grad_gate, w_feedr).reshape(cube)
+    spread_two = z_two - before_two
+    blend_key_grad = jnp.sum(grad_in * spread_two, axis=(0, 1))
+    blend_recept_grad = jnp.sum(grad_rin * spread_two, axis=(0, 1))
+    shift_two = keep * (grad_in * (1.0 - blend_key) + grad_rin * (1.0 - blend_recept))
+    after_two = along_row(shift_two[:, :1], -1)
+    grad_z_two = grad_in * blend_key + grad_rin * blend_recept + with_next(shift_two, after_two)
+    back_two, gain_two_grad, bias_two_grad = norm_back_rows(grad_z_two, unit_two, inverse_two, gain_two)
+    grad_residual = cotangent + back_two
+    grad_att = grad_residual.astype(BF).reshape(count, width)
+
+    middle = reduce_to_owner(*weight_grads(here, [feed_rin, weighted], [grad_gate, grad_att]))
+    grad_weighted = matmul_last(grad_att, w_output).reshape(cube)
+    grad_keys, grad_values, grad_recept, sums = backward_scan(
+        grad_weighted, keys, values, denom, mixed, prior_a, prior_b, recept, keep_lanes, scan_vectors, size
+    )
+    grad_keys, grad_values, grad_recept = [g.reshape(count, width) for g in (grad_keys, grad_values, grad_recept)]
+    front = reduce_to_owner(
+        *weight_grads(here, [in_key, in_value, in_recept], [grad_keys, grad_values, grad_recept])
+    )
+    grad_inkey = matmul_last(grad_keys, w_key).reshape(cube)
+    grad_invalue = matmul_last(grad_values, w_value).reshape(cube)
+    grad_inrecept = matmul_last(grad_recept, w_recept).reshape(cube)
+    spread_one = z_one - before_one
+    mix_grads = [jnp.sum(g * spread_one, axis=(0, 1)) for g in (grad_inkey, grad_invalue, grad_inrecept)]
+    shift_one = keep * (
+        grad_inkey * (1.0 - mix_key) + grad_invalue * (1.0 - mix_value) + grad_inrecept * (1.0 - mix_recept)
+    )
+    after_one = along_row(shift_one[:, :1], -1)
+    grad_z_one = (
+        grad_inkey * mix_key
+        + grad_invalue * mix_value
+        + grad_inrecept * mix_recept
+        + with_next(shift_one, after_one)
+    )
+    back_one, gain_one_grad, bias_one_grad = norm_back_rows(grad_z_one, unit_one, inverse_one, gain_one)
+    token_grads = grad_residual + back_one
+
+    vector_parts = [
+        gain_one_grad, bias_one_grad, gain_two_grad, bias_two_grad, *mix_grads,
+        -rates * decay * sums[1], sums[0], blend_key_grad, blend_recept_grad,
+    ]
+    summed = vector_sum(jnp.pad(jnp.stack(vector_parts), ((0, 16 - len(vector_parts)), (0, 0))))
+    mine = lax.dynamic_slice_in_dim(summed, (dp * size + t) * share, share, 1)
+
+    own_units = jnp.stack([key_total, value_total]).astype(BF)
+    x_units = permute(own_units, TO_X)
+    core_units = permute(jnp.stack([own_units, x_units]), TO_CORE)
+    unit_grads = []
+    for i in range(2):
+        blocks = []
+        for d in range(4):
+            pick = jnp.where(dp == d ^ 1, core_units[0, i], core_units[1, i])
+            pick = jnp.where(dp == d ^ 2, x_units[i], pick)
+            blocks.append(wide(jnp.where(dp == d, own_units[i], pick)))
+        unit_grads.append(jnp.concatenate(blocks, axis=0))
+    return (
+        result[:, None], token_grads[:, None],
+        front[0], front[1], front[2], middle[1], middle[0], unit_grads[0], unit_grads[1],
+    ) + tuple(mine[i] for i in range(len(vector_parts)))
+
+
+def is_two_by_two_by_four(mesh):
+    return mesh.shape["dp"] == 4 and mesh.shape["tensor"] == 8
+
+
 def solution(mesh):
     return jax.shard_map(
-        shards,
+        local_shards if is_two_by_two_by_four(mesh) else shards,
         mesh=mesh,
         in_specs=(
             P(None, "dp", "tensor", None),

time: 2260 us -> 513 us (0.23)
  waiting for transfers between devices: 1070 us -> 114 us
  blocking collectives: 458 us -> 0 us
  local copies, waits for them, and re-layouts: 407 us -> 26.9 us
  Pallas kernels: 0 us -> 206 us
  other arithmetic: 171 us -> 51.9 us
  matrix products: 97.2 us -> 22.9 us
  starting transfers between devices: 18.5 us -> 66.9 us
    reduce_scatter x9 -> x0, waiting for transfers between devices: 783 us -> none  [the longest x2 179 us: shards(): lax.psum_scatter(matmul_lead(hidden, feed_value), 'tensor', scatter_dimen...]
    all_gather x12 -> x0, blocking collectives: 371 us -> none  [entering(): everything = jax.tree.map(lambda part: lax.all_gather(part, axis), shard)]
    all_gather x9 -> x1, waiting for transfers between devices: 276 us -> 14.1 us  [local_shards(): lax.all_gather(feed_shard, BOTH, axis=0, tiled=True)]
    slice x293 -> x11, local copies, waits for them, and re-layouts: 234 us -> 4.08 us  [the longest x2 2.06 us: reduce_to_owner(): kept = wide(own[:, 0]) + wide(from_core[:, 0]) + wide(from_first)]
    pallas_call x0 -> x9, Pallas kernels: none -> 206 us  [the longest x1 81.5 us: gather(): pl.pallas_call(functools.partial(gather_kernel, count, chunks), out_shape...]
    ppermute x0 -> x26, waiting for transfers between devices: none -> 93.8 us  [permute(): return lax.ppermute(value, BOTH, route)]
    unnamed x2 -> x0, blocking collectives: 87 us -> none
    pad x142 -> x2, local copies, waits for them, and re-layouts: 86.6 us -> 1.24 us  [the longest x1 0.64 us: local_shards(): jnp.pad(jnp.stack(vector_parts), ((0, 16 - len(vector_parts)), (0, 0)))]
  transfers between devices with their start and end apart: 27 -> 31, of which waited for: 17 -> 14; matrix products, arithmetic and copies ran while one was open for 29% -> 16% of each run, Pallas kernels for 0% -> 33%
where the time goes in v1:
time: 513 us; the launch traced here: 505 us
  Pallas kernels  206 us (40%)
  waiting for transfers between devices  114 us (22%)
  starting transfers between devices  66.9 us (13%)
  other arithmetic  51.9 us (10%)
  local copies, waits for them, and re-layouts  26.9 us (5%)
  matrix products  22.9 us (4%)
  between operations  15.6 us (3%)
    ppermute x26, waiting for transfers between devices, permute(): return lax.ppermute(value, BOTH, route)  93.8 us
    pallas_call x1, Pallas kernels, gather(): pl.pallas_call(functools.partial(gather_kernel, count, chunks), out_shape...  81.5 us
    ppermute x26, starting transfers between devices, permute(): return lax.ppermute(value, BOTH, route)  53.6 us
    pallas_call x1, Pallas kernels, vector_sum(): pl.pallas_call(vector_sum_kernel, out_shape=jax.ShapeDtypeStruct(part.sha...  31.1 us
    pallas_call x2, Pallas kernels, channel_backward(): pl.pallas_call(channel_backward_kernel, out_shape=[grads, grads, jax.Shap...  24.7 us
    pallas_call x1, Pallas kernels, forward_scan(): pl.pallas_call(forward_scan_kernel, out_shape=[jax.ShapeDtypeStruct(shape...  21.7 us
    pallas_call x1, Pallas kernels, backward_scan(): pl.pallas_call(backward_scan_kernel, out_shape=[half, half, half, jax.Sha...  19.1 us
    pallas_call x2, Pallas kernels, weight_grads(): pl.pallas_call(weight_grad_kernel, out_shape=[out, out], grid_spec=pltpu....  14.5 us
  transfers between devices with their start and end apart: 31, of which 14 were waited for; matrix products, arithmetic and copies ran while one was open for 16% of the time, Pallas kernels for 33%

profile of v1, /device:TPU:0, one launch (start us, length us, event | category | flops | bytes accessed | tf_op | source)
XLA Modules:
  0.0 504.5 jit_solution(14628480483649643264)
XLA Ops:
  9.4 4.9 collective-permute-start
  15.2 81.5 %gather.1 = (bf16[2,2,4,2,16,128]{5,4,3,2,1,0:T(8,128)(2,1)}, bf16[2,2,4,2,32,1024]{5,4,3,2,1,0:T(8,128)(2,1)}, bf16[2,2,4,2,32,1024]{5,4,3,2,1,0:T(8,128)(2,1)}...) custom-call(bf16[16,128]{1,0:T(8,128)(2,1)} %pad.12.refs_0_, ...), custom_call_target="tpu_custom_call" | custom-call | bytes 84934656 | tf_op jit(solution)/shard_map/gather/pallas_call | solution.py:514
  111.8 21.7 %forward_scan.1 = (bf16[2,128,1024]{2,1,0:T(8,128)(2,1)}, f32[2,128,1024]{2,1,0:T(8,128)}, f32[2,128,1024]{2,1,0:T(8,128)}, f32[2,128,1024]{2,1,0:T(8,128)}, f32...) custom-call(f32[2,128,1024]{2,1,0:T(8,128)} %fusion.58.keys, f32[2,128,1024]{2,1,0:T(8,128)} %fusion.55.values, ...), custom_call_target="tpu_custom_call" | custom-call | flops 26214400 | bytes 9437184 | tf_op jit(solution)/shard_map/forward_scan/pallas_call | solution.py:656
  136.7 5.6 %collective-permute-start.1 = (bf16[2,1,1024]{2,1,0:T(2,128)(2,1)S(1)}, bf16[2,1,1024]{2,1,0:T(2,128)(2,1)S(1)}, u32[]{:S(2)}, u32[]{:S(2)}) collective-permute-start(bf16[2,1,1024]{2,1,0:T(2,128)(2,1)S(1)} %slice.411), channel_id=1, source_target_pairs={{0,1},{1,2},{2,3},{3,4},{4,5},{5,6},{6,7},{8,9},{9,10},{10,11},{11... | collective-permute-start | bytes 12296 | tf_op jit(solution)/shard_map/ppermute | solution.py:34
  144.9 14.1 %all-gather.2.cloned.1.call-done = bf16[4096,2048]{1,0:T(8,128)(2,1)} async-done(((bf16[128,2048]{1,0:T(8,128)(2,1)}), bf16[4096,2048]{1,0:T(8,128)(2,1)}) %all-gather.2.cloned.1.call-update) | async-done | bytes 16777232 | tf_op jit(solution)/shard_map/all_gather | solution.py:1022
  159.0 13.2 %channel_forward.1 = (f32[8,256,512]{2,1,0:T(8,128)}, f32[256,1024]{1,0:T(8,128)}) custom-call(bf16[256,1024]{1,0:T(8,128)(2,1)} %bitcast.397, bf16[2,2,4,2,128,2048]{5,4,3,2,1,0:T(8,128)(2,1)} %bitcast.386, bf16[2,2,4,2,128,2048]{5,4,3,2,1,0:T(8,128)(2,1)} %bitcast.387), custom_call_target="tpu_custom_call" | custom-call | flops 4294967296 | bytes 20971520 | tf_op jit(solution)/shard_map/channel_forward/pallas_call | solution.py:781
  172.2 4.0 fusion.48
  177.4 12.3 %channel_backward_other.1 = (bf16[4,4,128,1024]{3,2,1,0:T(8,128)(2,1)}, bf16[4,4,128,1024]{3,2,1,0:T(8,128)(2,1)}, f32[256,1024]{1,0:T(8,128)}) custom-call(s32[4]{0:T(128)} %pad_add_fusion.here, bf16[256,1024]{1,0:T(8,128)(2,1)} %bitcast.398, bf16[256,1024]{1,0:T(8,128)(2,1)} %get-tuple-element.145.grad_value, f32[8,256,512]{2,1,0:T(8,128)} %get-tuple-element.56.positive, ...), custom_call_target="tpu_custom_call" | custom-call | flops 4294967296 | bytes 16777216 | tf_op jit(solution)/shard_map/channel_backward_other/pallas_call | solution.py:849
  189.7 12.4 %channel_backward_own.1 = (bf16[4,4,128,1024]{3,2,1,0:T(8,128)(2,1)}, bf16[4,4,128,1024]{3,2,1,0:T(8,128)(2,1)}, f32[256,1024]{1,0:T(8,128)}) custom-call(s32[4]{0:T(128)} %pad_add_fusion.here, bf16[256,1024]{1,0:T(8,128)(2,1)} %bitcast.399, bf16[256,1024]{1,0:T(8,128)(2,1)} %get-tuple-element.145.grad_value, f32[8,256,512]{2,1,0:T(8,128)} %get-tuple-element.56.positive, ...), custom_call_target="tpu_custom_call" | custom-call | flops 4294967296 | bytes 16777216 | tf_op jit(solution)/shard_map/channel_backward_own/pallas_call | solution.py:849
  215.5 6.3 %weight_grads.3 = (bf16[2,4,4,32,1024]{4,3,2,1,0:T(8,128)(2,1)}, bf16[2,4,4,32,1024]{4,3,2,1,0:T(8,128)(2,1)}) custom-call(s32[4]{0:T(128)} %pad_add_fusion.here, bf16[2,256,1024]{2,1,0:T(8,128)(2,1)} %pad_maximum_fusion.3.left, bf16[2,256,1024]{2,1,0:T(8,128)(2,1)} %pad_maximum_fusion.4.right), custom_call_target="tpu_custom_call" | custom-call | flops 1073741824 | bytes 4194304 | tf_op jit(solution)/shard_map/weight_grads/pallas_call | solution.py:890
  225.1 19.1 %backward_scan.1 = (bf16[2,128,1024]{2,1,0:T(8,128)(2,1)}, bf16[2,128,1024]{2,1,0:T(8,128)(2,1)}, bf16[2,128,1024]{2,1,0:T(8,128)(2,1)}, f32[8,1024]{1,0:T(8,128)}) custom-call(f32[2,128,1024]{2,1,0:T(8,128)} %fusion.115.grads, f32[2,128,1024]{2,1,0:T(8,128)} %fusion.58.keys, f32[2,128,1024]{2,1,0:T(8,128)} %fusion.55.values, ...), custom_call_target="tpu_custom_call" | custom-call | flops 26214400 | bytes 9961472 | tf_op jit(solution)/shard_map/backward_scan/pallas_call | solution.py:744
  261.0 8.2 %weight_grads.2 = (bf16[3,4,4,32,1024]{4,3,2,1,0:T(8,128)(2,1)}, bf16[3,4,4,32,1024]{4,3,2,1,0:T(8,128)(2,1)}) custom-call(s32[4]{0:T(128)} %pad_add_fusion.here, bf16[3,256,1024]{2,1,0:T(8,128)(2,1)} %pad_maximum_fusion.left, bf16[3,256,1024]{2,1,0:T(8,128)(2,1)} %pad_maximum_fusion.1.right), custom_call_target="tpu_custom_call" | custom-call | flops 1610612736 | bytes 6291456 | tf_op jit(solution)/shard_map/weight_grads/pallas_call | solution.py:890
  269.3 4.1 copy.45
  285.4 7.1 %collective-permute-done.11 = bf16[2,2,4,32,1024]{4,3,0,2,1:T(8,128)(2,1)S(1)} collective-permute-done((bf16[2,2,4,32,1024]{4,3,0,2,1:T(8,128)(2,1)S(1)}, bf16[2,2,4,32,1024]{4,3,0,2,1:T(8,128)(2,1)S(1)}, u32[]{:S(2)}, u32[]{:S(2)}) %collective-permute-start.11) | collective-permute-done | bytes 1048608 | tf_op jit(solution)/shard_map/ppermute | solution.py:906
  303.4 11.2 %collective-permute-done.12 = bf16[2,4,32,1024]{3,2,0,1:T(8,128)(2,1)S(1)} collective-permute-done((bf16[2,4,32,1024]{3,2,0,1:T(8,128)(2,1)S(1)}, bf16[2,4,32,1024]{3,2,0,1:T(8,128)(2,1)S(1)}, u32[]{:S(2)}, u32[]{:S(2)}) %collective-permute-start.12) | collective-permute-done | bytes 524320 | tf_op jit(solution)/shard_map/ppermute | solution.py:906
  325.2 29.1 %collective-permute-done.17 = bf16[1,2,4,128,1024]{4,3,2,1,0:T(8,128)(2,1)S(1)} collective-permute-done((bf16[1,2,4,128,1024]{4,3,2,1,0:T(8,128)(2,1)S(1)}, bf16[1,2,4,128,1024]{4,3,2,1,0:T(8,128)(2,1)S(1)}, u32[]{:S(2)}, u32[]{:S(2)}) %collective-permute-start.17) | collective-permute-done | bytes 2097184 | tf_op jit(solution)/shard_map/ppermute | solution.py:906
  358.9 23.3 %collective-permute-done.5 = bf16[3,2,4,32,1024]{4,3,0,2,1:T(8,128)(2,1)S(1)} collective-permute-done((bf16[3,2,4,32,1024]{4,3,0,2,1:T(8,128)(2,1)S(1)}, bf16[3,2,4,32,1024]{4,3,0,2,1:T(8,128)(2,1)S(1)}, u32[]{:S(2)}, u32[]{:S(2)}) %collective-permute-start.5) | collective-permute-done | bytes 1572896 | tf_op jit(solution)/shard_map/ppermute | solution.py:906
  392.8 4.9 collective-permute-done.25
  397.6 9.8 %collective-permute-start.19 = (bf16[1,128,1024]{2,1,0:T(8,128)(2,1)S(1)}, bf16[1,128,1024]{2,1,0:T(8,128)(2,1)S(1)}, u32[]{:S(2)}, u32[]{:S(2)}) collective-permute-start(bf16[1,128,1024]{2,1,0:T(8,128)(2,1)S(1)} %get-tuple-element.149), channel_id=1, source_target_pairs={{0,2},{1,3},{2,4},{3,5},{4,6},{5,7},{6,0},{7,1},{8,10},{9,11},{10,... | collective-permute-start | bytes 786440 | tf_op jit(solution)/shard_map/ppermute | solution.py:906
  409.7 16.3 %collective-permute-start.21 = (bf16[1,128,1024]{2,1,0:T(8,128)(2,1)S(1)}, bf16[1,128,1024]{2,1,0:T(8,128)(2,1)S(1)}, u32[]{:S(2)}, u32[]{:S(2)}) collective-permute-start(bf16[1,128,1024]{2,1,0:T(8,128)(2,1)S(1)} %get-tuple-element.150), channel_id=1, source_target_pairs={{0,6},{1,7},{2,0},{3,1},{4,2},{5,3},{6,4},{7,5},{8,14},{9,15},{10,... | collective-permute-start | bytes 786440 | tf_op jit(solution)/shard_map/ppermute | solution.py:906
  427.7 3.6 collective-permute-done.21
  436.7 31.1 %vector_sum.1 = f32[16,1024]{1,0:T(8,128)} custom-call(f32[16,1024]{1,0:T(8,128)} %pad.14.part), custom_call_target="tpu_custom_call" | custom-call | bytes 1048576 | tf_op jit(solution)/shard_map/vector_sum/pallas_call | solution.py:971
  479.1 4.1 collective-permute-done.7
  483.2 7.9 %collective-permute-done.8 = bf16[3,32,1024]{2,1,0:T(8,128)(2,1)S(1)} collective-permute-done((bf16[3,32,1024]{2,1,0:T(8,128)(2,1)S(1)}, bf16[3,32,1024]{2,1,0:T(8,128)(2,1)S(1)}, u32[]{:S(2)}, u32[]{:S(2)}) %collective-permute-start.8) | collective-permute-done | bytes 196640 | tf_op jit(solution)/shard_map/ppermute | solution.py:906
  (254 shorter events, 133.0 us)
Async XLA Ops:
  7.3 151.7 %all-gather.2.cloned.1.call-start = ((), (), s32[]{:S(2)}) async-start(), calls=%async_computation | async-start | bytes 17301504 | tf_op jit(solution)/shard_map/all_gather | solution.py:1022
  9.4 93.7 %collective-permute-start = (bf16[2,1,1024]{2,1,0:T(2,128)(2,1)S(1)}, bf16[2,1,1024]{2,1,0:T(2,128)(2,1)S(1)}, u32[]{:S(2)}, u32[]{:S(2)}) collective-permute-start(bf16[2,1,1024]{2,1,0:T(2,128)(2,1)S(1)} %slice.402), channel_id=1, source_target_pairs={{0,1},{1,2},{2,3},{3,4},{4,5},{5,6},{6,7},{8,9},{9,10},{10,11},{11... | collective-permute-start | bytes 12296 | tf_op jit(solution)/shard_map/ppermute | solution.py:34
  207.4 73.5 %collective-permute-start.22 = (bf16[1,2,2,4,128,1024]{5,4,3,2,1,0:T(8,128)(2,1)}, bf16[1,2,2,4,128,1024]{5,4,3,2,1,0:T(8,128)(2,1)}, u32[]{:S(2)}, u32[]{:S(2)}) collective-permute-start(bf16[1,2,2,4,128,1024]{5,4,3,2,1,0:T(8,128)(2,1)} %bitcast.101), channel_id=1, source_target_pairs={{0,8},{1,9},{2,10},{3,11},{4,12},{5,13},{6,14},{7,15},{8,0},{9,1},... | collective-permute-start | bytes 12582920 | tf_op jit(solution)/shard_map/ppermute | solution.py:906
  207.7 86.7 %collective-permute-start.16 = (bf16[1,2,2,4,128,1024]{5,4,3,2,1,0:T(8,128)(2,1)}, bf16[1,2,2,4,128,1024]{5,4,3,2,1,0:T(8,128)(2,1)}, u32[]{:S(2)}, u32[]{:S(2)}) collective-permute-start(bf16[1,2,2,4,128,1024]{5,4,3,2,1,0:T(8,128)(2,1)} %bitcast.90), channel_id=1, source_target_pairs={{0,8},{1,9},{2,10},{3,11},{4,12},{5,13},{6,14},{7,15},{8,0},{9,1},... | collective-permute-start | bytes 12582920 | tf_op jit(solution)/shard_map/ppermute | solution.py:906
  225.1 50.1 %collective-permute-start.10 = (bf16[2,2,2,4,32,1024]{5,4,0,3,2,1:T(8,128)(2,1)}, bf16[2,2,2,4,32,1024]{5,4,0,3,2,1:T(8,128)(2,1)}, u32[]{:S(2)}, u32[]{:S(2)}) collective-permute-start(bf16[2,2,2,4,32,1024]{5,4,0,3,2,1:T(8,128)(2,1)} %copy.48), channel_id=1, source_target_pairs={{0,8},{1,9},{2,10},{3,11},{4,12},{5,13},{6,14},{7,15},{8,0},{9,1},... | collective-permute-start | bytes 6291464 | tf_op jit(solution)/shard_map/ppermute | solution.py:906
  273.4 27.8 %collective-permute-start.4 = (bf16[3,2,2,4,32,1024]{5,4,0,3,2,1:T(8,128)(2,1)}, bf16[3,2,2,4,32,1024]{5,4,0,3,2,1:T(8,128)(2,1)}, u32[]{:S(2)}, u32[]{:S(2)}) collective-permute-start(bf16[3,2,2,4,32,1024]{5,4,0,3,2,1:T(8,128)(2,1)} %copy.45), channel_id=1, source_target_pairs={{0,8},{1,9},{2,10},{3,11},{4,12},{5,13},{6,14},{7,15},{8,0},{9,1},... | collective-permute-start | bytes 9437192 | tf_op jit(solution)/shard_map/ppermute | solution.py:906
  276.9 15.5 %collective-permute-start.11 = (bf16[2,2,4,32,1024]{4,3,0,2,1:T(8,128)(2,1)S(1)}, bf16[2,2,4,32,1024]{4,3,0,2,1:T(8,128)(2,1)S(1)}, u32[]{:S(2)}, u32[]{:S(2)}) collective-permute-start(bf16[2,2,4,32,1024]{4,3,0,2,1:T(8,128)(2,1)S(1)} %fusion.36), channel_id=1, source_target_pairs={{0,1},{1,0},{2,3},{3,2},{4,5},{5,4},{6,7},{7,6},{8,24},{9,25},{10,... | collective-permute-start | bytes 3145736 | tf_op jit(solution)/shard_map/ppermute | solution.py:906
  285.3 35.2 %collective-permute-start.23 = (bf16[1,2,4,128,1024]{4,3,2,1,0:T(8,128)(2,1)S(1)}, bf16[1,2,4,128,1024]{4,3,2,1,0:T(8,128)(2,1)S(1)}, u32[]{:S(2)}, u32[]{:S(2)}) collective-permute-start(bf16[1,2,4,128,1024]{4,3,2,1,0:T(8,128)(2,1)S(1)} %fusion.1), channel_id=1, source_target_pairs={{0,1},{1,0},{2,3},{3,2},{4,5},{5,4},{6,7},{7,6},{8,24},{9,25},{10,... | collective-permute-start | bytes 6291464 | tf_op jit(solution)/shard_map/ppermute | solution.py:906
  297.5 56.7 %collective-permute-start.17 = (bf16[1,2,4,128,1024]{4,3,2,1,0:T(8,128)(2,1)S(1)}, bf16[1,2,4,128,1024]{4,3,2,1,0:T(8,128)(2,1)S(1)}, u32[]{:S(2)}, u32[]{:S(2)}) collective-permute-start(bf16[1,2,4,128,1024]{4,3,2,1,0:T(8,128)(2,1)S(1)} %fusion), channel_id=1, source_target_pairs={{0,1},{1,0},{2,3},{3,2},{4,5},{5,4},{6,7},{7,6},{8,24},{9,25},{10,... | collective-permute-start | bytes 6291464 | tf_op jit(solution)/shard_map/ppermute | solution.py:906
  303.3 79.0 %collective-permute-start.5 = (bf16[3,2,4,32,1024]{4,3,0,2,1:T(8,128)(2,1)S(1)}, bf16[3,2,4,32,1024]{4,3,0,2,1:T(8,128)(2,1)S(1)}, u32[]{:S(2)}, u32[]{:S(2)}) collective-permute-start(bf16[3,2,4,32,1024]{4,3,0,2,1:T(8,128)(2,1)S(1)} %fusion.4), channel_id=1, source_target_pairs={{0,1},{1,0},{2,3},{3,2},{4,5},{5,4},{6,7},{7,6},{8,24},{9,25},{10,... | collective-permute-start | bytes 4718600 | tf_op jit(solution)/shard_map/ppermute | solution.py:906
  316.5 152.9 %collective-permute-start.13 = (bf16[2,32,1024]{2,1,0:T(8,128)(2,1)}, bf16[2,32,1024]{2,1,0:T(8,128)(2,1)}, u32[]{:S(2)}, u32[]{:S(2)}) collective-permute-start(bf16[2,32,1024]{2,1,0:T(8,128)(2,1)} %get-tuple-element.159), channel_id=1, source_target_pairs={{0,2},{1,3},{2,4},{3,5},{4,6},{5,7},{6,0},{7,1},{8,10},{9,11},{10,... | collective-permute-start | bytes 393224 | tf_op jit(solution)/shard_map/ppermute | solution.py:906
  318.2 151.2 %collective-permute-start.14 = (bf16[2,32,1024]{2,1,0:T(8,128)(2,1)}, bf16[2,32,1024]{2,1,0:T(8,128)(2,1)}, u32[]{:S(2)}, u32[]{:S(2)}) collective-permute-start(bf16[2,32,1024]{2,1,0:T(8,128)(2,1)} %get-tuple-element.161), channel_id=1, source_target_pairs={{0,4},{1,5},{2,6},{3,7},{4,0},{5,1},{6,2},{7,3},{8,12},{9,13},{10,... | collective-permute-start | bytes 393224 | tf_op jit(solution)/shard_map/ppermute | solution.py:906
  323.7 62.0 %collective-permute-start.24 = (bf16[1,4,128,1024]{3,2,1,0:T(8,128)(2,1)S(1)}, bf16[1,4,128,1024]{3,2,1,0:T(8,128)(2,1)S(1)}, u32[]{:S(2)}, u32[]{:S(2)}) collective-permute-start(bf16[1,4,128,1024]{3,2,1,0:T(8,128)(2,1)S(1)} %fusion.38), channel_id=1, source_target_pairs={{0,16},{1,17},{2,18},{3,19},{4,20},{5,21},{6,22},{7,23},{8,9},{9,8... | collective-permute-start | bytes 3145736 | tf_op jit(solution)/shard_map/ppermute | solution.py:906
  357.4 32.0 %collective-permute-start.18 = (bf16[1,4,128,1024]{3,2,1,0:T(8,128)(2,1)S(1)}, bf16[1,4,128,1024]{3,2,1,0:T(8,128)(2,1)S(1)}, u32[]{:S(2)}, u32[]{:S(2)}) collective-permute-start(bf16[1,4,128,1024]{3,2,1,0:T(8,128)(2,1)S(1)} %fusion.37), channel_id=1, source_target_pairs={{0,16},{1,17},{2,18},{3,19},{4,20},{5,21},{6,22},{7,23},{8,9},{9,8... | collective-permute-start | bytes 3145736 | tf_op jit(solution)/shard_map/ppermute | solution.py:906
  388.4 19.2 %collective-permute-start.26 = (bf16[1,128,1024]{2,1,0:T(8,128)(2,1)S(1)}, bf16[1,128,1024]{2,1,0:T(8,128)(2,1)S(1)}, u32[]{:S(2)}, u32[]{:S(2)}) collective-permute-start(bf16[1,128,1024]{2,1,0:T(8,128)(2,1)S(1)} %get-tuple-element.148), channel_id=1, source_target_pairs={{0,4},{1,5},{2,6},{3,7},{4,0},{5,1},{6,2},{7,3},{8,12},{9,13},{10,... | collective-permute-start | bytes 786440 | tf_op jit(solution)/shard_map/ppermute | solution.py:906
  389.4 20.2 %collective-permute-start.27 = (bf16[1,128,1024]{2,1,0:T(8,128)(2,1)S(1)}, bf16[1,128,1024]{2,1,0:T(8,128)(2,1)S(1)}, u32[]{:S(2)}, u32[]{:S(2)}) collective-permute-start(bf16[1,128,1024]{2,1,0:T(8,128)(2,1)S(1)} %get-tuple-element.147), channel_id=1, source_target_pairs={{0,6},{1,7},{2,0},{3,1},{4,2},{5,3},{6,4},{7,5},{8,14},{9,15},{10,... | collective-permute-start | bytes 786440 | tf_op jit(solution)/shard_map/ppermute | solution.py:906
  397.6 28.5 %collective-permute-start.19 = (bf16[1,128,1024]{2,1,0:T(8,128)(2,1)S(1)}, bf16[1,128,1024]{2,1,0:T(8,128)(2,1)S(1)}, u32[]{:S(2)}, u32[]{:S(2)}) collective-permute-start(bf16[1,128,1024]{2,1,0:T(8,128)(2,1)S(1)} %get-tuple-element.149), channel_id=1, source_target_pairs={{0,2},{1,3},{2,4},{3,5},{4,6},{5,7},{6,0},{7,1},{8,10},{9,11},{10,... | collective-permute-start | bytes 786440 | tf_op jit(solution)/shard_map/ppermute | solution.py:906
  407.6 18.7 %collective-permute-start.20 = (bf16[1,128,1024]{2,1,0:T(8,128)(2,1)S(1)}, bf16[1,128,1024]{2,1,0:T(8,128)(2,1)S(1)}, u32[]{:S(2)}, u32[]{:S(2)}) collective-permute-start(bf16[1,128,1024]{2,1,0:T(8,128)(2,1)S(1)} %get-tuple-element.151), channel_id=1, source_target_pairs={{0,4},{1,5},{2,6},{3,7},{4,0},{5,1},{6,2},{7,3},{8,12},{9,13},{10,... | collective-permute-start | bytes 786440 | tf_op jit(solution)/shard_map/ppermute | solution.py:906
  409.7 21.7 %collective-permute-start.21 = (bf16[1,128,1024]{2,1,0:T(8,128)(2,1)S(1)}, bf16[1,128,1024]{2,1,0:T(8,128)(2,1)S(1)}, u32[]{:S(2)}, u32[]{:S(2)}) collective-permute-start(bf16[1,128,1024]{2,1,0:T(8,128)(2,1)S(1)} %get-tuple-element.150), channel_id=1, source_target_pairs={{0,6},{1,7},{2,0},{3,1},{4,2},{5,3},{6,4},{7,5},{8,14},{9,15},{10,... | collective-permute-start | bytes 786440 | tf_op jit(solution)/shard_map/ppermute | solution.py:906
  426.2 43.2 %collective-permute-start.15 = (bf16[2,32,1024]{2,1,0:T(8,128)(2,1)}, bf16[2,32,1024]{2,1,0:T(8,128)(2,1)}, u32[]{:S(2)}, u32[]{:S(2)}) collective-permute-start(bf16[2,32,1024]{2,1,0:T(8,128)(2,1)} %get-tuple-element.160), channel_id=1, source_target_pairs={{0,6},{1,7},{2,0},{3,1},{4,2},{5,3},{6,4},{7,5},{8,14},{9,15},{10,... | collective-permute-start | bytes 393224 | tf_op jit(solution)/shard_map/ppermute | solution.py:906
  426.3 45.7 %collective-permute-start.6 = (bf16[3,4,32,1024]{3,2,0,1:T(8,128)(2,1)}, bf16[3,4,32,1024]{3,2,0,1:T(8,128)(2,1)}, u32[]{:S(2)}, u32[]{:S(2)}) collective-permute-start(bf16[3,4,32,1024]{3,2,0,1:T(8,128)(2,1)} %fusion.49), channel_id=1, source_target_pairs={{0,16},{1,17},{2,18},{3,19},{4,20},{5,21},{6,22},{7,23},{8,9},{9,8... | collective-permute-start | bytes 2359304 | tf_op jit(solution)/shard_map/ppermute | solution.py:906
  432.5 38.1 %collective-permute-start.28 = (bf16[2,128,1024]{2,1,0:T(8,128)(2,1)}, bf16[2,128,1024]{2,1,0:T(8,128)(2,1)}, u32[]{:S(2)}, u32[]{:S(2)}) collective-permute-start(bf16[2,128,1024]{2,1,0:T(8,128)(2,1)} %pad_maximum_fusion.7), channel_id=1, source_target_pairs={{0,16},{1,17},{2,18},{3,19},{4,20},{5,21},{6,22},{7,23},{8,24},{9,... | collective-permute-start | bytes 1572872 | tf_op jit(solution)/shard_map/ppermute | solution.py:906
  471.8 20.1 %collective-permute-start.29 = (bf16[2,2,128,1024]{3,2,1,0:T(8,128)(2,1)S(1)}, bf16[2,2,128,1024]{3,2,1,0:T(8,128)(2,1)S(1)}, u32[]{:S(2)}, u32[]{:S(2)}) collective-permute-start(bf16[2,2,128,1024]{3,2,1,0:T(8,128)(2,1)S(1)} %pad_maximum_fusion.5), channel_id=1, source_target_pairs={{0,8},{1,9},{2,10},{3,11},{4,12},{5,13},{6,14},{7,15},{8,0},{9,1},... | collective-permute-start | bytes 3145736 | tf_op jit(solution)/shard_map/ppermute | solution.py:906
  474.7 16.4 %collective-permute-start.8 = (bf16[3,32,1024]{2,1,0:T(8,128)(2,1)S(1)}, bf16[3,32,1024]{2,1,0:T(8,128)(2,1)S(1)}, u32[]{:S(2)}, u32[]{:S(2)}) collective-permute-start(bf16[3,32,1024]{2,1,0:T(8,128)(2,1)S(1)} %get-tuple-element.158), channel_id=1, source_target_pairs={{0,4},{1,5},{2,6},{3,7},{4,0},{5,1},{6,2},{7,3},{8,12},{9,13},{10,... | collective-permute-start | bytes 589832 | tf_op jit(solution)/shard_map/ppermute | solution.py:906
  (52 other events, 419.3 us)
Sparse Core Ops, SparseCore 0:
  11.8 147.2 all-gather.1

commit v2 on v1

--- a/solution.py
+++ b/solution.py
@@ -401,23 +401,6 @@
 F32 = jnp.float32
 BOTH = ("dp", "tensor")
 MESH_ID = pl.DeviceIdType.MESH
-DEVICES = [(x, c, z, y) for x in range(2) for c in range(2) for z in range(4) for y in range(2)]
-
-
-def flat(x, c, z, y):
-    return (x * 2 + c) * 8 + z * 2 + y
-
-
-TO_CORE = [(flat(*d), flat(d[0], 1 - d[1], d[2], d[3])) for d in DEVICES]
-TO_X = [(flat(*d), flat(1 - d[0], d[1], d[2], d[3])) for d in DEVICES]
-TO_FIRST = [(flat(x, c, z, y), flat(x, c, z, 1 - y) if c == 0 else flat(1 - x, c, z, y)) for x, c, z, y in DEVICES]
-TO_SECOND = [(flat(x, c, z, y), flat(x, c, z, 1 - y) if c == 1 else flat(1 - x, c, z, y)) for x, c, z, y in DEVICES]
-TO_Z = [[(flat(x, c, z, y), flat(x, c, (z + o) % 4, y)) for x, c, z, y in DEVICES] for o in (1, 2, 3)]
-
-
-def place():
-    dp, t = lax.axis_index("dp"), lax.axis_index("tensor")
-    return dp // 2, dp % 2, t // 2, t % 2
 
 
 def cost(flops, moved):
@@ -665,94 +648,6 @@
     )(keys, values, gates, keep, vectors)
 
 
-def backward_scan_kernel(
-    grads, keys, values, denom, mixed, prior_a, prior_b, recept, keep, vectors,
-    grad_keys, grad_values, grad_recept, sums,
-    cum, up, low, summary, arrived, entering_rows, send, recv,
-):
-    dp, t = lax.axis_index("dp"), lax.axis_index("tensor")
-    size = arrived.shape[0]
-    micro, rows = keys.shape[:2]
-    greet_row(t, dp, size)
-    row = lax.broadcasted_iota(jnp.int32, (rows, 128), 0)
-    summary[...] = jnp.zeros_like(summary)
-    sums[...] = jnp.zeros_like(sums)
-
-    def quotient_grads(m, at):
-        gate = recept[m, :, at]
-        blended = mixed[m, :, at]
-        inner = grads[m, :, at] * gate
-        above = inner / denom[m, :, at]
-        return above, -above * blended, inner * blended * (1.0 - gate)
-
-    for m in range(micro):
-
-        def first_pass(j, carry, m=m):
-            at = lanes(j)
-            above, below, rec = quotient_grads(m, at)
-            grad_recept[m, :, at] = rec.astype(BF)
-            factor = keep[m] * vectors[0:1, at]
-            f, a, b = doubling(factor, keep[m] * above, keep[m] * below, row, -1)
-            cum[m, :, at] = f
-            up[m, :, at] = a
-            low[m, :, at] = b
-            summary[3 * m : 3 * m + 1, at] = f[:1]
-            summary[3 * m + 1 : 3 * m + 2, at] = a[:1]
-            summary[3 * m + 2 : 3 * m + 3, at] = b[:1]
-            return carry
-
-        lax.fori_loop(0, keys.shape[2] // 128, first_pass, 0)
-    copies = share_row(summary, arrived, send, recv, t, dp, size)
-    for m in range(micro):
-        a = jnp.zeros((1, keys.shape[2]), F32)
-        b = jnp.zeros((1, keys.shape[2]), F32)
-        for ahead in range(size - 1, 0, -1):
-            o = size - ahead
-            f = arrived[o, 3 * m : 3 * m + 1]
-            a = jnp.where(t + ahead < size, f * a + arrived[o, 3 * m + 1 : 3 * m + 2], a)
-            b = jnp.where(t + ahead < size, f * b + arrived[o, 3 * m + 2 : 3 * m + 3], b)
-        entering_rows[2 * m : 2 * m + 1] = a
-        entering_rows[2 * m + 1 : 2 * m + 2] = b
-    for m in range(micro):
-
-        def second_pass(j, carry, m=m):
-            at = lanes(j)
-            enter_a = entering_rows[2 * m : 2 * m + 1, at]
-            enter_b = entering_rows[2 * m + 1 : 2 * m + 2, at]
-            f = cum[m, :, at]
-            alpha = roll_rows(up[m, :, at] + f * enter_a, -1, enter_a, row)
-            beta = roll_rows(low[m, :, at] + f * enter_b, -1, enter_b, row)
-            above, below, _ = quotient_grads(m, at)
-            power = jnp.exp(keys[m, :, at])
-            bonus = jnp.exp(vectors[1:2, at] + keys[m, :, at])
-            premium = bonus * (values[m, :, at] * above + below)
-            grad_values[m, :, at] = (bonus * above + power * alpha).astype(BF)
-            grad_keys[m, :, at] = (premium + power * (values[m, :, at] * alpha + beta)).astype(BF)
-            fading = keep[m] * (alpha * prior_a[m, :, at] + beta * prior_b[m, :, at])
-            sums[0:1, at] += jnp.sum(premium, axis=0, keepdims=True)
-            sums[1:2, at] += jnp.sum(fading, axis=0, keepdims=True)
-            return carry
-
-        lax.fori_loop(0, keys.shape[2] // 128, second_pass, 0)
-    for copy in copies:
-        copy.wait_send()
-
-
-def backward_scan(grads, keys, values, denom, mixed, prior_a, prior_b, recept, keep, vectors, size):
-    shape = keys.shape
-    half = jax.ShapeDtypeStruct(shape, BF)
-    return pl.pallas_call(
-        backward_scan_kernel,
-        out_shape=[half, half, half, jax.ShapeDtypeStruct((8, shape[-1]), F32)],
-        in_specs=[whole()] * 10,
-        out_specs=[whole()] * 4,
-        scratch_shapes=scan_scratch(shape, size),
-        compiler_params=pltpu.CompilerParams(collective_id=2, has_side_effects=True),
-        cost_estimate=cost(100 * keys.size, 38 * keys.size),
-        name="backward_scan",
-    )(grads, keys, values, denom, mixed, prior_a, prior_b, recept, keep, vectors)
-
-
 def channel_forward_kernel(feed_in, key_block, value_block, positive, total):
     rows = 4 * key_block.shape[-2]
     keys = key_block[...].reshape(rows, key_block.shape[-1])
@@ -792,196 +687,632 @@
     )(feed_in, weights, weights)
 
 
-def channel_backward_kernel(here, feed_in, grad_value, positive, start, key_block, value_block, key_grad, value_grad, total):
-    rows = key_block.shape[-2]
-    width = key_block.shape[-1]
-    keys = key_block[...].reshape(4 * rows, width)
-    weights = value_block[...].reshape(4 * rows, width)
-    hidden = positive[0]
-    squares = (hidden * hidden).astype(BF)
-    value_part = matmul_lead(squares, grad_value[...]).astype(BF)
-    grad_pre = (matmul_last(grad_value[...], weights) * (2.0 * hidden)).astype(BF)
-    key_part = matmul_lead(grad_pre, feed_in[...]).astype(BF)
-    part = matmul(grad_pre, keys)
-    for k in range(4):
-        at = lax.rem(k + 4 - here[3], 4)
-        value_grad[0, at] = value_part[k * rows : (k + 1) * rows]
-        key_grad[0, at] = key_part[k * rows : (k + 1) * rows]
-
-    @pl.when(pl.program_id(0) == 0)
-    def _():
-        total[...] = start[...] + part
-
-    @pl.when(pl.program_id(0) > 0)
-    def _():
-        total[...] += part
-
-
-def owner(i, here, c):
+def owner(i, x, y, c):
     first, second = i // 2, i % 2
-    x, y = here[0], here[2]
     flip_x = first * c + second * (1 - c)
     flip_y = first * (1 - c) + second * c
     return x + flip_x - 2 * x * flip_x, y + flip_y - 2 * y * flip_y
 
 
-def channel_backward(here, feed_in, grad_value, positive, start, weights, own):
+def position(xx, yy, x, y, c):
+    flip_x = x + xx - 2 * x * xx
+    flip_y = y + yy - 2 * y * yy
+    return 2 * (flip_x * c + flip_y * (1 - c)) + flip_x * (1 - c) + flip_y * c
+
+
+class Links:
+    def __init__(self, size):
+        dp, t = lax.axis_index("dp"), lax.axis_index("tensor")
+        x, c, z, y = dp // 2, dp % 2, t // 2, t % 2
+        self.x, self.c, self.z, self.y, self.dp, self.t, self.size = x, c, z, y, dp, t, size
+        over_x, over_y = ((1 - x) * 2 + c, t), (dp, z * 2 + 1 - y)
+        self.over_x = over_x
+        self.core = (x * 2 + 1 - c, t)
+        self.first = (jnp.where(c == 0, over_y[0], over_x[0]), jnp.where(c == 0, over_y[1], over_x[1]))
+        self.second = (jnp.where(c == 0, over_x[0], over_y[0]), jnp.where(c == 0, over_x[1], over_y[1]))
+        self.along_z = [(dp, lax.rem(z + o, 4) * 2 + y) for o in (1, 2, 3)]
+        self.over_y = over_y
+
+    def row(self, o):
+        return (self.dp, lax.rem(self.t + o, self.size))
+
+    def greet(self, whole_row):
+        peers = [self.row(o) for o in range(1, self.size)] if whole_row else self.along_z + [self.over_y]
+        peers = peers + [self.over_x, self.core]
+        barrier = pltpu.get_barrier_semaphore()
+        for peer in peers:
+            pl.semaphore_signal(barrier, inc=1, device_id=peer, device_id_type=MESH_ID)
+        pl.semaphore_wait(barrier, len(peers))
+
+
+def remote(source, target, send, recv, device):
+    return pltpu.make_async_remote_copy(
+        src_ref=source, dst_ref=target, send_sem=send, recv_sem=recv, device_id=device, device_id_type=MESH_ID
+    )
+
+
+def add_blocks(target, sources):
+    count, rows = target.shape[:2]
+    tile = min(rows, 32)
+    per = rows // tile
+
+    def turn(k, carry):
+        n, at = k // per, pl.ds(pl.multiple_of(lax.rem(k, per) * tile, tile), tile)
+        value = sources[0][n, at].astype(F32)
+        for source in sources[1:]:
+            value = value + source[n, at].astype(F32)
+        target[n, at] = value.astype(target.dtype)
+        return carry
+
+    lax.fori_loop(0, count * per, turn, 0)
+
+
+def dot_rows(target, left, right):
+    tile = 256
+
+    def turn(n, carry):
+        at = pl.ds(pl.multiple_of(n * tile, tile), tile)
+        target[:, at] = matmul_last(left[...], right[at, :])
+        return carry
+
+    lax.fori_loop(0, right.shape[0] // tile, turn, 0)
+
+
+def norm_back_tiles(target, grads, normed, inverse, gain, base, sums, gain_row):
+    tile = 32
+    width = grads.shape[1]
+
+    def turn(k, carry):
+        at = pl.ds(pl.multiple_of(k * tile, tile), tile)
+        grad, unit = grads[at, :], normed[at, :]
+        scaled = grad * gain
+        middle = jnp.sum(scaled, axis=-1, keepdims=True) * (1.0 / width)
+        along = jnp.sum(scaled * unit, axis=-1, keepdims=True) * (1.0 / width)
+        target[at, :] = base[at, :].astype(F32) + inverse[at, 0:1] * (scaled - middle - unit * along)
+        sums[gain_row : gain_row + 1, :] += jnp.sum(grad * unit, axis=0, keepdims=True)
+        sums[gain_row + 1 : gain_row + 2, :] += jnp.sum(grad, axis=0, keepdims=True)
+        return carry
+
+    lax.fori_loop(0, grads.shape[0] // tile, turn, 0)
+
+
+GAIN_ONE, BIAS_ONE, GAIN_TWO, BIAS_TWO, MIX_KEY, MIX_VALUE, MIX_RECEPT, DECAY, PREMIUM, BLEND_KEY, BLEND_RECEPT = range(11)
+
+
+def channel_backward_kernel(
+    feed_in, grad_value, grad_gate, vectors, keep, inverse, cotangent,
+    weights, positive, w_feedr, w_output, spread, unit, keys, values, denom, mixed, prior_a, prior_b, recept,
+    feed_part, grad_keys, grad_values, grad_recept, grad_att, grad_residual, sums,
+    weight_slots, positive_slots, feedr, output, spread_in, unit_in, keys_in, values_in, denom_in, mixed_in,
+    prior_a_in, prior_b_in, recept_in, value_part, key_part, outgoing, gathered, from_first, from_second,
+    grad_in, grad_rin, grad_z, grad_w, cum, up, low, summary, arrived, entering_rows, halo_out, halo_in,
+    slot_sem, load_sem, core_send, core_recv, first_send, first_recv, second_send, second_recv,
+    scan_send, scan_recv, halo_send, halo_recv,
+):
+    size = arrived.shape[0]
+    links = Links(size)
+    x, c, z, y, t = links.x, links.c, links.z, links.y, links.t
+    rows, width = weight_slots.shape[2], feed_in.shape[1]
+    micro, length = keep.shape[:2]
+
+    def fetches(s, slot):
+        own = s // 4
+        cc = own * c + (1 - own) * (1 - c)
+        xx, yy = owner(3 - lax.rem(s, 4), x, y, cc)
+        return (
+            pltpu.make_async_copy(weights.at[xx, cc, :, yy], weight_slots.at[slot], slot_sem.at[0, slot]),
+            pltpu.make_async_copy(positive.at[xx * 4 + cc * 2 + yy], positive_slots.at[slot], slot_sem.at[1, slot]),
+        )
+
+    for copy in fetches(0, 0):
+        copy.start()
+    late = [
+        (w_feedr, feedr), (spread, spread_in), (unit, unit_in), (w_output, output), (recept, recept_in),
+        (mixed, mixed_in), (denom, denom_in), (keys, keys_in), (values, values_in), (prior_a, prior_a_in),
+        (prior_b, prior_b_in),
+    ]
+    loads = [pltpu.make_async_copy(source, target, load_sem.at[k]) for k, (source, target) in enumerate(late)]
+    for load in loads:
+        load.start()
+    links.greet(True)
+    grad_in[...] = jnp.zeros_like(grad_in)
+    sums[...] = jnp.zeros_like(sums)
+    summary[...] = jnp.zeros_like(summary)
+    halo_out[...] = jnp.zeros_like(halo_out)
+
+    def to_core(i, slot):
+        return remote(outgoing.at[slot], gathered.at[i], core_send.at[i], core_recv.at[i], links.core)
+
+    def to_first(q, side):
+        return remote(
+            gathered.at[2 + q, side], from_first.at[q, side], first_send.at[q, side], first_recv.at[q, side], links.first
+        )
+
+    def column(s, carry):
+        slot = lax.rem(s, 2)
+        i = 3 - lax.rem(s, 4)
+        for copy in fetches(s, slot):
+            copy.wait()
+
+        @pl.when(s < 7)
+        def _():
+            for copy in fetches(s + 1, 1 - slot):
+                copy.start()
+
+        hidden = positive_slots[slot]
+        squares = (hidden * hidden).astype(BF)
+        key_rows = weight_slots[slot, :, :, :width].reshape(4 * rows, width)
+        value_rows = weight_slots[slot, :, :, width:].reshape(4 * rows, width)
+        value_part[...] = matmul_lead(squares, grad_value[...])
+        grad_pre = (matmul_last(grad_value[...], value_rows) * (2.0 * hidden)).astype(BF)
+        key_part[...] = matmul_lead(grad_pre, feed_in[...])
+        grad_in[...] += matmul(grad_pre, key_rows)
+
+        @pl.when(s < 4)
+        def _():
+            @pl.when(s >= 2)
+            def _():
+                to_core(i + 2, slot).wait_send()
+
+            for k in range(4):
+                at = lax.rem(k + 4 - z, 4)
+                outgoing[slot, 0, at] = value_part[k * rows : (k + 1) * rows].astype(BF)
+                outgoing[slot, 1, at] = key_part[k * rows : (k + 1) * rows].astype(BF)
+            to_core(i, slot).start()
+
+        @pl.when(s >= 4)
+        def _():
+            to_core(i, slot).wait_recv()
+            for side, part in ((0, value_part), (1, key_part)):
+                for k in range(4):
+                    at = lax.rem(k + 4 - z, 4)
+                    total = gathered[i, side, at].astype(F32) + part[k * rows : (k + 1) * rows]
+                    gathered[i, side, at] = total.astype(BF)
+
+        @pl.when(jnp.logical_and(s >= 4, s < 6))
+        def _():
+            for side in (0, 1):
+                to_first(i - 2, side).start()
+
+        return carry
+
+    lax.fori_loop(0, 8, column, 0)
+    to_core(1, 0).wait_send()
+    to_core(0, 1).wait_send()
+
+    def to_second(side):
+        return remote(
+            gathered.at[1, side], from_second.at[side], second_send.at[side], second_recv.at[side], links.second
+        )
+
+    def pass_second(side):
+        to_first(1, side).wait_recv()
+        add_blocks(gathered.at[1, side], [gathered.at[1, side], from_first.at[1, side]])
+        to_second(side).start()
+
+    row = lax.broadcasted_iota(jnp.int32, (length, 128), 0)
+    loads[0].wait()
+    dot_rows(grad_rin, grad_gate, feedr)
+
+    def shift_two(m, rows_at, at, keeping):
+        return keeping * (
+            grad_in[rows_at, at] * (1.0 - vectors[BLEND_KEY : BLEND_KEY + 1, at])
+            + grad_rin[rows_at, at] * (1.0 - vectors[BLEND_RECEPT : BLEND_RECEPT + 1, at])
+        )
+
+    for m in range(micro):
+        start = m * length
+        halo_out[m : m + 1] = shift_two(m, slice(start, start + 1), slice(None), keep[m, 0:1, 0:1])
+    halo = remote(halo_out, halo_in, halo_send.at[0], halo_recv.at[0], links.row(size - 1))
+    halo.start()
+    pass_second(0)
+    loads[1].wait()
+    halo.wait_recv()
+    for m in range(micro):
+        rows_at = slice(m * length, (m + 1) * length)
+
+        def shift_pass(j, carry, m=m, rows_at=rows_at):
+            at = lanes(j)
+            after = jnp.where(t < size - 1, halo_in[m : m + 1, at], 0.0)
+            shift = shift_two(m, rows_at, at, keep[m])
+            from_in, from_rin, apart = grad_in[rows_at, at], grad_rin[rows_at, at], spread_in[rows_at, at]
+            grad_z[rows_at, at] = (
+                from_in * vectors[BLEND_KEY : BLEND_KEY + 1, at]
+                + from_rin * vectors[BLEND_RECEPT : BLEND_RECEPT + 1, at]
+                + roll_rows(shift, -1, after, row)
+            )
+            sums[BLEND_KEY : BLEND_KEY + 1, at] += jnp.sum(from_in * apart, axis=0, keepdims=True)
+            sums[BLEND_RECEPT : BLEND_RECEPT + 1, at] += jnp.sum(from_rin * apart, axis=0, keepdims=True)
+            return carry
+
+        lax.fori_loop(0, width // 128, shift_pass, 0)
+    loads[2].wait()
+    norm_back_tiles(
+        grad_residual, grad_z, unit_in, inverse, vectors[GAIN_TWO : GAIN_TWO + 1, :], cotangent, sums, GAIN_TWO
+    )
+    grad_att[...] = grad_residual[...].astype(BF)
+    pass_second(1)
+
+    loads[3].wait()
+    dot_rows(grad_w, grad_att, output)
+    for load in loads[4:]:
+        load.wait()
+
+    def quotient_grads(rows_at, at):
+        gate = recept_in[rows_at, at]
+        blended = mixed_in[rows_at, at]
+        inner = grad_w[rows_at, at] * gate
+        above = inner / denom_in[rows_at, at]
+        return above, -above * blended, inner * blended * (1.0 - gate)
+
+    for m in range(micro):
+        rows_at = slice(m * length, (m + 1) * length)
+
+        def first_pass(j, carry, m=m, rows_at=rows_at):
+            at = lanes(j)
+            above, below, rec = quotient_grads(rows_at, at)
+            grad_recept[rows_at, at] = rec.astype(BF)
+            factor = keep[m] * vectors[DECAY : DECAY + 1, at]
+            f, a, b = doubling(factor, keep[m] * above, keep[m] * below, row, -1)
+            cum[rows_at, at] = f
+            up[rows_at, at] = a
+            low[rows_at, at] = b
+            summary[3 * m : 3 * m + 1, at] = f[:1]
+            summary[3 * m + 1 : 3 * m + 2, at] = a[:1]
+            summary[3 * m + 2 : 3 * m + 3, at] = b[:1]
+            return carry
+
+        lax.fori_loop(0, width // 128, first_pass, 0)
+    copies = share_row(summary, arrived, scan_send, scan_recv, t, links.dp, size)
+    for m in range(micro):
+        a = jnp.zeros((1, width), F32)
+        b = jnp.zeros((1, width), F32)
+        for ahead in range(size - 1, 0, -1):
+            o = size - ahead
+            f = arrived[o, 3 * m : 3 * m + 1]
+            a = jnp.where(t + ahead < size, f * a + arrived[o, 3 * m + 1 : 3 * m + 2], a)
+            b = jnp.where(t + ahead < size, f * b + arrived[o, 3 * m + 2 : 3 * m + 3], b)
+        entering_rows[2 * m : 2 * m + 1] = a
+        entering_rows[2 * m + 1 : 2 * m + 2] = b
+    for m in range(micro):
+        rows_at = slice(m * length, (m + 1) * length)
+
+        def second_pass(j, carry, m=m, rows_at=rows_at):
+            at = lanes(j)
+            enter_a = entering_rows[2 * m : 2 * m + 1, at]
+            enter_b = entering_rows[2 * m + 1 : 2 * m + 2, at]
+            f = cum[rows_at, at]
+            alpha = roll_rows(up[rows_at, at] + f * enter_a, -1, enter_a, row)
+            beta = roll_rows(low[rows_at, at] + f * enter_b, -1, enter_b, row)
+            above, below, _ = quotient_grads(rows_at, at)
+            key, value = keys_in[rows_at, at], values_in[rows_at, at]
+            power = jnp.exp(key)
+            bonus = jnp.exp(vectors[PREMIUM : PREMIUM + 1, at] + key)
+            premium = bonus * (value * above + below)
+            grad_values[rows_at, at] = (bonus * above + power * alpha).astype(BF)
+            grad_keys[rows_at, at] = (premium + power * (value * alpha + beta)).astype(BF)
+            fading = keep[m] * (alpha * prior_a_in[rows_at, at] + beta * prior_b_in[rows_at, at])
+            sums[PREMIUM : PREMIUM + 1, at] += jnp.sum(premium, axis=0, keepdims=True)
+            sums[DECAY : DECAY + 1, at] += jnp.sum(fading, axis=0, keepdims=True)
+            return carry
+
+        lax.fori_loop(0, width // 128, second_pass, 0)
+
+    for side in (0, 1):
+        to_first(0, side).wait_recv()
+        to_second(side).wait_recv()
+        add_blocks(
+            feed_part.at[side], [gathered.at[0, side], from_first.at[0, side], from_second.at[side]]
+        )
+    for side in (0, 1):
+        to_first(0, side).wait_send()
+        to_first(1, side).wait_send()
+        to_second(side).wait_send()
+    halo.wait_send()
+    for copy in copies:
+        copy.wait_send()
+
+
+def channel_backward(near, far, size):
+    feed_in = near[0]
+    weights = far[0]
     tokens, width = feed_in.shape
+    micro, length = near[4].shape[:2]
     rows = weights.shape[4]
-
-    def side_of(here):
-        return here[1] if own else 1 - here[1]
-
-    def block(side):
-        def at(i, here):
-            x, y = owner(i, here, side_of(here))
-            return (x, side_of(here), 0, y, 0, side)
-
-        return pl.BlockSpec((1, 1, 4, 1, rows, width), at)
-
-    def saved(i, here):
-        x, y = owner(i, here, side_of(here))
-        return (x * 4 + side_of(here) * 2 + y, 0, 0)
-
-    full = pl.BlockSpec((tokens, width), lambda i, here: (0, 0))
-    grads = jax.ShapeDtypeStruct((4, 4, rows, width), BF)
-    grads_spec = pl.BlockSpec((1, 4, rows, width), lambda i, here: (i, 0, 0, 0))
+    flat_f32, flat_bf = (tokens, width), jax.ShapeDtypeStruct((tokens, width), BF)
+    dma = pltpu.SemaphoreType.DMA
+    big = pltpu.VMEM(flat_f32, F32)
     return pl.pallas_call(
         channel_backward_kernel,
-        out_shape=[grads, grads, jax.ShapeDtypeStruct((tokens, width), F32)],
-        grid_spec=pltpu.PrefetchScalarGridSpec(
-            num_scalar_prefetch=1,
-            grid=(4,),
-            in_specs=[full, full, pl.BlockSpec((1, tokens, 4 * rows), saved), full, block(0), block(1)],
-            out_specs=[grads_spec, grads_spec, full],
+        out_shape=[
+            jax.ShapeDtypeStruct((2, 4, rows, width), BF), flat_bf, flat_bf, flat_bf, flat_bf,
+            jax.ShapeDtypeStruct(flat_f32, F32), jax.ShapeDtypeStruct((16, width), F32),
+        ],
+        in_specs=[whole()] * len(near) + [anywhere()] * len(far),
+        out_specs=[whole()] * 7,
+        scratch_shapes=[
+            pltpu.VMEM((2, 4, rows, 2 * width), BF), pltpu.VMEM((2, tokens, 4 * rows), F32),
+            pltpu.VMEM((width, width), BF), pltpu.VMEM((width, width), BF),
+        ]
+        + [big] * 9
+        + [
+            pltpu.VMEM((4 * rows, width), F32), pltpu.VMEM((4 * rows, width), F32),
+            pltpu.VMEM((2, 2, 4, rows, width), BF), pltpu.VMEM((4, 2, 4, rows, width), BF),
+            pltpu.VMEM((2, 2, 4, rows, width), BF), pltpu.VMEM((2, 4, rows, width), BF),
+        ]
+        + [big] * 7
+        + [
+            pltpu.VMEM((8, width), F32), pltpu.VMEM((size, 8, width), F32), pltpu.VMEM((8, width), F32),
+            pltpu.VMEM((8, width), F32), pltpu.VMEM((8, width), F32),
+            dma((2, 2)), dma((11,)), dma((4,)), dma((4,)), dma((2, 2)), dma((2, 2)), dma((2,)), dma((2,)),
+            dma((size,)), dma((size,)), dma((1,)), dma((1,)),
+        ],
+        compiler_params=pltpu.CompilerParams(
+            collective_id=2, has_side_effects=True, vmem_limit_bytes=66_000_000
         ),
-        cost_estimate=cost(8 * tokens * 16 * rows * width, 8 * 16 * rows * width),
-        name="channel_backward_own" if own else "channel_backward_other",
-    )(here, feed_in, grad_value, positive, start, weights, weights)
-
-
-def weight_grad_kernel(here, left, right, other, own, total):
-    width = left.shape[-1]
-    tile = 256
-
-    def turn(j, carry):
-        at = pl.multiple_of(j * tile, tile)
-        total[pl.ds(at, tile), :] = matmul_lead(left[0, :, pl.ds(at, tile)], right[0])
+        cost_estimate=cost(8 * tokens * 32 * rows * width, 16 * 32 * rows * width),
+        name="channel_backward",
+    )(*near, *far)
+
+
+def front_backward_kernel(
+    feed_part, lefts, rights, vectors, keep, inverse, grad_residual, sums_in, rates,
+    w_key, w_value, w_recept, spread, unit,
+    square_grads, unit_key, unit_value, token_grads, vector_grads,
+    key_in, value_in, recept_in, spread_in, unit_in, outgoing, gathered, from_first, from_second, from_z, feed_z,
+    own_units, x_units, core_units, grad_key, grad_value, grad_recept, grad_z, sums, held, halo_out, halo_in,
+    load_sem, core_send, core_recv, first_send, first_recv, second_send, second_recv, z_send, z_recv,
+    feed_send, feed_recv, unit_send, unit_recv, halo_send, halo_recv, sum_send, sum_recv,
+):
+    links = Links(8)
+    x, c, z, y, t, size = links.x, links.c, links.z, links.y, links.t, links.size
+    count = lefts.shape[0]
+    width = lefts.shape[2]
+    rows = width // 32
+    micro, length = keep.shape[:2]
+    late = [(w_key, key_in), (w_value, value_in), (w_recept, recept_in), (spread, spread_in), (unit, unit_in)]
+    loads = [pltpu.make_async_copy(source, target, load_sem.at[k]) for k, (source, target) in enumerate(late)]
+    for load in loads:
+        load.start()
+    links.greet(True)
+    feed_copies = {}
+    for side in (0, 1):
+        for o in (1, 2, 3):
+            feed_copies[side, o] = remote(
+                feed_part.at[side, o], feed_z.at[side, o - 1], feed_send.at[side, o - 1], feed_recv.at[side, o - 1],
+                links.along_z[o - 1],
+            )
+            feed_copies[side, o].start()
+    halo_out[...] = jnp.zeros_like(halo_out)
+    sums[...] = sums_in[...]
+
+    def part(n, cc, xx):
+        at = pl.ds(pl.multiple_of((xx * 2 + cc) * 8 * rows, 8 * rows), 8 * rows)
+        return matmul_lead(lefts[n, :, at], rights[n])
+
+    def blocks():
+        for zz in range(4):
+            for yy in range(2):
+                yield zz, yy, slice((zz * 2 + yy) * rows, (zz * 2 + yy + 1) * rows)
+
+    def to_core(n):
+        return remote(outgoing.at[n], gathered.at[n], core_send.at[n], core_recv.at[n], links.core)
+
+    def to_first(n):
+        return remote(
+            gathered.at[n, pl.ds(2, 2)], from_first.at[n], first_send.at[n], first_recv.at[n], links.first
+        )
+
+    def to_second(n):
+        return remote(gathered.at[n, 1], from_second.at[n], second_send.at[n], second_recv.at[n], links.second)
+
+    def to_z(n, o):
+        return remote(
+            gathered.at[n, 0, o], from_z.at[n, o - 1], z_send.at[n, o - 1], z_recv.at[n, o - 1], links.along_z[o - 1]
+        )
+
+    def other(n, carry):
+        for xx in range(2):
+            value = part(n, 1 - c, xx)
+            for zz, yy, at in blocks():
+                outgoing[n, position(xx, yy, x, y, 1 - c), lax.rem(zz + 4 - z, 4)] = value[at].astype(BF)
+        to_core(n).start()
         return carry
 
-    lax.fori_loop(0, width // tile, turn, 0)
-    rows = width // 32
-    for i in range(4):
-        for target, c in ((own, here[1]), (other, 1 - here[1])):
-            x, y = owner(i, here, c)
-            for o in range(4):
-                z = lax.rem(here[3] + o, 4)
-                at = pl.multiple_of((x * 16 + c * 8 + z * 2 + y) * rows, rows)
-                target[0, i, o] = total[pl.ds(at, rows), :].astype(BF)
-
-
-def weight_grads(here, lefts, rights):
-    count = len(lefts)
-    left, right = jnp.stack(lefts), jnp.stack(rights)
-    tokens, width = left.shape[1:]
-    out = jax.ShapeDtypeStruct((count, 4, 4, width // 32, width), BF)
-    spec = pl.BlockSpec((1, tokens, width), lambda i, here: (i, 0, 0))
-    out_spec = pl.BlockSpec((1, 4, 4, width // 32, width), lambda i, here: (i, 0, 0, 0, 0))
+    def own(n, carry):
+        to_core(n).wait_recv()
+        for xx in range(2):
+            value = part(n, c, xx)
+            for zz, yy, at in blocks():
+                i, o = position(xx, yy, x, y, c), lax.rem(zz + 4 - z, 4)
+                gathered[n, i, o] = (gathered[n, i, o].astype(F32) + value[at]).astype(BF)
+        to_first(n).start()
+        return carry
+
+    lax.fori_loop(0, count, other, 0)
+    lax.fori_loop(0, count, own, 0)
+
+    def pass_second(n):
+        to_first(n).wait_recv()
+        add_blocks(gathered.at[n, 1], [gathered.at[n, 1], from_first.at[n, 1]])
+        to_second(n).start()
+
+    def pass_z(n):
+        to_second(n).wait_recv()
+        add_blocks(gathered.at[n, 0], [gathered.at[n, 0], from_first.at[n, 0], from_second.at[n]])
+        for o in (1, 2, 3):
+            to_z(n, o).start()
+
+    def finish(n):
+        value = gathered[n, 0, 0].astype(F32)
+        for o in (1, 2, 3):
+            to_z(n, o).wait_recv()
+            value = value + from_z[n, o - 1].astype(F32)
+        square_grads[n] = value
+
+    for side in (0, 1):
+        for o in (1, 2, 3):
+            feed_copies[side, o].wait_recv()
+        for r in range(0, feed_part.shape[2], 32):
+            at = slice(r, r + 32)
+            value = feed_part[side, 0, at].astype(F32)
+            for o in range(3):
+                value = value + feed_z[side, o, at].astype(F32)
+            own_units[side, at] = value.astype(BF)
+    units_over_x = remote(own_units, x_units, unit_send.at[0], unit_recv.at[0], links.over_x)
+    units_over_x.start()
+    units_over_core = remote(own_units, core_units.at[0], unit_send.at[1], unit_recv.at[1], links.core)
+    units_over_core.start()
+
+    loads[0].wait()
+    dot_rows(grad_key, rights.at[2], key_in)
+    pass_second(0)
+    loads[1].wait()
+    dot_rows(grad_value, rights.at[3], value_in)
+    pass_second(1)
+    loads[2].wait()
+    dot_rows(grad_recept, rights.at[4], recept_in)
+    units_over_x.wait_recv()
+    both_over_core = remote(x_units, core_units.at[1], unit_send.at[2], unit_recv.at[2], links.core)
+    both_over_core.start()
+    grads = ((grad_key, MIX_KEY), (grad_value, MIX_VALUE), (grad_recept, MIX_RECEPT))
+
+    def shift_one(rows_at, at, keeping):
+        return keeping * sum(g[rows_at, at] * (1.0 - vectors[k : k + 1, at]) for g, k in grads)
+
+    for m in range(micro):
+        start = m * length
+        halo_out[m : m + 1] = shift_one(slice(start, start + 1), slice(None), keep[m, 0:1, 0:1])
+    halo = remote(halo_out, halo_in, halo_send.at[0], halo_recv.at[0], links.row(size - 1))
+    halo.start()
+    pass_second(2)
+    pass_z(0)
+    loads[3].wait()
+    halo.wait_recv()
+    row = lax.broadcasted_iota(jnp.int32, (length, 128), 0)
+    for m in range(micro):
+        rows_at = slice(m * length, (m + 1) * length)
+
+        def shift_pass(j, carry, m=m, rows_at=rows_at):
+            at = lanes(j)
+            after = jnp.where(t < size - 1, halo_in[m : m + 1, at], 0.0)
+            apart = spread_in[rows_at, at]
+            value = roll_rows(shift_one(rows_at, at, keep[m]), -1, after, row)
+            for g, k in grads:
+                value = value + g[rows_at, at] * vectors[k : k + 1, at]
+                sums[k : k + 1, at] += jnp.sum(g[rows_at, at] * apart, axis=0, keepdims=True)
+            grad_z[rows_at, at] = value
+            return carry
+
+        lax.fori_loop(0, width // 128, shift_pass, 0)
+    pass_second(3)
+    pass_z(1)
+    loads[4].wait()
+    norm_back_tiles(
+        token_grads, grad_z, unit_in, inverse, vectors[GAIN_ONE : GAIN_ONE + 1, :], grad_residual, sums, GAIN_ONE
+    )
+    sums[DECAY : DECAY + 1, :] = -sums[DECAY : DECAY + 1, :] * rates[0:1, :] * vectors[DECAY : DECAY + 1, :]
+    pass_second(4)
+
+    stages = [[links.core], [links.over_x], [links.over_y], links.along_z]
+    pending = []
+    source, slot = sums, 0
+
+    def begin(stage, source, slot):
+        copies = [
+            remote(source, held.at[slot + k], sum_send.at[slot + k], sum_recv.at[slot + k], peer)
+            for k, peer in enumerate(stage)
+        ]
+        for copy in copies:
+            copy.start()
+        return copies
+
+    def collect(copies, source, slot, target):
+        value = source[...]
+        for k, copy in enumerate(copies):
+            copy.wait_recv()
+            value = value + held[slot + k]
+        target[...] = value
+
+    copies = begin(stages[0], sums, 0)
+    pending += copies
+    pass_z(2)
+    collect(copies, sums, 0, held.at[6])
+    copies = begin(stages[1], held.at[6], 1)
+    pending += copies
+    pass_z(3)
+    finish(0)
+    collect(copies, held.at[6], 1, held.at[7])
+    copies = begin(stages[2], held.at[7], 2)
+    pending += copies
+    pass_z(4)
+    finish(1)
+    collect(copies, held.at[7], 2, held.at[8])
+    copies = begin(stages[3], held.at[8], 3)
+    pending += copies
+    units_over_core.wait_recv()
+    both_over_core.wait_recv()
+    for side, target in ((1, unit_key), (0, unit_value)):
+        for d in range(4):
+            for r in range(0, own_units.shape[1], 32):
+                at = slice(r, r + 32)
+                pick = jnp.where(links.dp == d ^ 1, core_units[0, side, at], core_units[1, side, at])
+                pick = jnp.where(links.dp == d ^ 2, x_units[side, at], pick)
+                pick = jnp.where(links.dp == d, own_units[side, at], pick)
+                target[d, at] = pick.astype(F32)
+    collect(copies, held.at[8], 3, vector_grads)
+    finish(2)
+    finish(3)
+    finish(4)
+    for n in range(count):
+        to_core(n).wait_send()
+        to_first(n).wait_send()
+        to_second(n).wait_send()
+        for o in (1, 2, 3):
+            to_z(n, o).wait_send()
+    for copy in pending + list(feed_copies.values()) + [units_over_x, units_over_core, both_over_core, halo]:
+        copy.wait_send()
+
+
+def front_backward(near, far):
+    feed_part, lefts = near[:2]
+    rows = feed_part.shape[2]
+    count, tokens, width = lefts.shape
+    own = width // 32
+    dma = pltpu.SemaphoreType.DMA
+    big = pltpu.VMEM((tokens, width), F32)
+    square = pltpu.VMEM((width, width), BF)
     return pl.pallas_call(
-        weight_grad_kernel,
-        out_shape=[out, out],
-        grid_spec=pltpu.PrefetchScalarGridSpec(
-            num_scalar_prefetch=1,
-            grid=(count,),
-            in_specs=[spec, spec],
-            out_specs=[out_spec, out_spec],
-            scratch_shapes=[pltpu.VMEM((width, width), F32)],
+        front_backward_kernel,
+        out_shape=[
+            jax.ShapeDtypeStruct((count, own, width), F32),
+            jax.ShapeDtypeStruct((4, rows, width), F32), jax.ShapeDtypeStruct((4, rows, width), F32),
+            jax.ShapeDtypeStruct((tokens, width), F32), jax.ShapeDtypeStruct((16, width), F32),
+        ],
+        in_specs=[whole()] * len(near) + [anywhere()] * len(far),
+        out_specs=[whole()] * 5,
+        scratch_shapes=[square] * 3
+        + [big] * 2
+        + [
+            pltpu.VMEM((count, 4, 4, own, width), BF), pltpu.VMEM((count, 4, 4, own, width), BF),
+            pltpu.VMEM((count, 2, 4, own, width), BF), pltpu.VMEM((count, 4, own, width), BF),
+            pltpu.VMEM((count, 3, own, width), BF), pltpu.VMEM((2, 3, rows, width), BF),
+            pltpu.VMEM((2, rows, width), BF), pltpu.VMEM((2, rows, width), BF), pltpu.VMEM((2, 2, rows, width), BF),
+        ]
+        + [big] * 4
+        + [
+            pltpu.VMEM((16, width), F32), pltpu.VMEM((9, 16, width), F32), pltpu.VMEM((8, width), F32),
+            pltpu.VMEM((8, width), F32),
+            dma((5,)), dma((count,)), dma((count,)), dma((count,)), dma((count,)), dma((count,)), dma((count,)),
+            dma((count, 3)), dma((count, 3)), dma((2, 3)), dma((2, 3)), dma((3,)), dma((3,)), dma((1,)), dma((1,)),
+            dma((6,)), dma((6,)),
+        ],
+        compiler_params=pltpu.CompilerParams(
+            collective_id=3, has_side_effects=True, vmem_limit_bytes=66_000_000
         ),
-        cost_estimate=cost(2 * count * tokens * width * width, 2 * count * width * width),
-        name="weight_grads",
-    )(here, left, right)
-
-
-def permute(value, route):
-    return lax.ppermute(value, BOTH, route)
-
-
-def reduce_to_owner(other, own):
-    shape = (own.shape[0], 2, 2) + own.shape[2:]
-    other, own = other.reshape(shape), own.reshape(shape)
-    wide = lambda v: v.astype(F32)
-    from_core = permute(other, TO_CORE)
-    from_first = permute((wide(own[:, 1]) + wide(from_core[:, 1])).astype(BF), TO_FIRST)
-    kept = wide(own[:, 0]) + wide(from_core[:, 0]) + wide(from_first)
-    from_second = permute(kept[:, 1].astype(BF), TO_SECOND)
-    kept = kept[:, 0] + wide(from_second)
-    total = kept[:, 0]
-    for o in (1, 2, 3):
-        total = total + wide(permute(kept[:, o].astype(BF), TO_Z[o - 1]))
-    return total
-
-
-def vector_sum_kernel(part, total, held, send, recv):
-    dp, t = lax.axis_index("dp"), lax.axis_index("tensor")
-    x, c, z, y = dp // 2, dp % 2, t // 2, t % 2
-    stages = [
-        [(x * 2 + 1 - c, t)],
-        [((1 - x) * 2 + c, t)],
-        [(dp, z * 2 + 1 - y)],
-        [(dp, lax.rem(z + o, 4) * 2 + y) for o in (1, 2, 3)],
-    ]
-    barrier = pltpu.get_barrier_semaphore()
-    for stage in stages:
-        for peer in stage:
-            pl.semaphore_signal(barrier, inc=1, device_id=peer, device_id_type=MESH_ID)
-    pl.semaphore_wait(barrier, 6)
-    slot = 0
-    sending = []
-    source = part
-    for s, stage in enumerate(stages):
-        copies = []
-        for peer in stage:
-            copies.append(
-                pltpu.make_async_remote_copy(
-                    src_ref=source,
-                    dst_ref=held.at[slot],
-                    send_sem=send.at[slot],
-                    recv_sem=recv.at[slot],
-                    device_id=peer,
-                    device_id_type=MESH_ID,
-                )
-            )
-            copies[-1].start()
-            slot += 1
-        value = source[...]
-        for i, copy in enumerate(copies):
-            copy.wait_recv()
-            value = value + held[slot - len(copies) + i]
-        sending += copies
-        if s < len(stages) - 1:
-            held[6 + s] = value
-            source = held.at[6 + s]
-        else:
-            total[...] = value
-    for copy in sending:
-        copy.wait_send()
-
-
-def vector_sum(part):
-    return pl.pallas_call(
-        vector_sum_kernel,
-        out_shape=jax.ShapeDtypeStruct(part.shape, F32),
-        in_specs=[whole()],
-        out_specs=whole(),
-        scratch_shapes=[
-            pltpu.VMEM((9,) + part.shape, F32),
-            pltpu.SemaphoreType.DMA((6,)),
-            pltpu.SemaphoreType.DMA((6,)),
-        ],
-        compiler_params=pltpu.CompilerParams(collective_id=3, has_side_effects=True),
-        cost_estimate=cost(0, 4 * 16 * part.size),
-        name="vector_sum",
-    )(part)
+        cost_estimate=cost(4 * count * tokens * width * width, 40 * width * width),
+        name="front_backward",
+    )(*near, *far)
 
 
 def along_row(block, distance):
@@ -990,17 +1321,6 @@
 
 def with_prior(value, prior):
     return jnp.concatenate([prior, value[:, :-1]], axis=1)
-
-
-def with_next(value, following):
-    return jnp.concatenate([value[:, 1:], following], axis=1)
-
-
-def norm_back_rows(grad_out, normed, inverse, gain):
-    scaled = grad_out * gain
-    centred = scaled - jnp.mean(scaled, axis=-1, keepdims=True)
-    grad_in = inverse * (centred - normed * jnp.mean(scaled * normed, axis=-1, keepdims=True))
-    return grad_in, jnp.sum(grad_out * normed, axis=(0, 1)), jnp.sum(grad_out, axis=(0, 1))
 
 
 def local_shards(tokens, resets, out_grads, *weights):
@@ -1009,8 +1329,6 @@
     ) = weights
     size = lax.axis_size("tensor")
     dp, t = lax.axis_index("dp"), lax.axis_index("tensor")
-    x, c, z, y = place()
-    here = jnp.stack([x, c, y, z]).astype(jnp.int32)
     micro, _, length, width = tokens.shape
     count = micro * length
     wide = lambda v: v.astype(F32)
@@ -1067,72 +1385,25 @@
 
     grad_value = (cotangent * gate).astype(BF).reshape(count, width)
     grad_gate = (cotangent * value_out * gate * (1.0 - gate)).astype(BF).reshape(count, width)
-    nothing = jnp.zeros((count, width), F32)
-    key_other, value_other, partial = channel_backward(here, feed_in, grad_value, positive, nothing, feed, False)
-    key_own, value_own, grad_in = channel_backward(here, feed_in, grad_value, positive, partial, feed, True)
-    value_total = reduce_to_owner(value_other[None], value_own[None])[0]
-    key_total = reduce_to_owner(key_other[None], key_own[None])[0]
-    grad_in = grad_in.reshape(cube)
-    grad_rin = matmul_last(grad_gate, w_feedr).reshape(cube)
-    spread_two = z_two - before_two
-    blend_key_grad = jnp.sum(grad_in * spread_two, axis=(0, 1))
-    blend_recept_grad = jnp.sum(grad_rin * spread_two, axis=(0, 1))
-    shift_two = keep * (grad_in * (1.0 - blend_key) + grad_rin * (1.0 - blend_recept))
-    after_two = along_row(shift_two[:, :1], -1)
-    grad_z_two = grad_in * blend_key + grad_rin * blend_recept + with_next(shift_two, after_two)
-    back_two, gain_two_grad, bias_two_grad = norm_back_rows(grad_z_two, unit_two, inverse_two, gain_two)
-    grad_residual = cotangent + back_two
-    grad_att = grad_residual.astype(BF).reshape(count, width)
-
-    middle = reduce_to_owner(*weight_grads(here, [feed_rin, weighted], [grad_gate, grad_att]))
-    grad_weighted = matmul_last(grad_att, w_output).reshape(cube)
-    grad_keys, grad_values, grad_recept, sums = backward_scan(
-        grad_weighted, keys, values, denom, mixed, prior_a, prior_b, recept, keep_lanes, scan_vectors, size
-    )
-    grad_keys, grad_values, grad_recept = [g.reshape(count, width) for g in (grad_keys, grad_values, grad_recept)]
-    front = reduce_to_owner(
-        *weight_grads(here, [in_key, in_value, in_recept], [grad_keys, grad_values, grad_recept])
-    )
-    grad_inkey = matmul_last(grad_keys, w_key).reshape(cube)
-    grad_invalue = matmul_last(grad_values, w_value).reshape(cube)
-    grad_inrecept = matmul_last(grad_recept, w_recept).reshape(cube)
-    spread_one = z_one - before_one
-    mix_grads = [jnp.sum(g * spread_one, axis=(0, 1)) for g in (grad_inkey, grad_invalue, grad_inrecept)]
-    shift_one = keep * (
-        grad_inkey * (1.0 - mix_key) + grad_invalue * (1.0 - mix_value) + grad_inrecept * (1.0 - mix_recept)
-    )
-    after_one = along_row(shift_one[:, :1], -1)
-    grad_z_one = (
-        grad_inkey * mix_key
-        + grad_invalue * mix_value
-        + grad_inrecept * mix_recept
-        + with_next(shift_one, after_one)
-    )
-    back_one, gain_one_grad, bias_one_grad = norm_back_rows(grad_z_one, unit_one, inverse_one, gain_one)
-    token_grads = grad_residual + back_one
-
-    vector_parts = [
-        gain_one_grad, bias_one_grad, gain_two_grad, bias_two_grad, *mix_grads,
-        -rates * decay * sums[1], sums[0], blend_key_grad, blend_recept_grad,
-    ]
-    summed = vector_sum(jnp.pad(jnp.stack(vector_parts), ((0, 16 - len(vector_parts)), (0, 0))))
-    mine = lax.dynamic_slice_in_dim(summed, (dp * size + t) * share, share, 1)
-
-    own_units = jnp.stack([key_total, value_total]).astype(BF)
-    x_units = permute(own_units, TO_X)
-    core_units = permute(jnp.stack([own_units, x_units]), TO_CORE)
-    unit_grads = []
-    for i in range(2):
-        blocks = []
-        for d in range(4):
-            pick = jnp.where(dp == d ^ 1, core_units[0, i], core_units[1, i])
-            pick = jnp.where(dp == d ^ 2, x_units[i], pick)
-            blocks.append(wide(jnp.where(dp == d, own_units[i], pick)))
-        unit_grads.append(jnp.concatenate(blocks, axis=0))
+    table = jnp.pad(vectors.at[DECAY].set(decay), ((0, 5), (0, 0)))
+    flat = lambda v: v.reshape(count, width)
+    over_lanes = lambda v: jnp.broadcast_to(v.reshape(count, 1), (count, 128))
+    near = [feed_in, grad_value, grad_gate, table, keep_lanes, over_lanes(inverse_two), flat(out_grads)]
+    far = [feed, positive, w_feedr, w_output, flat(z_two - before_two), flat(unit_two)]
+    far += [flat(v) for v in (keys, values, denom, mixed, prior_a, prior_b, recept)]
+    feed_part, grad_keys, grad_values, grad_recept, grad_att, grad_residual, sums = channel_backward(near, far, size)
+    lefts = jnp.stack([feed_rin, weighted, in_key, in_value, in_recept])
+    rights = jnp.stack([grad_gate, grad_att, grad_keys, grad_values, grad_recept])
+    near = [feed_part, lefts, rights, table, keep_lanes, over_lanes(inverse_one), grad_residual, sums]
+    near += [jnp.broadcast_to(rates, (8, width))]
+    far = [w_key, w_value, w_recept, flat(z_one - before_one), flat(unit_one)]
+    square_grads, unit_key, unit_value, token_grads, vector_grads = front_backward(near, far)
+    mine = lax.dynamic_slice_in_dim(vector_grads, (dp * size + t) * share, share, 1)
     return (
-        result[:, None], token_grads[:, None],
-        front[0], front[1], front[2], middle[1], middle[0], unit_grads[0], unit_grads[1],
-    ) + tuple(mine[i] for i in range(len(vector_parts)))
+        result[:, None], token_grads.reshape(cube)[:, None],
+        square_grads[2], square_grads[3], square_grads[4], square_grads[1], square_grads[0],
+        unit_key.reshape(feed_key.shape), unit_value.reshape(feed_value.shape),
+    ) + tuple(mine[i] for i in range(len(vector_shards)))
 
 
 def is_two_by_two_by_four(mesh):

time: 513 us -> 409 us (0.80); the launches traced: 505 us -> 406 us
  Pallas kernels: 206 us -> 320 us
  waiting for transfers between devices: 114 us -> 8.21 us
  starting transfers between devices: 66.9 us -> 10.3 us
  other arithmetic: 51.9 us -> 15 us
  matrix products: 22.9 us -> 11.6 us
    pallas_call x6 -> x2, Pallas kernels: 89.5 us -> 203 us  [the longest x1 111 us: channel_backward(): pl.pallas_call(channel_backward_kernel, out_shape=[jax.ShapeDtypeStruct((...]
    ppermute x26 -> x0, waiting for transfers between devices: 93.8 us -> none  [permute(): return lax.ppermute(value, BOTH, route)]
    ppermute x26 -> x0, starting transfers between devices: 53.6 us -> none  [permute(): return lax.ppermute(value, BOTH, route)]
    add x6 -> x0, other arithmetic: 11.6 us -> none  [the longest x4 10.3 us: reduce_to_owner(): kept = wide(own[:, 0]) + wide(from_core[:, 0]) + wide(from_first)]
    unnamed x90 -> x55, local copies, waits for them, and re-layouts: 4.9 us -> 15.5 us
    another operation x11 -> x1, other arithmetic: 11 us -> 1.04 us  [local_shards(): lefts = jnp.stack([feed_rin, weighted, in_key, in_value, in_recept])]
    convert_element_type x5 -> x0, other arithmetic: 9.36 us -> none  [the longest x4 8.96 us: reduce_to_owner(): (wide(own[:, 1]) + wide(from_core[:, 1])).astype(BF)]
    dot_general x5 -> x0, matrix products: 8.77 us -> none  [matmul_last(): lax.dot_general(left, right, (((1,), (1,)), ((), ())), preferred_element_...]
  transfers between devices with their start and end apart: 31 -> 3, of which waited for: 14 -> 1; matrix products, arithmetic and copies ran while one was open for 16% -> 6% of each run, Pallas kernels for 33% -> 26%
where the time goes in v2:
time: 409 us; the launch traced here: 406 us
  Pallas kernels  320 us (78%)
  local copies, waits for them, and re-layouts  26.6 us (7%)
  other arithmetic  15 us (4%)
  between operations  14.5 us (4%)
  matrix products  11.6 us (3%)
  starting transfers between devices  10.3 us (3%)
  waiting for transfers between devices  8.21 us (2%)
    pallas_call x1, Pallas kernels, channel_backward(): pl.pallas_call(channel_backward_kernel, out_shape=[jax.ShapeDtypeStruct((...  111 us
    pallas_call x1, Pallas kernels, front_backward(): pl.pallas_call(front_backward_kernel, out_shape=[jax.ShapeDtypeStruct((co...  91.4 us
    pallas_call x1, Pallas kernels, gather(): pl.pallas_call(functools.partial(gather_kernel, count, chunks), out_shape...  82.4 us
    pallas_call x1, Pallas kernels, forward_scan(): pl.pallas_call(forward_scan_kernel, out_shape=[jax.ShapeDtypeStruct(shape...  21.2 us
    unnamed x55, local copies, waits for them, and re-layouts  15.5 us
    pallas_call x1, Pallas kernels, channel_forward(): pl.pallas_call(channel_forward_kernel, grid=(8,), out_shape=[jax.ShapeDty...  13.2 us
    dot_general x5, matrix products, matmul(): return jnp.dot(left, right, preferred_element_type=jnp.float32)  11.6 us
    ppermute x2, starting transfers between devices, shifted(): return lax.ppermute(block, axis, route)  10.3 us
  transfers between devices with their start and end apart: 3, of which 1 were waited for; matrix products, arithmetic and copies ran while one was open for 6% of the time, Pallas kernels for 26%

profile of v2, /device:TPU:0, one launch (start us, length us, event | category | flops | bytes accessed | tf_op | source)
XLA Modules:
  0.0 405.8 jit_solution(4355652002431830071)
XLA Ops:
  9.5 4.9 %collective-permute-start = (bf16[2,1,1024]{2,1,0:T(2,128)(2,1)S(1)}, bf16[2,1,1024]{2,1,0:T(2,128)(2,1)S(1)}, u32[]{:S(2)}, u32[]{:S(2)}) collective-permute-start(bf16[2,1,1024]{2,1,0:T(2,128)(2,1)S(1)} %slice.165), channel_id=1, source_target_pairs={{0,1},{1,2},{2,3},{3,4},{4,5},{5,6},{6,7},{8,9},{9,10},{10,11},{11... | collective-permute-start | bytes 12296 | tf_op jit(solution)/shard_map/ppermute | solution.py:34
  15.1 82.4 %gather.1 = (bf16[2,2,4,2,16,128]{5,4,3,2,1,0:T(8,128)(2,1)}, bf16[2,2,4,2,32,1024]{5,4,3,2,1,0:T(8,128)(2,1)}, bf16[2,2,4,2,32,1024]{5,4,3,2,1,0:T(8,128)(2,1)}...) custom-call(bf16[16,128]{1,0:T(8,128)(2,1)} %pad.14.refs_0_, ...), custom_call_target="tpu_custom_call" | custom-call | bytes 84934656 | tf_op jit(solution)/shard_map/gather/pallas_call | solution.py:497
  105.1 1.7 fusion.45.keys
  106.8 1.7 fusion.46.values
  108.5 2.0 fusion.33.gates
  111.2 21.2 %forward_scan.1 = (bf16[2,128,1024]{2,1,0:T(8,128)(2,1)}, f32[2,128,1024]{2,1,0:T(8,128)}, f32[2,128,1024]{2,1,0:T(8,128)}, f32[2,128,1024]{2,1,0:T(8,128)}, f32...) custom-call(f32[2,128,1024]{2,1,0:T(8,128)} %bitcast.185, f32[2,128,1024]{2,1,0:T(8,128)} %bitcast.186, ...), custom_call_target="tpu_custom_call" | custom-call | flops 26214400 | bytes 9437184 | tf_op jit(solution)/shard_map/forward_scan/pallas_call | solution.py:639
  132.4 2.6 fusion.44
  136.5 5.4 %collective-permute-start.1 = (bf16[2,1,1024]{2,1,0:T(2,128)(2,1)S(1)}, bf16[2,1,1024]{2,1,0:T(2,128)(2,1)S(1)}, u32[]{:S(2)}, u32[]{:S(2)}) collective-permute-start(bf16[2,1,1024]{2,1,0:T(2,128)(2,1)S(1)} %slice.175), channel_id=1, source_target_pairs={{0,1},{1,2},{2,3},{3,4},{4,5},{5,6},{6,7},{8,9},{9,10},{10,11},{11... | collective-permute-start | bytes 12296 | tf_op jit(solution)/shard_map/ppermute | solution.py:34
  142.1 1.6 fusion.22
  143.9 1.7 convert_subtract_fusion.1
  147.2 1.3 fusion.31
  150.7 8.2 %all-gather.2.cloned.1.call-done = bf16[4096,2048]{1,0:T(8,128)(2,1)} async-done(((bf16[128,2048]{1,0:T(8,128)(2,1)}), bf16[4096,2048]{1,0:T(8,128)(2,1)}) %all-gather.2.cloned.1.call-update) | async-done | bytes 16777232 | tf_op jit(solution)/shard_map/all_gather | solution.py:1340
  158.9 13.2 %channel_forward.1 = (f32[8,256,512]{2,1,0:T(8,128)}, f32[256,1024]{1,0:T(8,128)}) custom-call(bf16[256,1024]{1,0:T(8,128)(2,1)} %bitcast.189, bf16[2,2,4,2,128,2048]{5,4,3,2,1,0:T(8,128)(2,1)} %bitcast.178, bf16[2,2,4,2,128,2048]{5,4,3,2,1,0:T(8,128)(2,1)} %bitcast.179), custom_call_target="tpu_custom_call" | custom-call | flops 4294967296 | bytes 20971520 | tf_op jit(solution)/shard_map/channel_forward/pallas_call | solution.py:676
  172.1 3.7 fusion.6
  178.5 111.4 %channel_backward.1 = (bf16[2,4,128,1024]{3,2,1,0:T(8,128)(2,1)}, bf16[256,1024]{1,0:T(8,128)(2,1)}, bf16[256,1024]{1,0:T(8,128)(2,1)}, bf16[256,1024]{1,0:T(8,1...) custom-call(bf16[256,1024]{1,0:T(8,128)(2,1)} %bitcast.190, ...), custom_call_target="tpu_custom_call" | custom-call | flops 8589934592 | bytes 67108864 | tf_op jit(solution)/shard_map/channel_backward/pallas_call | solution.py:1025
  289.9 1.9 bitcast_dynamic-update-slice_fusion.3
  291.8 1.9 bitcast_dynamic-update-slice_fusion.2
  293.7 1.9 bitcast_dynamic-update-slice_fusion.1
  297.8 91.4 %front_backward.1 = (f32[5,32,1024]{2,1,0:T(8,128)}, f32[4,128,1024]{2,1,0:T(8,128)}, f32[4,128,1024]{2,1,0:T(8,128)}, f32[256,1024]{1,0:T(8,128)}, f32[16,1024]{1,0:T(8,128)}) custom-call(bf16[2,4,128,1024]{3,2,1,0:T(8,128)(2,1)} %get-tuple-element.72.feed_part, bf16[5,256,1024]{2,1,0:T(8,128)(2,1)} %fusion.29.lefts, ...), custom_call_target="tpu_custom_call" | custom-call | flops 5368709120 | bytes 41943040 | tf_op jit(solution)/shard_map/front_backward/pallas_call | solution.py:1285
  389.2 2.1 slice_bitcast_fusion
  391.3 1.6 dynamic-slice_bitcast_fusion
  392.9 2.3 copy.60
  395.2 1.3 copy.61
  397.6 1.3 copy.62
  (110 shorter events, 22.7 us)
Async XLA Ops:
  7.2 2.2 copy-start
  7.2 7.2 %copy-start.11 = (bf16[32]{0:T(256)(128)(2,1)S(1)}, bf16[32]{0:T(256)(128)(2,1)}, u32[]{:S(2)}) copy-start(bf16[32]{0:T(256)(128)(2,1)} %param.33) | copy-start | bytes 196
  7.2 7.2 %copy-start.12 = (bf16[32]{0:T(256)(128)(2,1)S(1)}, bf16[32]{0:T(256)(128)(2,1)}, u32[]{:S(2)}) copy-start(bf16[32]{0:T(256)(128)(2,1)} %param.34) | copy-start | bytes 196
  7.2 7.2 %copy-start.13 = (bf16[32]{0:T(256)(128)(2,1)S(1)}, bf16[32]{0:T(256)(128)(2,1)}, u32[]{:S(2)}) copy-start(bf16[32]{0:T(256)(128)(2,1)} %param.35) | copy-start | bytes 196
  7.2 7.2 %copy-start.14 = (bf16[32]{0:T(256)(128)(2,1)S(1)}, bf16[32]{0:T(256)(128)(2,1)}, u32[]{:S(2)}) copy-start(bf16[32]{0:T(256)(128)(2,1)} %param.36) | copy-start | bytes 196
  7.2 7.2 %copy-start.15 = (bf16[32]{0:T(256)(128)(2,1)S(1)}, bf16[32]{0:T(256)(128)(2,1)}, u32[]{:S(2)}) copy-start(bf16[32]{0:T(256)(128)(2,1)} %param.37) | copy-start | bytes 196
  7.3 7.2 %copy-start.16 = (bf16[32]{0:T(256)(128)(2,1)S(1)}, bf16[32]{0:T(256)(128)(2,1)}, u32[]{:S(2)}) copy-start(bf16[32]{0:T(256)(128)(2,1)} %param.38) | copy-start | bytes 196
  7.3 7.2 %copy-start.17 = (bf16[32]{0:T(256)(128)(2,1)S(1)}, bf16[32]{0:T(256)(128)(2,1)}, u32[]{:S(2)}) copy-start(bf16[32]{0:T(256)(128)(2,1)} %param.39) | copy-start | bytes 196
  7.3 7.2 %copy-start.18 = (bf16[32]{0:T(256)(128)(2,1)S(1)}, bf16[32]{0:T(256)(128)(2,1)}, u32[]{:S(2)}) copy-start(bf16[32]{0:T(256)(128)(2,1)} %param.40) | copy-start | bytes 196
  7.3 7.2 %copy-start.19 = (bf16[32]{0:T(256)(128)(2,1)S(1)}, bf16[32]{0:T(256)(128)(2,1)}, u32[]{:S(2)}) copy-start(bf16[32]{0:T(256)(128)(2,1)} %param.41) | copy-start | bytes 196
  7.3 7.2 %copy-start.20 = (bf16[32]{0:T(256)(128)(2,1)S(1)}, bf16[32]{0:T(256)(128)(2,1)}, u32[]{:S(2)}) copy-start(bf16[32]{0:T(256)(128)(2,1)} %param.42) | copy-start | bytes 196
  7.3 7.2 %copy-start.21 = (bf16[32]{0:T(256)(128)(2,1)S(1)}, bf16[32]{0:T(256)(128)(2,1)}, u32[]{:S(2)}) copy-start(bf16[32]{0:T(256)(128)(2,1)} %param.43) | copy-start | bytes 196
  7.3 151.5 %all-gather.2.cloned.1.call-start = ((), (), s32[]{:S(2)}) async-start(), calls=%async_computation | async-start | bytes 17301504 | tf_op jit(solution)/shard_map/all_gather | solution.py:1340
  8.5 91.1 %copy-start.10 = (s32[2,1,128]{2,1,0:T(1,128)S(1)}, s32[2,1,128]{2,1,0:T(1,128)}, u32[]{:S(2)}) copy-start(s32[2,1,128]{2,1,0:T(1,128)} %param.24) | copy-start | bytes 3076
  9.5 93.4 %collective-permute-start = (bf16[2,1,1024]{2,1,0:T(2,128)(2,1)S(1)}, bf16[2,1,1024]{2,1,0:T(2,128)(2,1)S(1)}, u32[]{:S(2)}, u32[]{:S(2)}) collective-permute-start(bf16[2,1,1024]{2,1,0:T(2,128)(2,1)S(1)} %slice.165), channel_id=1, source_target_pairs={{0,1},{1,2},{2,3},{3,4},{4,5},{5,6},{6,7},{8,9},{9,10},{10,11},{11... | collective-permute-start | bytes 12296 | tf_op jit(solution)/shard_map/ppermute | solution.py:34
  103.3 3.5 copy-start.4
  135.0 7.0 %copy-start.1 = (f32[2,127,1024]{2,1,0:T(8,128)S(1)}, f32[2,127,1024]{2,1,0:T(8,128)}, u32[]{:S(2)}) copy-start(f32[2,127,1024]{2,1,0:T(8,128)} %fusion.28) | copy-start | bytes 3121156
  136.5 7.3 %collective-permute-start.1 = (bf16[2,1,1024]{2,1,0:T(2,128)(2,1)S(1)}, bf16[2,1,1024]{2,1,0:T(2,128)(2,1)S(1)}, u32[]{:S(2)}, u32[]{:S(2)}) collective-permute-start(bf16[2,1,1024]{2,1,0:T(2,128)(2,1)S(1)} %slice.175), channel_id=1, source_target_pairs={{0,1},{1,2},{2,3},{3,4},{4,5},{5,6},{6,7},{8,9},{9,10},{10,11},{11... | collective-permute-start | bytes 12296 | tf_op jit(solution)/shard_map/ppermute | solution.py:34
  143.8 2.6 copy-start.5
  158.9 13.2 %copy-start.8 = (bf16[2,1,128,1024]{3,2,1,0:T(8,128)(2,1)S(1)}, bf16[2,1,128,1024]{3,2,1,0:T(8,128)(2,1)}, u32[]{:S(2)}) copy-start(bf16[2,1,128,1024]{3,2,1,0:T(8,128)(2,1)} %param.25) | copy-start | bytes 1572868
  175.7 2.7 copy-start.2
  289.8 5.7 %copy-start.9 = (bf16[256,1024]{1,0:T(8,128)(2,1)S(1)}, bf16[256,1024]{1,0:T(8,128)(2,1)}, u32[]{:S(2)}) copy-start(bf16[256,1024]{1,0:T(8,128)(2,1)} %get-tuple-element.76) | copy-start | bytes 1572868
  389.2 6.1 %copy-start.7 = (f32[4,128,1024]{2,1,0:T(8,128)S(1)}, f32[4,128,1024]{2,1,0:T(8,128)}, u32[]{:S(2)}) copy-start(f32[4,128,1024]{2,1,0:T(8,128)} %get-tuple-element.81) | copy-start | bytes 6291460
  395.2 2.3 copy-start.6
  (2 other events, 3.9 us)
Sparse Core Ops, SparseCore 0:
  11.2 147.6 all-gather.1

commit v3 on v2

--- a/solution.py
+++ b/solution.py
@@ -415,101 +415,6 @@
     return pl.BlockSpec(memory_space=pl.ANY)
 
 
-def gather_kernel(count, chunks, *refs):
-    ins, outs = refs[:count], refs[count : 2 * count]
-    send, recv, local_sem = refs[2 * count :]
-    dp, t = lax.axis_index("dp"), lax.axis_index("tensor")
-    x, c, z, y = dp // 2, dp % 2, t // 2, t % 2
-    over_x, over_y, over_core = (1 - x) * 2 + c, z * 2 + 1 - y, x * 2 + 1 - c
-    first = (jnp.where(c == 0, dp, over_x), jnp.where(c == 0, over_y, t))
-    second = (jnp.where(c == 0, over_x, dp), jnp.where(c == 0, t, over_y))
-    x_first, y_first = jnp.where(c == 0, x, 1 - x), jnp.where(c == 0, 1 - y, y)
-    along_z = [(dp, lax.rem(z + o, 4) * 2 + y) for o in (1, 2, 3)]
-    barrier = pltpu.get_barrier_semaphore()
-    peers = along_z + [(over_x, t), (dp, over_y), (over_core, t)]
-    for peer in peers:
-        pl.semaphore_signal(barrier, inc=1, device_id=peer, device_id_type=MESH_ID)
-    pl.semaphore_wait(barrier, len(peers))
-
-    def copy(source, target, k, j, device):
-        return pltpu.make_async_remote_copy(
-            src_ref=source,
-            dst_ref=target,
-            send_sem=send.at[k, j],
-            recv_sem=recv.at[k, j],
-            device_id=device,
-            device_id_type=MESH_ID,
-        )
-
-    copies = {}
-
-    def begin(k, j, source, target, device):
-        copies[k, j] = copy(source, target, k, j, device)
-        copies[k, j].start()
-
-    def column(k, xx, yy):
-        i, start, rows = chunks[k]
-        return outs[i].at[xx, c, :, yy, pl.ds(start, rows)]
-
-    own = []
-    for i in range(count):
-        own.append(pltpu.make_async_copy(ins[i], outs[i].at[x, c, z, y], local_sem.at[i]))
-        own[i].start()
-    steps = len(chunks)
-    for k in range(steps):
-        i, start, rows = chunks[k]
-        for o in range(3):
-            begin(k, o, ins[i].at[pl.ds(start, rows)], outs[i].at[x, c, z, y, pl.ds(start, rows)], along_z[o])
-    for i in range(count):
-        own[i].wait()
-    for s in range(steps + 2):
-        if s < steps:
-            for o in range(3):
-                copies[s, o].wait_recv()
-            begin(s, 3, column(s, x, y), column(s, x, y), first)
-            begin(s, 4, column(s, x, y), column(s, x, y), second)
-        if 0 <= s - 1 < steps:
-            k = s - 1
-            copies[k, 3].wait_recv()
-            begin(k, 5, column(k, x_first, y_first), column(k, x_first, y_first), second)
-        if 0 <= s - 2 < steps:
-            k = s - 2
-            i, start, rows = chunks[k]
-            copies[k, 4].wait_recv()
-            copies[k, 5].wait_recv()
-            half = outs[i].at[:, c, :, :, pl.ds(start, rows)]
-            begin(k, 6, half, half, (over_core, t))
-    for k in range(steps):
-        copies[k, 6].wait_recv()
-    for k in range(steps):
-        for j in range(7):
-            copies[k, j].wait_send()
-
-
-def gather(parts):
-    count = len(parts)
-    chunks = []
-    for i, part in enumerate(parts):
-        for start in range(0, part.shape[0], 16):
-            chunks.append((i, start, 16))
-    outs = [jax.ShapeDtypeStruct((2, 2, 4, 2) + p.shape, p.dtype) for p in parts]
-    moved = sum(2 * 32 * p.size for p in parts)
-    return pl.pallas_call(
-        functools.partial(gather_kernel, count, chunks),
-        out_shape=outs,
-        in_specs=[anywhere()] * count,
-        out_specs=[anywhere()] * count,
-        scratch_shapes=[
-            pltpu.SemaphoreType.DMA((len(chunks), 7)),
-            pltpu.SemaphoreType.DMA((len(chunks), 7)),
-            pltpu.SemaphoreType.DMA((count,)),
-        ],
-        compiler_params=pltpu.CompilerParams(collective_id=0, has_side_effects=True),
-        cost_estimate=cost(0, 8 * moved),
-        name="gather",
-    )(*parts)
-
-
 def roll_rows(value, distance, fill, row):
     size = value.shape[0]
     moved = pltpu.roll(value, distance % size, 0)
@@ -527,27 +432,24 @@
     return factor, up, low
 
 
-def greet_row(t, dp, size):
-    barrier = pltpu.get_barrier_semaphore()
-    for o in range(1, size):
-        pl.semaphore_signal(barrier, inc=1, device_id=(dp, lax.rem(t + o, size)), device_id_type=MESH_ID)
-    pl.semaphore_wait(barrier, size - 1)
+def row_copies(summary, arrived, send, recv, t, dp, size):
+    return [
+        pltpu.make_async_remote_copy(
+            src_ref=summary,
+            dst_ref=arrived.at[o],
+            send_sem=send.at[o],
+            recv_sem=recv.at[o],
+            device_id=(dp, lax.rem(t + o, size)),
+            device_id_type=MESH_ID,
+        )
+        for o in range(1, size)
+    ]
 
 
 def share_row(summary, arrived, send, recv, t, dp, size):
-    copies = []
-    for o in range(1, size):
-        copies.append(
-            pltpu.make_async_remote_copy(
-                src_ref=summary,
-                dst_ref=arrived.at[o],
-                send_sem=send.at[o],
-                recv_sem=recv.at[o],
-                device_id=(dp, lax.rem(t + o, size)),
-                device_id_type=MESH_ID,
-            )
-        )
-        copies[-1].start()
+    copies = row_copies(summary, arrived, send, recv, t, dp, size)
+    for copy in copies:
+        copy.start()
     for copy in copies:
         copy.wait_recv()
     return copies
@@ -555,136 +457,6 @@
 
 def lanes(j):
     return pl.ds(pl.multiple_of(j * 128, 128), 128)
-
-
-def forward_scan_kernel(
-    keys, values, gates, keep, vectors, weighted, denom, mixed, prior_a, prior_b, recept,
-    cum, up, low, summary, arrived, entering_rows, send, recv,
-):
-    dp, t = lax.axis_index("dp"), lax.axis_index("tensor")
-    size = arrived.shape[0]
-    micro, rows = keys.shape[:2]
-    greet_row(t, dp, size)
-    row = lax.broadcasted_iota(jnp.int32, (rows, 128), 0)
-    summary[...] = jnp.zeros_like(summary)
-    for m in range(micro):
-
-        def first_pass(j, carry, m=m):
-            at = lanes(j)
-            power = jnp.exp(keys[m, :, at])
-            factor = keep[m] * vectors[0:1, at]
-            f, a, b = doubling(factor, power * values[m, :, at], power, row, 1)
-            cum[m, :, at] = f
-            up[m, :, at] = a
-            low[m, :, at] = b
-            summary[3 * m : 3 * m + 1, at] = f[rows - 1 :]
-            summary[3 * m + 1 : 3 * m + 2, at] = a[rows - 1 :]
-            summary[3 * m + 2 : 3 * m + 3, at] = b[rows - 1 :]
-            return carry
-
-        lax.fori_loop(0, keys.shape[2] // 128, first_pass, 0)
-    copies = share_row(summary, arrived, send, recv, t, dp, size)
-    for m in range(micro):
-        a = jnp.zeros((1, keys.shape[2]), F32)
-        b = jnp.zeros((1, keys.shape[2]), F32)
-        for o in range(size - 1, 0, -1):
-            f = arrived[o, 3 * m : 3 * m + 1]
-            a = jnp.where(t >= o, f * a + arrived[o, 3 * m + 1 : 3 * m + 2], a)
-            b = jnp.where(t >= o, f * b + arrived[o, 3 * m + 2 : 3 * m + 3], b)
-        entering_rows[2 * m : 2 * m + 1] = a
-        entering_rows[2 * m + 1 : 2 * m + 2] = b
-    for m in range(micro):
-
-        def second_pass(j, carry, m=m):
-            at = lanes(j)
-            enter_a = entering_rows[2 * m : 2 * m + 1, at]
-            enter_b = entering_rows[2 * m + 1 : 2 * m + 2, at]
-            f = cum[m, :, at]
-            before_a = roll_rows(up[m, :, at] + f * enter_a, 1, enter_a, row)
-            before_b = roll_rows(low[m, :, at] + f * enter_b, 1, enter_b, row)
-            bonus = jnp.exp(vectors[1:2, at] + keys[m, :, at])
-            below = keep[m] * before_b + bonus
-            blended = (keep[m] * before_a + bonus * values[m, :, at]) / below
-            gate = jax.nn.sigmoid(gates[m, :, at])
-            weighted[m, :, at] = (gate * blended).astype(BF)
-            denom[m, :, at] = below
-            mixed[m, :, at] = blended
-            prior_a[m, :, at] = before_a
-            prior_b[m, :, at] = before_b
-            recept[m, :, at] = gate
-            return carry
-
-        lax.fori_loop(0, keys.shape[2] // 128, second_pass, 0)
-    for copy in copies:
-        copy.wait_send()
-
-
-def scan_scratch(shape, size):
-    width = shape[-1]
-    return [
-        pltpu.VMEM(shape, F32),
-        pltpu.VMEM(shape, F32),
-        pltpu.VMEM(shape, F32),
-        pltpu.VMEM((8, width), F32),
-        pltpu.VMEM((size, 8, width), F32),
-        pltpu.VMEM((8, width), F32),
-        pltpu.SemaphoreType.DMA((size,)),
-        pltpu.SemaphoreType.DMA((size,)),
-    ]
-
-
-def forward_scan(keys, values, gates, keep, vectors, size):
-    shape = keys.shape
-    full = jax.ShapeDtypeStruct(shape, F32)
-    return pl.pallas_call(
-        forward_scan_kernel,
-        out_shape=[jax.ShapeDtypeStruct(shape, BF)] + [full] * 5,
-        in_specs=[whole()] * 5,
-        out_specs=[whole()] * 6,
-        scratch_shapes=scan_scratch(shape, size),
-        compiler_params=pltpu.CompilerParams(collective_id=1, has_side_effects=True),
-        cost_estimate=cost(100 * keys.size, 36 * keys.size),
-        name="forward_scan",
-    )(keys, values, gates, keep, vectors)
-
-
-def channel_forward_kernel(feed_in, key_block, value_block, positive, total):
-    rows = 4 * key_block.shape[-2]
-    keys = key_block[...].reshape(rows, key_block.shape[-1])
-    hidden = jnp.maximum(matmul_last(feed_in[...], keys), 0.0)
-    positive[0] = hidden
-    squares = (hidden * hidden).astype(BF)
-    part = matmul(squares, value_block[...].reshape(rows, value_block.shape[-1]))
-
-    @pl.when(pl.program_id(0) == 0)
-    def _():
-        total[...] = part
-
-    @pl.when(pl.program_id(0) > 0)
-    def _():
-        total[...] += part
-
-
-def channel_forward(feed_in, weights):
-    tokens, width = feed_in.shape
-    rows = weights.shape[4]
-    units = 32 * rows
-
-    def block(side):
-        return pl.BlockSpec((1, 1, 4, 1, rows, width), lambda i: (i // 4, (i // 2) % 2, 0, i % 2, 0, side))
-
-    return pl.pallas_call(
-        channel_forward_kernel,
-        grid=(8,),
-        out_shape=[jax.ShapeDtypeStruct((8, tokens, 4 * rows), F32), jax.ShapeDtypeStruct((tokens, width), F32)],
-        in_specs=[pl.BlockSpec((tokens, width), lambda i: (0, 0)), block(0), block(1)],
-        out_specs=[
-            pl.BlockSpec((1, tokens, 4 * rows), lambda i: (i, 0, 0)),
-            pl.BlockSpec((tokens, width), lambda i: (0, 0)),
-        ],
-        cost_estimate=cost(4 * tokens * units * width, 4 * units * width + 4 * tokens * units),
-        name="channel_forward",
-    )(feed_in, weights, weights)
 
 
 def owner(i, x, y, c):
@@ -779,10 +551,449 @@
 GAIN_ONE, BIAS_ONE, GAIN_TWO, BIAS_TWO, MIX_KEY, MIX_VALUE, MIX_RECEPT, DECAY, PREMIUM, BLEND_KEY, BLEND_RECEPT = range(11)
 
 
+def norm_tiles(source, unit, inverse):
+    rows, width = source.shape
+    tile = min(rows, 32)
+
+    def turn(k, carry):
+        at = pl.ds(pl.multiple_of(k * tile, tile), tile)
+        value = source[at, :].astype(F32)
+        center = value - jnp.sum(value, axis=-1, keepdims=True) * (1.0 / width)
+        scale = lax.rsqrt(jnp.sum(center * center, axis=-1, keepdims=True) * (1.0 / width) + EPSILON)
+        unit[at, :] = center * scale
+        inverse[at, :] = jnp.broadcast_to(scale, (tile, 128))
+        return carry
+
+    lax.fori_loop(0, rows // tile, turn, 0)
+
+
+def dot_columns(finish, left, right):
+    tile = 256
+    depth = left.shape[1]
+
+    def turn(n, carry):
+        at = pl.ds(pl.multiple_of(n * tile, tile), tile)
+        finish(at, matmul(left[...], right[:, :, :, :, :, at].reshape(depth, tile)))
+        return carry
+
+    lax.fori_loop(0, right.shape[5] // tile, turn, 0)
+
+
+SKEW = 2
+
+
+def forward_kernel(
+    tokens, cotangent, keep,
+    own_vectors, own_key, own_value, own_recept, own_output, own_feedr, own_feed,
+    all_vectors, all_key, all_value, all_recept, all_output, all_feedr, all_feed,
+    result, table_out, rates_out, lefts, feed_in_out, grad_value_out, grad_gate_out, positive, spread_one_out,
+    unit_one_out, inverse_one_out, spread_two_out, unit_two_out, inverse_two_out, keys_out, values_out, denom_out,
+    mixed_out, prior_a_out, prior_b_out, recept_out,
+    packed, table, rates, squares, feed_slot, positive_slot, left_parts, feed_in, grad_value, grad_gate, spread_one,
+    unit_one, inverse_one, spread_two, unit_two, inverse_two, keys, values, gates, denom, mixed, prior_a, prior_b,
+    cum, up, low, residual, total, halo_tokens, halo_unit, halo_inverse, summary, arrived, entering_rows, halo_out, halo_in,
+    send, recv, own_sem, load_sem, out_sem, slot_sem, scan_send, scan_recv, halo_send, halo_recv,
+):
+    size = arrived.shape[0]
+    links = Links(size)
+    x, c, z, y, t, dp = links.x, links.c, links.z, links.y, links.t, links.dp
+    count, width = tokens.shape
+    micro, length = keep.shape[:2]
+    ins = [own_vectors, own_key, own_value, own_recept, own_output, own_feedr, own_feed]
+    outs = [all_vectors, all_key, all_value, all_recept, all_output, all_feedr, all_feed]
+    piece = 16
+    chunks = [(i, r) for i in range(7) for r in range(0, ins[i].shape[0], piece)]
+    steps = len(chunks)
+    feed_steps = ins[6].shape[0] // piece
+    feed_base = steps - feed_steps
+    x_first, y_first = jnp.where(c == 0, x, 1 - x), jnp.where(c == 0, 1 - y, y)
+    first, second = links.first, links.second
+
+    def place(n):
+        if isinstance(n, int):
+            i, start = chunks[n]
+            return i, pl.ds(start, piece)
+        return 6, pl.ds(pl.multiple_of((n - feed_base) * piece, piece), piece)
+
+    def copy_z(n, o):
+        i, at = place(n)
+        return remote(ins[i].at[at], outs[i].at[x, c, z, y, at], send.at[n, o], recv.at[n, o], links.along_z[o])
+
+    def copy_column(n, j, xx, yy, device):
+        i, at = place(n)
+        column = outs[i].at[xx, c, :, yy, at]
+        return remote(column, column, send.at[n, j], recv.at[n, j], device)
+
+    def copy_first(n):
+        return copy_column(n, 3, x, y, first)
+
+    def copy_second(n):
+        return copy_column(n, 4, x, y, second)
+
+    def copy_passed(n):
+        return copy_column(n, 5, x_first, y_first, second)
+
+    def copy_core(n):
+        i, at = place(n)
+        half = outs[i].at[:, c, :, :, at]
+        return remote(half, half, send.at[n, 6], recv.at[n, 6], links.core)
+
+    def step_a(n):
+        for o in range(3):
+            copy_z(n, o).wait_recv()
+        copy_first(n).start()
+        copy_second(n).start()
+
+    def step_b(n):
+        copy_first(n).wait_recv()
+        copy_passed(n).start()
+
+    def step_c(n):
+        copy_second(n).wait_recv()
+        copy_passed(n).wait_recv()
+        copy_core(n).start()
+
+    def advance(*numbers):
+        for s in numbers:
+            if s < steps:
+                step_a(s)
+            if 0 <= s - SKEW < steps:
+                step_b(s - SKEW)
+            if 0 <= s - 2 * SKEW < steps:
+                step_c(s - 2 * SKEW)
+
+    def load(k):
+        return pltpu.make_async_copy(outs[1 + k], squares.at[k], load_sem.at[k])
+
+    def ready(k):
+        for n in (2 * k + 1, 2 * k + 2):
+            copy_core(n).wait_recv()
+        load(k).start()
+
+    written = []
+
+    def write(source, target):
+        copy = pltpu.make_async_copy(source, target, out_sem.at[len(written)])
+        copy.start()
+        written.append(copy)
+
+    owns = [pltpu.make_async_copy(ins[i], outs[i].at[x, c, z, y], own_sem.at[i]) for i in range(7)]
+    for own in owns:
+        own.start()
+    links.greet(True)
+    for n in range(steps):
+        for o in range(3):
+            copy_z(n, o).start()
+    halo_copies = [
+        remote(
+            tokens.at[pl.ds((m + 1) * length - piece, piece)], halo_tokens.at[pl.ds(m * piece, piece)],
+            halo_send.at[m], halo_recv.at[m], links.row(1),
+        )
+        for m in range(micro)
+    ]
+    for halo in halo_copies:
+        halo.start()
+    summary[...] = jnp.zeros_like(summary)
+    halo_out[...] = jnp.zeros_like(halo_out)
+    total[...] = jnp.zeros_like(total)
+    for own in owns:
+        own.wait()
+    advance(0, 1)
+    norm_tiles(tokens, unit_one, inverse_one)
+    write(unit_one, unit_one_out)
+    write(inverse_one, inverse_one_out)
+    advance(2, 3, 4)
+    for halo in halo_copies:
+        halo.wait_recv()
+    norm_tiles(halo_tokens, halo_unit, halo_inverse)
+    copy_core(0).wait_recv()
+
+    vector_load = pltpu.make_async_copy(all_vectors, packed, load_sem.at[5])
+    vector_load.start()
+    advance(5)
+    vector_load.wait()
+    share = width // 32
+    per = 128 // share
+    for j in range(width // 128):
+        value = None
+        for q in range(per):
+            d = j * per + q
+            part = packed[d // 16, (d // 8) % 2, (d // 2) % 4, d % 2].astype(F32)
+            part = pltpu.roll(part, q * share, 1) if q else part
+            value = part if value is None else value + part
+        table[:, j * 128 : (j + 1) * 128] = value
+    speed = jnp.exp(table[DECAY : DECAY + 1, :])
+    rates[...] = jnp.broadcast_to(speed, rates.shape)
+    table[DECAY : DECAY + 1, :] = jnp.exp(-speed)
+    write(table, table_out)
+    write(rates, rates_out)
+    row = lax.broadcasted_iota(jnp.int32, (length, 128), 0)
+
+    def vector(k, at):
+        return table[k : k + 1, at]
+
+    def normed(unit, gain, bias, at):
+        return (unit * vector(gain, at) + vector(bias, at)).astype(BF).astype(F32)
+
+    def blends(spread, unit, m, prior, gain, bias, mixes):
+        rows_at = slice(m * length, (m + 1) * length)
+
+        def turn(j, carry):
+            at = lanes(j)
+            now = normed(unit[rows_at, at], gain, bias, at)
+            before = roll_rows(now, 1, jnp.where(t > 0, prior(at), 0.0), row) * keep[m]
+            spread[rows_at, at] = now - before
+            for target, mix in mixes:
+                target[rows_at, at] = (now * vector(mix, at) + before * (1.0 - vector(mix, at))).astype(BF)
+            return carry
+
+        lax.fori_loop(0, width // 128, turn, 0)
+
+    mixes = [(left_parts.at[2 + k], MIX_KEY + k) for k in range(3)]
+    for m in range(micro):
+        last = (m + 1) * piece - 1
+
+        def prior(at, last=last):
+            return normed(halo_unit[last : last + 1, at], GAIN_ONE, BIAS_ONE, at)
+
+        blends(spread_one, unit_one, m, prior, GAIN_ONE, BIAS_ONE, mixes)
+        advance(6 + m)
+    write(spread_one, spread_one_out)
+    for k in range(3):
+        write(left_parts.at[2 + k], lefts.at[2 + k])
+
+    def keep_in(target):
+        def finish(at, value):
+            target[:, at] = value
+
+        return finish
+
+    ready(0)
+    advance(8)
+    load(0).wait()
+    dot_columns(keep_in(keys), left_parts.at[2], squares.at[0])
+    write(keys, keys_out)
+    ready(1)
+    advance(9, 10)
+    load(1).wait()
+    dot_columns(keep_in(values), left_parts.at[3], squares.at[1])
+    write(values, values_out)
+
+    for m in range(micro):
+        rows_at = slice(m * length, (m + 1) * length)
+
+        def first_pass(j, carry, m=m, rows_at=rows_at):
+            at = lanes(j)
+            power = jnp.exp(keys[rows_at, at])
+            f, a, b = doubling(keep[m] * vector(DECAY, at), power * values[rows_at, at], power, row, 1)
+            cum[rows_at, at] = f
+            up[rows_at, at] = a
+            low[rows_at, at] = b
+            summary[3 * m : 3 * m + 1, at] = f[length - 1 :]
+            summary[3 * m + 1 : 3 * m + 2, at] = a[length - 1 :]
+            summary[3 * m + 2 : 3 * m + 3, at] = b[length - 1 :]
+            return carry
+
+        lax.fori_loop(0, width // 128, first_pass, 0)
+        advance(11 + m)
+    scan_copies = row_copies(summary, arrived, scan_send, scan_recv, t, dp, size)
+    for copy in scan_copies:
+        copy.start()
+    ready(2)
+    load(2).wait()
+
+    def finish_gate(at, value):
+        gates[:, at] = jax.nn.sigmoid(value)
+
+    dot_columns(finish_gate, left_parts.at[4], squares.at[2])
+    write(gates, recept_out)
+    for copy in scan_copies:
+        copy.wait_recv()
+    for m in range(micro):
+        a = jnp.zeros((1, width), F32)
+        b = jnp.zeros((1, width), F32)
+        for o in range(size - 1, 0, -1):
+            f = arrived[o, 3 * m : 3 * m + 1]
+            a = jnp.where(t >= o, f * a + arrived[o, 3 * m + 1 : 3 * m + 2], a)
+            b = jnp.where(t >= o, f * b + arrived[o, 3 * m + 2 : 3 * m + 3], b)
+        entering_rows[2 * m : 2 * m + 1] = a
+        entering_rows[2 * m + 1 : 2 * m + 2] = b
+    advance(13)
+    for m in range(micro):
+        rows_at = slice(m * length, (m + 1) * length)
+
+        def second_pass(j, carry, m=m, rows_at=rows_at):
+            at = lanes(j)
+            enter_a = entering_rows[2 * m : 2 * m + 1, at]
+            enter_b = entering_rows[2 * m + 1 : 2 * m + 2, at]
+            f = cum[rows_at, at]
+            before_a = roll_rows(up[rows_at, at] + f * enter_a, 1, enter_a, row)
+            before_b = roll_rows(low[rows_at, at] + f * enter_b, 1, enter_b, row)
+            bonus = jnp.exp(vector(PREMIUM, at) + keys[rows_at, at])
+            below = keep[m] * before_b + bonus
+            blended = (keep[m] * before_a + bonus * values[rows_at, at]) / below
+            left_parts[1, rows_at, at] = (gates[rows_at, at] * blended).astype(BF)
+            denom[rows_at, at] = below
+            mixed[rows_at, at] = blended
+            prior_a[rows_at, at] = before_a
+            prior_b[rows_at, at] = before_b
+            return carry
+
+        lax.fori_loop(0, width // 128, second_pass, 0)
+    write(left_parts.at[1], lefts.at[1])
+    write(denom, denom_out)
+    write(mixed, mixed_out)
+    write(prior_a, prior_a_out)
+    write(prior_b, prior_b_out)
+    ready(3)
+    advance(14)
+    load(3).wait()
+
+    def finish_residual(at, value):
+        residual[:, at] = tokens[:, at].astype(F32) + value
+
+    dot_columns(finish_residual, left_parts.at[1], squares.at[3])
+    norm_tiles(residual, unit_two, inverse_two)
+    write(unit_two, unit_two_out)
+    write(inverse_two, inverse_two_out)
+    for m in range(micro):
+        last = (m + 1) * length - 1
+        halo_out[m : m + 1, :] = normed(unit_two[last : last + 1, :], GAIN_TWO, BIAS_TWO, slice(None))
+    halo_two = remote(halo_out, halo_in, halo_send.at[micro], halo_recv.at[micro], links.row(1))
+    halo_two.start()
+    ready(4)
+    advance(15)
+    halo_two.wait_recv()
+    mixes = [(feed_in, BLEND_KEY), (left_parts.at[0], BLEND_RECEPT)]
+    for m in range(micro):
+
+        def prior(at, m=m):
+            return halo_in[m : m + 1, at]
+
+        blends(spread_two, unit_two, m, prior, GAIN_TWO, BIAS_TWO, mixes)
+    write(spread_two, spread_two_out)
+    write(feed_in, feed_in_out)
+    write(left_parts.at[0], lefts.at[0])
+    advance(16)
+    load(4).wait()
+
+    def finish_second_gate(at, value):
+        cum[:, at] = jax.nn.sigmoid(value)
+
+    dot_columns(finish_second_gate, left_parts.at[0], squares.at[4])
+
+    def arrive(s, carry):
+        @pl.when(s + 2 * SKEW < feed_steps)
+        def _():
+            step_a(feed_base + s + 2 * SKEW)
+
+        @pl.when(s + SKEW < feed_steps)
+        def _():
+            step_b(feed_base + s + SKEW)
+
+        @pl.when(s < feed_steps)
+        def _():
+            step_c(feed_base + s)
+
+        k = s - SKEW
+        slot = lax.rem(s, 2)
+        at = pl.ds(pl.multiple_of(k * piece, piece), piece)
+        copy_core(feed_base + k).wait_recv()
+        fetch = pltpu.make_async_copy(outs[6].at[:, :, :, :, at], feed_slot, slot_sem.at[0])
+        fetch.start()
+
+        def put(k, slot):
+            at = pl.ds(pl.multiple_of(k * piece, piece), piece)
+            return pltpu.make_async_copy(positive_slot.at[slot], positive.at[:, :, :, :, at], slot_sem.at[1 + slot])
+
+        @pl.when(k >= 2)
+        def _():
+            put(k - 2, slot).wait()
+
+        fetch.wait()
+        units = 32 * piece
+        hidden = jnp.maximum(matmul_last(feed_slot[:, :, :, :, :, :width].reshape(units, width), feed_in[...]), 0.0)
+        positive_slot[slot] = hidden.reshape(positive_slot.shape[1:])
+        put(k, slot).start()
+        hidden_squares = (hidden * hidden).astype(BF)
+        total[...] += matmul_lead(hidden_squares, feed_slot[:, :, :, :, :, width:].reshape(units, width))
+
+        @pl.when(k == feed_steps - 1)
+        def _():
+            put(k - 1, 1 - slot).wait()
+            put(k, slot).wait()
+
+        return carry
+
+    lax.fori_loop(SKEW, feed_steps + SKEW, arrive, 0)
+
+    def last_pass(k, carry):
+        at = pl.ds(pl.multiple_of(k * 32, 32), 32)
+        gate, value_out, grad = cum[at, :], total[at, :], cotangent[at, :].astype(F32)
+        residual[at, :] = residual[at, :] + gate * value_out
+        grad_value[at, :] = (grad * gate).astype(BF)
+        grad_gate[at, :] = (grad * value_out * gate * (1.0 - gate)).astype(BF)
+        return carry
+
+    lax.fori_loop(0, count // 32, last_pass, 0)
+    write(residual, result)
+    write(grad_value, grad_value_out)
+    write(grad_gate, grad_gate_out)
+    for n in range(steps):
+        for o in range(3):
+            copy_z(n, o).wait_send()
+        for copy in (copy_first(n), copy_second(n), copy_passed(n), copy_core(n)):
+            copy.wait_send()
+    for copy in halo_copies + [halo_two] + scan_copies:
+        copy.wait_send()
+    for copy in written:
+        copy.wait()
+
+
+def forward(near, parts, size):
+    count, width = near[0].shape
+    rows = parts[6].shape[0]
+    flat = lambda kind: jax.ShapeDtypeStruct((count, width), kind)
+    narrow = jax.ShapeDtypeStruct((count, 128), F32)
+    dma = pltpu.SemaphoreType.DMA
+    big, low = pltpu.VMEM((count, width), F32), pltpu.VMEM((count, width), BF)
+    lines = pltpu.VMEM((count, 128), F32)
+    steps = sum(p.shape[0] // 16 for p in parts)
+    eight = pltpu.VMEM((8, width), F32)
+    return pl.pallas_call(
+        forward_kernel,
+        out_shape=[jax.ShapeDtypeStruct((2, 2, 4, 2) + p.shape, p.dtype) for p in parts]
+        + [
+            flat(F32), jax.ShapeDtypeStruct((16, width), F32), jax.ShapeDtypeStruct((8, width), F32),
+            jax.ShapeDtypeStruct((5, count, width), BF), flat(BF), flat(BF), flat(BF),
+            jax.ShapeDtypeStruct((2, 2, 4, 2, rows, count), F32), flat(F32), flat(F32), narrow, flat(F32), flat(F32), narrow,
+        ]
+        + [flat(F32)] * 7,
+        in_specs=[whole()] * len(near) + [anywhere()] * len(parts),
+        out_specs=[anywhere()] * 28,
+        scratch_shapes=[
+            pltpu.VMEM((2, 2, 4, 2, 16, 128), BF), pltpu.VMEM((16, width), F32), eight,
+            pltpu.VMEM((5, 2, 2, 4, 2, width // 32, width), BF), pltpu.VMEM((2, 2, 4, 2, 16, 2 * width), BF),
+            pltpu.VMEM((2, 2, 2, 4, 2, 16, count), F32), pltpu.VMEM((5, count, width), BF), low, low, low, big,
+            big, lines, big, big, lines,
+        ]
+        + [big] * 12
+        + [
+            pltpu.VMEM((32, width), BF), pltpu.VMEM((32, width), F32), pltpu.VMEM((32, 128), F32), eight,
+            pltpu.VMEM((size, 8, width), F32), eight, eight, eight,
+            dma((steps, 7)), dma((steps, 7)), dma((7,)), dma((6,)), dma((24,)), dma((3,)), dma((size,)), dma((size,)),
+            dma((3,)), dma((3,)),
+        ],
+        compiler_params=pltpu.CompilerParams(collective_id=0, has_side_effects=True, vmem_limit_bytes=66_000_000),
+        cost_estimate=cost(6 * count * width * width + 4 * count * 32 * rows * width, 60_000_000),
+        name="forward",
+    )(*near, *parts)
+
+
 def channel_backward_kernel(
     feed_in, grad_value, grad_gate, vectors, keep, inverse, cotangent,
     weights, positive, w_feedr, w_output, spread, unit, keys, values, denom, mixed, prior_a, prior_b, recept,
-    feed_part, grad_keys, grad_values, grad_recept, grad_att, grad_residual, sums,
+    feed_part, rights, grad_residual, sums,
     weight_slots, positive_slots, feedr, output, spread_in, unit_in, keys_in, values_in, denom_in, mixed_in,
     prior_a_in, prior_b_in, recept_in, value_part, key_part, outgoing, gathered, from_first, from_second,
     grad_in, grad_rin, grad_z, grad_w, cum, up, low, summary, arrived, entering_rows, halo_out, halo_in,
@@ -801,7 +1012,7 @@
         xx, yy = owner(3 - lax.rem(s, 4), x, y, cc)
         return (
             pltpu.make_async_copy(weights.at[xx, cc, :, yy], weight_slots.at[slot], slot_sem.at[0, slot]),
-            pltpu.make_async_copy(positive.at[xx * 4 + cc * 2 + yy], positive_slots.at[slot], slot_sem.at[1, slot]),
+            pltpu.make_async_copy(positive.at[xx, cc, :, yy], positive_slots.at[slot], slot_sem.at[1, slot]),
         )
 
     for copy in fetches(0, 0):
@@ -815,6 +1026,8 @@
     for load in loads:
         load.start()
     links.greet(True)
+    grad_att, grad_keys, grad_values, grad_recept = [rights.at[n] for n in range(1, 5)]
+    rights[0] = grad_gate[...]
     grad_in[...] = jnp.zeros_like(grad_in)
     sums[...] = jnp.zeros_like(sums)
     summary[...] = jnp.zeros_like(summary)
@@ -839,14 +1052,14 @@
             for copy in fetches(s + 1, 1 - slot):
                 copy.start()
 
-        hidden = positive_slots[slot]
+        hidden = positive_slots[slot].reshape(4 * rows, feed_in.shape[0])
         squares = (hidden * hidden).astype(BF)
         key_rows = weight_slots[slot, :, :, :width].reshape(4 * rows, width)
         value_rows = weight_slots[slot, :, :, width:].reshape(4 * rows, width)
-        value_part[...] = matmul_lead(squares, grad_value[...])
-        grad_pre = (matmul_last(grad_value[...], value_rows) * (2.0 * hidden)).astype(BF)
-        key_part[...] = matmul_lead(grad_pre, feed_in[...])
-        grad_in[...] += matmul(grad_pre, key_rows)
+        value_part[...] = matmul(squares, grad_value[...])
+        grad_pre = (matmul_last(value_rows, grad_value[...]) * (2.0 * hidden)).astype(BF)
+        key_part[...] = matmul(grad_pre, feed_in[...])
+        grad_in[...] += matmul_lead(grad_pre, key_rows)
 
         @pl.when(s < 4)
         def _():
@@ -1019,19 +1232,19 @@
     tokens, width = feed_in.shape
     micro, length = near[4].shape[:2]
     rows = weights.shape[4]
-    flat_f32, flat_bf = (tokens, width), jax.ShapeDtypeStruct((tokens, width), BF)
+    flat_f32 = (tokens, width)
     dma = pltpu.SemaphoreType.DMA
     big = pltpu.VMEM(flat_f32, F32)
     return pl.pallas_call(
         channel_backward_kernel,
         out_shape=[
-            jax.ShapeDtypeStruct((2, 4, rows, width), BF), flat_bf, flat_bf, flat_bf, flat_bf,
+            jax.ShapeDtypeStruct((2, 4, rows, width), BF), jax.ShapeDtypeStruct((5, tokens, width), BF),
             jax.ShapeDtypeStruct(flat_f32, F32), jax.ShapeDtypeStruct((16, width), F32),
         ],
         in_specs=[whole()] * len(near) + [anywhere()] * len(far),
-        out_specs=[whole()] * 7,
+        out_specs=[whole()] * 4,
         scratch_shapes=[
-            pltpu.VMEM((2, 4, rows, 2 * width), BF), pltpu.VMEM((2, tokens, 4 * rows), F32),
+            pltpu.VMEM((2, 4, rows, 2 * width), BF), pltpu.VMEM((2, 4, rows, tokens), F32),
             pltpu.VMEM((width, width), BF), pltpu.VMEM((width, width), BF),
         ]
         + [big] * 9
@@ -1315,14 +1528,6 @@
     )(*near, *far)
 
 
-def along_row(block, distance):
-    return shifted(block, "tensor", distance)
-
-
-def with_prior(value, prior):
-    return jnp.concatenate([prior, value[:, :-1]], axis=1)
-
-
 def local_shards(tokens, resets, out_grads, *weights):
     (
         mixer_key, mixer_value, mixer_recept, mixer_output, feed_recept, feed_key, feed_value, *vector_shards
@@ -1331,76 +1536,34 @@
     dp, t = lax.axis_index("dp"), lax.axis_index("tensor")
     micro, _, length, width = tokens.shape
     count = micro * length
-    wide = lambda v: v.astype(F32)
-
     unit_rows = feed_key.shape[0] // 4
     feed_shard = jnp.concatenate(
         [lax.dynamic_slice_in_dim(w, dp * unit_rows, unit_rows, 0) for w in (feed_key, feed_value)], axis=1
     )
-    feed = lax.all_gather(feed_shard, BOTH, axis=0, tiled=True).reshape(2, 2, 4, 2, unit_rows, 2 * width)
     share = vector_shards[0].shape[0]
     vector_pack = jnp.pad(jnp.stack(vector_shards), ((0, 16 - len(vector_shards)), (0, 128 - share)))
-    token_block = tokens[:, 0]
-    last_token = along_row(token_block[:, -1:], 1)
-    packed, *squares = gather([vector_pack, mixer_key, mixer_value, mixer_recept, mixer_output, feed_recept])
-    w_key, w_value, w_recept, w_output, w_feedr = [w.reshape(width, width) for w in squares]
-    vectors = wide(packed.reshape(32, 16, 128)[:, : len(vector_shards), :share].transpose(1, 0, 2).reshape(-1, width))
+    keep = (1 - resets[:, 0]).astype(F32)[:, :, None]
+    keep_lanes = jnp.broadcast_to(keep, (micro, length, 128))
+    cotangent = out_grads.reshape(count, width)
+    near = [tokens.reshape(count, width), cotangent, keep_lanes]
+    parts = [vector_pack, mixer_key, mixer_value, mixer_recept, mixer_output, feed_recept, feed_shard]
     (
-        gain_one, bias_one, gain_two, bias_two, mix_key, mix_value, mix_recept, fading, premium, blend_key, blend_recept
-    ) = [vectors[i] for i in range(len(vector_shards))]
-    rates = jnp.exp(fading)
-    decay = jnp.exp(-rates)
-    scan_vectors = jnp.pad(jnp.stack([decay, premium]), ((0, 6), (0, 0)))
-
-    inputs = wide(token_block)
-    cotangent = wide(out_grads[:, 0])
-    keep = wide(1 - resets[:, 0])[:, :, None]
-    keep_lanes = jnp.broadcast_to(keep, (micro, length, 128))
-    normed_one, unit_one, inverse_one = norm_rows(inputs, gain_one, bias_one)
-    z_one = wide(normed_one.astype(BF))
-    prior_one = wide(norm_rows(wide(last_token), gain_one, bias_one)[0].astype(BF))
-    before_one = with_prior(z_one, prior_one) * keep
-    blend = lambda z, before, mix: (z * mix + before * (1.0 - mix)).astype(BF)
-    in_key, in_value, in_recept = [
-        blend(z_one, before_one, m).reshape(count, width) for m in (mix_key, mix_value, mix_recept)
+        _, all_key, all_value, all_recept, all_output, all_feedr, feed,
+        result, table, rates, lefts, feed_in, grad_value, grad_gate, positive, spread_one, unit_one, inverse_one,
+        spread_two, unit_two, inverse_two, keys, values, denom, mixed, prior_a, prior_b, recept,
+    ) = forward(near, parts, size)
+    w_key, w_value, w_recept, w_output, w_feedr = [
+        w.reshape(width, width) for w in (all_key, all_value, all_recept, all_output, all_feedr)
     ]
-    cube = (micro, length, width)
-    keys = matmul(in_key, w_key).reshape(cube)
-    values = matmul(in_value, w_value).reshape(cube)
-    gates = matmul(in_recept, w_recept).reshape(cube)
-    weighted, denom, mixed, prior_a, prior_b, recept = forward_scan(keys, values, gates, keep_lanes, scan_vectors, size)
-    weighted = weighted.reshape(count, width)
-    residual = inputs + matmul(weighted, w_output).reshape(cube)
-
-    normed_two, unit_two, inverse_two = norm_rows(residual, gain_two, bias_two)
-    low_two = normed_two.astype(BF)
-    z_two = wide(low_two)
-    before_two = with_prior(z_two, wide(along_row(low_two[:, -1:], 1))) * keep
-    feed_in = blend(z_two, before_two, blend_key).reshape(count, width)
-    feed_rin = blend(z_two, before_two, blend_recept).reshape(count, width)
-    gate = jax.nn.sigmoid(matmul(feed_rin, w_feedr)).reshape(cube)
-    positive, value_out = channel_forward(feed_in, feed)
-    value_out = value_out.reshape(cube)
-    result = residual + gate * value_out
-
-    grad_value = (cotangent * gate).astype(BF).reshape(count, width)
-    grad_gate = (cotangent * value_out * gate * (1.0 - gate)).astype(BF).reshape(count, width)
-    table = jnp.pad(vectors.at[DECAY].set(decay), ((0, 5), (0, 0)))
-    flat = lambda v: v.reshape(count, width)
-    over_lanes = lambda v: jnp.broadcast_to(v.reshape(count, 1), (count, 128))
-    near = [feed_in, grad_value, grad_gate, table, keep_lanes, over_lanes(inverse_two), flat(out_grads)]
-    far = [feed, positive, w_feedr, w_output, flat(z_two - before_two), flat(unit_two)]
-    far += [flat(v) for v in (keys, values, denom, mixed, prior_a, prior_b, recept)]
-    feed_part, grad_keys, grad_values, grad_recept, grad_att, grad_residual, sums = channel_backward(near, far, size)
-    lefts = jnp.stack([feed_rin, weighted, in_key, in_value, in_recept])
-    rights = jnp.stack([grad_gate, grad_att, grad_keys, grad_values, grad_recept])
-    near = [feed_part, lefts, rights, table, keep_lanes, over_lanes(inverse_one), grad_residual, sums]
-    near += [jnp.broadcast_to(rates, (8, width))]
-    far = [w_key, w_value, w_recept, flat(z_one - before_one), flat(unit_one)]
+    near = [feed_in, grad_value, grad_gate, table, keep_lanes, inverse_two, cotangent]
+    far = [feed, positive, w_feedr, w_output, spread_two, unit_two, keys, values, denom, mixed, prior_a, prior_b, recept]
+    feed_part, rights, grad_residual, sums = channel_backward(near, far, size)
+    near = [feed_part, lefts, rights, table, keep_lanes, inverse_one, grad_residual, sums, rates]
+    far = [w_key, w_value, w_recept, spread_one, unit_one]
     square_grads, unit_key, unit_value, token_grads, vector_grads = front_backward(near, far)
     mine = lax.dynamic_slice_in_dim(vector_grads, (dp * size + t) * share, share, 1)
     return (
-        result[:, None], token_grads.reshape(cube)[:, None],
+        result.reshape(tokens.shape), token_grads.reshape(tokens.shape),
         square_grads[2], square_grads[3], square_grads[4], square_grads[1], square_grads[0],
         unit_key.reshape(feed_key.shape), unit_value.reshape(feed_value.shape),
     ) + tuple(mine[i] for i in range(len(vector_shards)))

time: 409 us -> 417 us (1.020)
  Pallas kernels: 320 us -> 398 us
  local copies, waits for them, and re-layouts: 26.6 us -> 12.1 us
  other arithmetic: 15 us -> 0.83 us
  between operations: 14.5 us -> 0.89 us
  matrix products: 11.6 us -> 0 us
  starting transfers between devices: 10.3 us -> 0 us
  waiting for transfers between devices: 8.21 us -> 0 us
    pallas_call x3 -> x1, Pallas kernels: 117 us -> 190 us  [forward(): pl.pallas_call(forward_kernel, out_shape=[jax.ShapeDtypeStruct((2, 2, 4,...]
    dot_general x5 -> x0, matrix products: 11.6 us -> none  [matmul(): return jnp.dot(left, right, preferred_element_type=jnp.float32)]
    ppermute x2 -> x0, starting transfers between devices: 10.3 us -> none  [shifted(): return lax.ppermute(block, axis, route)]
    unnamed x55 -> x36, local copies, waits for them, and re-layouts: 15.5 us -> 5.71 us
    all_gather x1 -> x0, waiting for transfers between devices: 8.19 us -> none  [local_shards(): lax.all_gather(feed_shard, BOTH, axis=0, tiled=True)]
  transfers between devices with their start and end apart: 3 -> 0, of which waited for: 1 -> 0; matrix products, arithmetic and copies ran while one was open for 6% -> 0% of each run, Pallas kernels for 26% -> 0%
where the time goes in v3:
time: 417 us; the launch traced here: 411 us
  Pallas kernels  398 us (95%)
  local copies, waits for them, and re-layouts  12.1 us (3%)
    pallas_call x1, Pallas kernels, forward(): pl.pallas_call(forward_kernel, out_shape=[jax.ShapeDtypeStruct((2, 2, 4,...  190 us
    pallas_call x1, Pallas kernels, channel_backward(): pl.pallas_call(channel_backward_kernel, out_shape=[jax.ShapeDtypeStruct((...  115 us
    pallas_call x1, Pallas kernels, front_backward(): pl.pallas_call(front_backward_kernel, out_shape=[jax.ShapeDtypeStruct((co...  92.5 us

profile of v3, /device:TPU:0, one launch (start us, length us, event | category | flops | bytes accessed | tf_op | source)
XLA Modules:
  0.0 411.3 jit_solution(8643271607323222945)
XLA Ops:
  0.8 1.1 constant_dynamic-slice_fusion.1
  1.9 0.8 pad_maximum_fusion.own_feed
  2.8 0.8 broadcast_in_dim.2.keep
  3.5 0.0 copy-done.12
  3.5 0.0 copy-done.5
  3.5 0.0 copy-done.6
  3.5 0.0 copy-done.7
  3.6 0.0 copy-done.8
  3.6 0.0 copy-done.9
  3.6 0.0 copy-done.10
  3.6 0.0 copy-done.11
  3.6 0.1 stack.47
  3.7 0.6 pad.4.own_vectors
  4.3 189.9 %forward.1 = (bf16[2,2,4,2,16,128]{5,4,3,2,1,0:T(8,128)(2,1)}, bf16[2,2,4,2,32,1024]{5,4,3,2,1,0:T(8,128)(2,1)}, bf16[2,2,4,2,32,1024]{5,4,3,2,1,0:T(8,128)(2,1)...) custom-call(bf16[256,1024]{1,0:T(8,128)(2,1)} %bitcast.79, ...), custom_call_target="tpu_custom_call" | custom-call | flops 5905580032 | bytes 60000000 | tf_op jit(solution)/shard_map/forward/pallas_call | solution.py:963
  194.2 115.2 %channel_backward.1 = (bf16[2,4,128,1024]{3,2,1,0:T(8,128)(2,1)}, bf16[5,256,1024]{2,1,0:T(8,128)(2,1)}, f32[256,1024]{1,0:T(8,128)}, f32[16,1024]{1,0:T(8,128)}) custom-call(bf16[256,1024]{1,0:T(8,128)(2,1)} %get-tuple-element.57.feed_in, bf16[256,1024]{1,0:T(8,128)(2,1)} %get-tuple-element.58.grad_value, bf16[256,1024]{1,0:T(8,128)(2,1)} %get-tuple-element.59.grad_gate, ...), custom_call_target="tpu_custom_call" | custom-call | flops 8589934592 | bytes 67108864 | tf_op jit(solution)/shard_map/channel_backward/pallas_call | solution.py:1238
  309.3 92.5 %front_backward.1 = (f32[5,32,1024]{2,1,0:T(8,128)}, f32[4,128,1024]{2,1,0:T(8,128)}, f32[4,128,1024]{2,1,0:T(8,128)}, f32[256,1024]{1,0:T(8,128)}, f32[16,1024]{1,0:T(8,128)}) custom-call(bf16[2,4,128,1024]{3,2,1,0:T(8,128)(2,1)} %get-tuple-element.75.feed_part, bf16[5,256,1024]{2,1,0:T(8,128)(2,1)} %get-tuple-element.76.lefts, ...), custom_call_target="tpu_custom_call" | custom-call | flops 5368709120 | bytes 41943040 | tf_op jit(solution)/shard_map/front_backward/pallas_call | solution.py:1498
  401.8 2.1 slice_bitcast_fusion
  404.0 1.7 dynamic-slice_bitcast_fusion
  405.7 1.0 copy.47
  406.6 1.0 copy.48
  407.6 0.0 copy-done.1
  407.6 1.3 copy.49
  409.0 1.0 copy-done
  410.0 1.3 copy.50
  (23 shorter events, 0.0 us)
Async XLA Ops:
  0.7 2.1 copy-start.4
  0.7 2.8 copy-start.12
  0.7 2.8 copy-start.13
  0.7 2.8 copy-start.14
  0.7 2.8 copy-start.15
  0.7 2.8 copy-start.5
  0.7 2.8 copy-start.6
  0.7 2.8 copy-start.7
  0.7 2.8 copy-start.8
  0.8 2.8 copy-start.9
  0.8 2.8 copy-start.10
  0.8 2.8 copy-start.11
  401.8 3.8 copy-start.2
  401.8 4.8 %copy-start.3 = (f32[256,1024]{1,0:T(8,128)S(1)}, f32[256,1024]{1,0:T(8,128)}, u32[]{:S(2)}) copy-start(f32[256,1024]{1,0:T(8,128)} %get-tuple-element.87) | copy-start | bytes 3145732
  405.7 2.0 copy-start.1
  407.6 2.3 copy-start

commit v4 on v3

--- a/solution.py
+++ b/solution.py
@@ -579,7 +579,7 @@
     lax.fori_loop(0, right.shape[5] // tile, turn, 0)
 
 
-SKEW = 2
+AHEAD = 3
 
 
 def forward_kernel(
@@ -638,6 +638,10 @@
         half = outs[i].at[:, c, :, :, at]
         return remote(half, half, send.at[n, 6], recv.at[n, 6], links.core)
 
+    def step_z(n):
+        for o in range(3):
+            copy_z(n, o).start()
+
     def step_a(n):
         for o in range(3):
             copy_z(n, o).wait_recv()
@@ -655,12 +659,14 @@
 
     def advance(*numbers):
         for s in numbers:
+            if s + AHEAD < steps:
+                step_z(s + AHEAD)
             if s < steps:
                 step_a(s)
-            if 0 <= s - SKEW < steps:
-                step_b(s - SKEW)
-            if 0 <= s - 2 * SKEW < steps:
-                step_c(s - 2 * SKEW)
+            if 0 <= s - 1 < steps:
+                step_b(s - 1)
+            if 0 <= s - 2 < steps:
+                step_c(s - 2)
 
     def load(k):
         return pltpu.make_async_copy(outs[1 + k], squares.at[k], load_sem.at[k])
@@ -681,9 +687,6 @@
     for own in owns:
         own.start()
     links.greet(True)
-    for n in range(steps):
-        for o in range(3):
-            copy_z(n, o).start()
     halo_copies = [
         remote(
             tokens.at[pl.ds((m + 1) * length - piece, piece)], halo_tokens.at[pl.ds(m * piece, piece)],
@@ -693,16 +696,18 @@
     ]
     for halo in halo_copies:
         halo.start()
+    for n in range(AHEAD):
+        step_z(n)
     summary[...] = jnp.zeros_like(summary)
     halo_out[...] = jnp.zeros_like(halo_out)
     total[...] = jnp.zeros_like(total)
     for own in owns:
         own.wait()
-    advance(0, 1)
+    advance(0)
     norm_tiles(tokens, unit_one, inverse_one)
     write(unit_one, unit_one_out)
     write(inverse_one, inverse_one_out)
-    advance(2, 3, 4)
+    advance(1, 2)
     for halo in halo_copies:
         halo.wait_recv()
     norm_tiles(halo_tokens, halo_unit, halo_inverse)
@@ -710,7 +715,7 @@
 
     vector_load = pltpu.make_async_copy(all_vectors, packed, load_sem.at[5])
     vector_load.start()
-    advance(5)
+    advance(3)
     vector_load.wait()
     share = width // 32
     per = 128 // share
@@ -757,7 +762,7 @@
             return normed(halo_unit[last : last + 1, at], GAIN_ONE, BIAS_ONE, at)
 
         blends(spread_one, unit_one, m, prior, GAIN_ONE, BIAS_ONE, mixes)
-        advance(6 + m)
+        advance(4 + m)
     write(spread_one, spread_one_out)
     for k in range(3):
         write(left_parts.at[2 + k], lefts.at[2 + k])
@@ -769,12 +774,12 @@
         return finish
 
     ready(0)
-    advance(8)
+    advance(6)
     load(0).wait()
     dot_columns(keep_in(keys), left_parts.at[2], squares.at[0])
     write(keys, keys_out)
     ready(1)
-    advance(9, 10)
+    advance(7)
     load(1).wait()
     dot_columns(keep_in(values), left_parts.at[3], squares.at[1])
     write(values, values_out)
@@ -795,7 +800,7 @@
             return carry
 
         lax.fori_loop(0, width // 128, first_pass, 0)
-        advance(11 + m)
+        advance(8 + m)
     scan_copies = row_copies(summary, arrived, scan_send, scan_recv, t, dp, size)
     for copy in scan_copies:
         copy.start()
@@ -807,6 +812,7 @@
 
     dot_columns(finish_gate, left_parts.at[4], squares.at[2])
     write(gates, recept_out)
+    advance(10, 11)
     for copy in scan_copies:
         copy.wait_recv()
     for m in range(micro):
@@ -818,7 +824,6 @@
             b = jnp.where(t >= o, f * b + arrived[o, 3 * m + 2 : 3 * m + 3], b)
         entering_rows[2 * m : 2 * m + 1] = a
         entering_rows[2 * m + 1 : 2 * m + 2] = b
-    advance(13)
     for m in range(micro):
         rows_at = slice(m * length, (m + 1) * length)
 
@@ -846,7 +851,7 @@
     write(prior_a, prior_a_out)
     write(prior_b, prior_b_out)
     ready(3)
-    advance(14)
+    advance(12)
     load(3).wait()
 
     def finish_residual(at, value):
@@ -862,7 +867,7 @@
     halo_two = remote(halo_out, halo_in, halo_send.at[micro], halo_recv.at[micro], links.row(1))
     halo_two.start()
     ready(4)
-    advance(15)
+    advance(13)
     halo_two.wait_recv()
     mixes = [(feed_in, BLEND_KEY), (left_parts.at[0], BLEND_RECEPT)]
     for m in range(micro):
@@ -874,7 +879,7 @@
     write(spread_two, spread_two_out)
     write(feed_in, feed_in_out)
     write(left_parts.at[0], lefts.at[0])
-    advance(16)
+    advance(14)
     load(4).wait()
 
     def finish_second_gate(at, value):
@@ -882,21 +887,13 @@
 
     dot_columns(finish_second_gate, left_parts.at[0], squares.at[4])
 
-    def arrive(s, carry):
-        @pl.when(s + 2 * SKEW < feed_steps)
-        def _():
-            step_a(feed_base + s + 2 * SKEW)
-
-        @pl.when(s + SKEW < feed_steps)
-        def _():
-            step_b(feed_base + s + SKEW)
-
-        @pl.when(s < feed_steps)
-        def _():
-            step_c(feed_base + s)
-
-        k = s - SKEW
-        slot = lax.rem(s, 2)
+    advance(15)
+    later = {0: 16, 1: 17, 3: 18, 5: 19, 7: 20}
+
+    def arrive(k, carry):
+        for turn, number in later.items():
+            pl.when(k == turn)(functools.partial(advance, number))
+        slot = lax.rem(k, 2)
         at = pl.ds(pl.multiple_of(k * piece, piece), piece)
         copy_core(feed_base + k).wait_recv()
         fetch = pltpu.make_async_copy(outs[6].at[:, :, :, :, at], feed_slot, slot_sem.at[0])
@@ -925,7 +922,7 @@
 
         return carry
 
-    lax.fori_loop(SKEW, feed_steps + SKEW, arrive, 0)
+    lax.fori_loop(0, feed_steps, arrive, 0)
 
     def last_pass(k, carry):
         at = pl.ds(pl.multiple_of(k * 32, 32), 32)
@@ -969,7 +966,7 @@
             jax.ShapeDtypeStruct((2, 2, 4, 2, rows, count), F32), flat(F32), flat(F32), narrow, flat(F32), flat(F32), narrow,
         ]
         + [flat(F32)] * 7,
-        in_specs=[whole()] * len(near) + [anywhere()] * len(parts),
+        in_specs=[whole()] * (len(near) + len(parts)),
         out_specs=[anywhere()] * 28,
         scratch_shapes=[
             pltpu.VMEM((2, 2, 4, 2, 16, 128), BF), pltpu.VMEM((16, width), F32), eight,

time: 417 us -> 375 us (0.90)
  Pallas kernels: 398 us -> 357 us
    pallas_call x1, Pallas kernels: 190 us -> 146 us  [forward(): pl.pallas_call(forward_kernel, out_shape=[jax.ShapeDtypeStruct((2, 2, 4,...]
where the time goes in v4:
time: 375 us; the launch traced here: 370 us
  Pallas kernels  357 us (95%)
  local copies, waits for them, and re-layouts  12.1 us (3%)
    pallas_call x1, Pallas kernels, forward(): pl.pallas_call(forward_kernel, out_shape=[jax.ShapeDtypeStruct((2, 2, 4,...  146 us
    pallas_call x1, Pallas kernels, channel_backward(): pl.pallas_call(channel_backward_kernel, out_shape=[jax.ShapeDtypeStruct((...  118 us
    pallas_call x1, Pallas kernels, front_backward(): pl.pallas_call(front_backward_kernel, out_shape=[jax.ShapeDtypeStruct((co...  93 us

profile of v4, /device:TPU:0, one launch (start us, length us, event | category | flops | bytes accessed | tf_op | source)
XLA Modules:
  0.0 370.4 jit_solution(6488198344041819603)
XLA Ops:
  0.7 0.0 copy-start.4
  0.7 0.0 copy-start.12
  0.7 0.0 copy-start.13
  0.7 0.0 copy-start.14
  0.7 0.0 copy-start.15
  0.7 0.0 copy-start.5
  0.7 0.0 copy-start.6
  0.7 0.0 copy-start.7
  0.8 1.1 constant_dynamic-slice_fusion.1
  1.9 0.8 pad_maximum_fusion.own_feed
  2.8 0.8 broadcast_in_dim.2.keep
  3.6 0.1 stack.47
  3.7 0.6 pad.4.own_vectors
  4.3 145.8 %forward.1 = (bf16[2,2,4,2,16,128]{5,4,3,2,1,0:T(8,128)(2,1)}, bf16[2,2,4,2,32,1024]{5,4,3,2,1,0:T(8,128)(2,1)}, bf16[2,2,4,2,32,1024]{5,4,3,2,1,0:T(8,128)(2,1)...) custom-call(bf16[256,1024]{1,0:T(8,128)(2,1)} %bitcast.79, ...), custom_call_target="tpu_custom_call" | custom-call | flops 5905580032 | bytes 60000000 | tf_op jit(solution)/shard_map/forward/pallas_call | solution.py:960
  150.1 117.9 %channel_backward.1 = (bf16[2,4,128,1024]{3,2,1,0:T(8,128)(2,1)}, bf16[5,256,1024]{2,1,0:T(8,128)(2,1)}, f32[256,1024]{1,0:T(8,128)}, f32[16,1024]{1,0:T(8,128)}) custom-call(bf16[256,1024]{1,0:T(8,128)(2,1)} %get-tuple-element.57.feed_in, bf16[256,1024]{1,0:T(8,128)(2,1)} %get-tuple-element.58.grad_value, bf16[256,1024]{1,0:T(8,128)(2,1)} %get-tuple-element.59.grad_gate, ...), custom_call_target="tpu_custom_call" | custom-call | flops 8589934592 | bytes 67108864 | tf_op jit(solution)/shard_map/channel_backward/pallas_call | solution.py:1235
  268.0 93.0 %front_backward.1 = (f32[5,32,1024]{2,1,0:T(8,128)}, f32[4,128,1024]{2,1,0:T(8,128)}, f32[4,128,1024]{2,1,0:T(8,128)}, f32[256,1024]{1,0:T(8,128)}, f32[16,1024]{1,0:T(8,128)}) custom-call(bf16[2,4,128,1024]{3,2,1,0:T(8,128)(2,1)} %get-tuple-element.75.feed_part, bf16[5,256,1024]{2,1,0:T(8,128)(2,1)} %get-tuple-element.76.lefts, ...), custom_call_target="tpu_custom_call" | custom-call | flops 5368709120 | bytes 41943040 | tf_op jit(solution)/shard_map/front_backward/pallas_call | solution.py:1495
  360.9 2.1 slice_bitcast_fusion
  363.1 1.7 dynamic-slice_bitcast_fusion
  364.8 1.0 copy.47
  365.7 1.0 copy.48
  366.7 0.0 copy-done.1
  366.7 1.3 copy.49
  368.1 1.0 copy-done
  369.1 1.3 copy.50
  (23 shorter events, 0.0 us)
Async XLA Ops:
  0.7 2.1 copy-start.4
  0.7 2.8 copy-start.12
  0.7 2.8 copy-start.13
  0.7 2.8 copy-start.14
  0.7 2.8 copy-start.15
  0.7 2.8 copy-start.5
  0.7 2.8 copy-start.6
  0.7 2.8 copy-start.7
  0.7 2.8 copy-start.8
  0.8 2.8 copy-start.9
  0.8 2.8 copy-start.10
  0.8 2.8 copy-start.11
  360.9 3.8 %copy-start.2 = (f32[256,1024]{1,0:T(8,128)S(1)}, f32[256,1024]{1,0:T(8,128)}, u32[]{:S(2)}) copy-start(f32[256,1024]{1,0:T(8,128)} %get-tuple-element.56) | copy-start | bytes 3145732
  360.9 4.8 %copy-start.3 = (f32[256,1024]{1,0:T(8,128)S(1)}, f32[256,1024]{1,0:T(8,128)}, u32[]{:S(2)}) copy-start(f32[256,1024]{1,0:T(8,128)} %get-tuple-element.87) | copy-start | bytes 3145732
  364.8 2.0 copy-start.1
  366.7 2.3 copy-start

commit v5 on v4

--- a/solution.py
+++ b/solution.py
@@ -446,15 +446,6 @@
     ]
 
 
-def share_row(summary, arrived, send, recv, t, dp, size):
-    copies = row_copies(summary, arrived, send, recv, t, dp, size)
-    for copy in copies:
-        copy.start()
-    for copy in copies:
-        copy.wait_recv()
-    return copies
-
-
 def lanes(j):
     return pl.ds(pl.multiple_of(j * 128, 128), 128)
 
@@ -990,11 +981,11 @@
 def channel_backward_kernel(
     feed_in, grad_value, grad_gate, vectors, keep, inverse, cotangent,
     weights, positive, w_feedr, w_output, spread, unit, keys, values, denom, mixed, prior_a, prior_b, recept,
-    feed_part, rights, grad_residual, sums,
+    own_units, rights, grad_residual, sums,
     weight_slots, positive_slots, feedr, output, spread_in, unit_in, keys_in, values_in, denom_in, mixed_in,
-    prior_a_in, prior_b_in, recept_in, value_part, key_part, outgoing, gathered, from_first, from_second,
+    prior_a_in, prior_b_in, recept_in, value_part, key_part, outgoing, gathered, from_first, from_second, feed_part, feed_z,
     grad_in, grad_rin, grad_z, grad_w, cum, up, low, summary, arrived, entering_rows, halo_out, halo_in,
-    slot_sem, load_sem, core_send, core_recv, first_send, first_recv, second_send, second_recv,
+    slot_sem, load_sem, core_send, core_recv, first_send, first_recv, second_send, second_recv, feed_send, feed_recv,
     scan_send, scan_recv, halo_send, halo_recv,
 ):
     size = arrived.shape[0]
@@ -1003,10 +994,13 @@
     rows, width = weight_slots.shape[2], feed_in.shape[1]
     micro, length = keep.shape[:2]
 
+    def which(s):
+        return lax.rem(s // 2, 2), 3 - 2 * (s // 4) - lax.rem(s, 2)
+
     def fetches(s, slot):
-        own = s // 4
+        own, i = which(s)
         cc = own * c + (1 - own) * (1 - c)
-        xx, yy = owner(3 - lax.rem(s, 4), x, y, cc)
+        xx, yy = owner(i, x, y, cc)
         return (
             pltpu.make_async_copy(weights.at[xx, cc, :, yy], weight_slots.at[slot], slot_sem.at[0, slot]),
             pltpu.make_async_copy(positive.at[xx, cc, :, yy], positive_slots.at[slot], slot_sem.at[1, slot]),
@@ -1033,14 +1027,19 @@
     def to_core(i, slot):
         return remote(outgoing.at[slot], gathered.at[i], core_send.at[i], core_recv.at[i], links.core)
 
-    def to_first(q, side):
+    half = rows // 2
+
+    def piece(ref, u, *first):
+        return ref.at[(*first, u // 2, slice(None), slice((u % 2) * half, (u % 2 + 1) * half))]
+
+    def to_first(q, u):
         return remote(
-            gathered.at[2 + q, side], from_first.at[q, side], first_send.at[q, side], first_recv.at[q, side], links.first
+            piece(gathered, u, 2 + q), piece(from_first, u, q), first_send.at[q, u], first_recv.at[q, u], links.first
         )
 
     def column(s, carry):
         slot = lax.rem(s, 2)
-        i = 3 - lax.rem(s, 4)
+        own, i = which(s)
         for copy in fetches(s, slot):
             copy.wait()
 
@@ -1058,9 +1057,9 @@
         key_part[...] = matmul(grad_pre, feed_in[...])
         grad_in[...] += matmul_lead(grad_pre, key_rows)
 
-        @pl.when(s < 4)
+        @pl.when(own == 0)
         def _():
-            @pl.when(s >= 2)
+            @pl.when(s >= 4)
             def _():
                 to_core(i + 2, slot).wait_send()
 
@@ -1070,7 +1069,7 @@
                 outgoing[slot, 1, at] = key_part[k * rows : (k + 1) * rows].astype(BF)
             to_core(i, slot).start()
 
-        @pl.when(s >= 4)
+        @pl.when(own == 1)
         def _():
             to_core(i, slot).wait_recv()
             for side, part in ((0, value_part), (1, key_part)):
@@ -1079,10 +1078,12 @@
                     total = gathered[i, side, at].astype(F32) + part[k * rows : (k + 1) * rows]
                     gathered[i, side, at] = total.astype(BF)
 
-        @pl.when(jnp.logical_and(s >= 4, s < 6))
-        def _():
-            for side in (0, 1):
-                to_first(i - 2, side).start()
+        for turn, q in ((2, 1), (3, 0)):
+
+            @pl.when(s == turn)
+            def _(q=q):
+                to_first(q, 0).start()
+                to_first(q, 1).start()
 
         return carry
 
@@ -1090,15 +1091,43 @@
     to_core(1, 0).wait_send()
     to_core(0, 1).wait_send()
 
-    def to_second(side):
+    def to_second(u):
         return remote(
-            gathered.at[1, side], from_second.at[side], second_send.at[side], second_recv.at[side], links.second
-        )
-
-    def pass_second(side):
-        to_first(1, side).wait_recv()
-        add_blocks(gathered.at[1, side], [gathered.at[1, side], from_first.at[1, side]])
-        to_second(side).start()
+            piece(gathered, u, 1), piece(from_second, u), second_send.at[u], second_recv.at[u], links.second
+        )
+
+    def to_z(u, o):
+        at = slice((u % 2) * half, (u % 2 + 1) * half)
+        return remote(
+            feed_part.at[u // 2, o, at], feed_z.at[u // 2, o - 1, at], feed_send.at[u, o - 1], feed_recv.at[u, o - 1],
+            links.along_z[o - 1],
+        )
+
+    def pass_first(u):
+        to_first(1, u).start()
+        to_first(0, u).start()
+
+    def pass_second(u):
+        to_first(1, u).wait_recv()
+        add_blocks(piece(gathered, u, 1), [piece(gathered, u, 1), piece(from_first, u, 1)])
+        to_second(u).start()
+
+    def pass_z(u):
+        to_first(0, u).wait_recv()
+        to_second(u).wait_recv()
+        add_blocks(piece(feed_part, u), [piece(gathered, u, 0), piece(from_first, u, 0), piece(from_second, u)])
+        for o in (1, 2, 3):
+            to_z(u, o).start()
+
+    def finish(u):
+        for o in (1, 2, 3):
+            to_z(u, o).wait_recv()
+        for r in range((u % 2) * half, (u % 2 + 1) * half, 32):
+            at = slice(r, r + 32)
+            value = feed_part[u // 2, 0, at].astype(F32)
+            for o in range(3):
+                value = value + feed_z[u // 2, o, at].astype(F32)
+            own_units[u // 2, at] = value.astype(BF)
 
     row = lax.broadcasted_iota(jnp.int32, (length, 128), 0)
     loads[0].wait()
@@ -1116,6 +1145,8 @@
     halo = remote(halo_out, halo_in, halo_send.at[0], halo_recv.at[0], links.row(size - 1))
     halo.start()
     pass_second(0)
+    pass_first(2)
+    pass_second(1)
     loads[1].wait()
     halo.wait_recv()
     for m in range(micro):
@@ -1141,12 +1172,12 @@
         grad_residual, grad_z, unit_in, inverse, vectors[GAIN_TWO : GAIN_TWO + 1, :], cotangent, sums, GAIN_TWO
     )
     grad_att[...] = grad_residual[...].astype(BF)
-    pass_second(1)
 
     loads[3].wait()
     dot_rows(grad_w, grad_att, output)
     for load in loads[4:]:
         load.wait()
+    pass_z(0)
 
     def quotient_grads(rows_at, at):
         gate = recept_in[rows_at, at]
@@ -1173,7 +1204,14 @@
             return carry
 
         lax.fori_loop(0, width // 128, first_pass, 0)
-    copies = share_row(summary, arrived, scan_send, scan_recv, t, links.dp, size)
+    copies = row_copies(summary, arrived, scan_send, scan_recv, t, links.dp, size)
+    for copy in copies:
+        copy.start()
+    pass_first(3)
+    pass_second(2)
+    pass_z(1)
+    for copy in copies:
+        copy.wait_recv()
     for m in range(micro):
         a = jnp.zeros((1, width), F32)
         b = jnp.zeros((1, width), F32)
@@ -1207,17 +1245,21 @@
             return carry
 
         lax.fori_loop(0, width // 128, second_pass, 0)
-
-    for side in (0, 1):
-        to_first(0, side).wait_recv()
-        to_second(side).wait_recv()
-        add_blocks(
-            feed_part.at[side], [gathered.at[0, side], from_first.at[0, side], from_second.at[side]]
-        )
-    for side in (0, 1):
-        to_first(0, side).wait_send()
-        to_first(1, side).wait_send()
-        to_second(side).wait_send()
+        if m == 0:
+            pass_second(3)
+
+    pass_z(2)
+    finish(0)
+    finish(1)
+    pass_z(3)
+    finish(2)
+    finish(3)
+    for u in range(4):
+        to_first(0, u).wait_send()
+        to_first(1, u).wait_send()
+        to_second(u).wait_send()
+        for o in (1, 2, 3):
+            to_z(u, o).wait_send()
     halo.wait_send()
     for copy in copies:
         copy.wait_send()
@@ -1235,7 +1277,7 @@
     return pl.pallas_call(
         channel_backward_kernel,
         out_shape=[
-            jax.ShapeDtypeStruct((2, 4, rows, width), BF), jax.ShapeDtypeStruct((5, tokens, width), BF),
+            jax.ShapeDtypeStruct((2, rows, width), BF), jax.ShapeDtypeStruct((5, tokens, width), BF),
             jax.ShapeDtypeStruct(flat_f32, F32), jax.ShapeDtypeStruct((16, width), F32),
         ],
         in_specs=[whole()] * len(near) + [anywhere()] * len(far),
@@ -1249,12 +1291,14 @@
             pltpu.VMEM((4 * rows, width), F32), pltpu.VMEM((4 * rows, width), F32),
             pltpu.VMEM((2, 2, 4, rows, width), BF), pltpu.VMEM((4, 2, 4, rows, width), BF),
             pltpu.VMEM((2, 2, 4, rows, width), BF), pltpu.VMEM((2, 4, rows, width), BF),
+            pltpu.VMEM((2, 4, rows, width), BF), pltpu.VMEM((2, 3, rows, width), BF),
         ]
         + [big] * 7
         + [
             pltpu.VMEM((8, width), F32), pltpu.VMEM((size, 8, width), F32), pltpu.VMEM((8, width), F32),
             pltpu.VMEM((8, width), F32), pltpu.VMEM((8, width), F32),
-            dma((2, 2)), dma((11,)), dma((4,)), dma((4,)), dma((2, 2)), dma((2, 2)), dma((2,)), dma((2,)),
+            dma((2, 2)), dma((11,)), dma((4,)), dma((4,)), dma((2, 4)), dma((2, 4)), dma((4,)), dma((4,)),
+            dma((4, 3)), dma((4, 3)),
             dma((size,)), dma((size,)), dma((1,)), dma((1,)),
         ],
         compiler_params=pltpu.CompilerParams(
@@ -1266,13 +1310,13 @@
 
 
 def front_backward_kernel(
-    feed_part, lefts, rights, vectors, keep, inverse, grad_residual, sums_in, rates,
+    own_units, lefts, rights, vectors, keep, inverse, grad_residual, sums_in, rates,
     w_key, w_value, w_recept, spread, unit,
     square_grads, unit_key, unit_value, token_grads, vector_grads,
-    key_in, value_in, recept_in, spread_in, unit_in, outgoing, gathered, from_first, from_second, from_z, feed_z,
-    own_units, x_units, core_units, grad_key, grad_value, grad_recept, grad_z, sums, held, halo_out, halo_in,
+    key_in, value_in, recept_in, spread_in, unit_in, outgoing, gathered, from_first, from_second, from_z,
+    x_units, core_units, grad_key, grad_value, grad_recept, grad_z, sums, held, halo_out, halo_in,
     load_sem, core_send, core_recv, first_send, first_recv, second_send, second_recv, z_send, z_recv,
-    feed_send, feed_recv, unit_send, unit_recv, halo_send, halo_recv, sum_send, sum_recv,
+    unit_send, unit_recv, halo_send, halo_recv, sum_send, sum_recv,
 ):
     links = Links(8)
     x, c, z, y, t, size = links.x, links.c, links.z, links.y, links.t, links.size
@@ -1285,14 +1329,10 @@
     for load in loads:
         load.start()
     links.greet(True)
-    feed_copies = {}
-    for side in (0, 1):
-        for o in (1, 2, 3):
-            feed_copies[side, o] = remote(
-                feed_part.at[side, o], feed_z.at[side, o - 1], feed_send.at[side, o - 1], feed_recv.at[side, o - 1],
-                links.along_z[o - 1],
-            )
-            feed_copies[side, o].start()
+    units_over_x = remote(own_units, x_units, unit_send.at[0], unit_recv.at[0], links.over_x)
+    pl.when(c == 0)(units_over_x.start)
+    units_over_core = remote(own_units, core_units.at[0], unit_send.at[1], unit_recv.at[1], links.core)
+    units_over_core.start()
     halo_out[...] = jnp.zeros_like(halo_out)
     sums[...] = sums_in[...]
 
@@ -1327,7 +1367,6 @@
             for zz, yy, at in blocks():
                 outgoing[n, position(xx, yy, x, y, 1 - c), lax.rem(zz + 4 - z, 4)] = value[at].astype(BF)
         to_core(n).start()
-        return carry
 
     def own(n, carry):
         to_core(n).wait_recv()
@@ -1337,10 +1376,14 @@
                 i, o = position(xx, yy, x, y, c), lax.rem(zz + 4 - z, 4)
                 gathered[n, i, o] = (gathered[n, i, o].astype(F32) + value[at]).astype(BF)
         to_first(n).start()
+
+    def both(n, carry):
+        pl.when(n < count)(lambda: other(n, None))
+        pl.when(n >= 1)(lambda: own(n - 1, None))
         return carry
 
-    lax.fori_loop(0, count, other, 0)
-    lax.fori_loop(0, count, own, 0)
+    lax.fori_loop(0, count + 1, both, 0)
+    pl.when(c == 1)(units_over_x.start)
 
     def pass_second(n):
         to_first(n).wait_recv()
@@ -1359,20 +1402,6 @@
             to_z(n, o).wait_recv()
             value = value + from_z[n, o - 1].astype(F32)
         square_grads[n] = value
-
-    for side in (0, 1):
-        for o in (1, 2, 3):
-            feed_copies[side, o].wait_recv()
-        for r in range(0, feed_part.shape[2], 32):
-            at = slice(r, r + 32)
-            value = feed_part[side, 0, at].astype(F32)
-            for o in range(3):
-                value = value + feed_z[side, o, at].astype(F32)
-            own_units[side, at] = value.astype(BF)
-    units_over_x = remote(own_units, x_units, unit_send.at[0], unit_recv.at[0], links.over_x)
-    units_over_x.start()
-    units_over_core = remote(own_units, core_units.at[0], unit_send.at[1], unit_recv.at[1], links.core)
-    units_over_core.start()
 
     loads[0].wait()
     dot_rows(grad_key, rights.at[2], key_in)
@@ -1382,9 +1411,7 @@
     pass_second(1)
     loads[2].wait()
     dot_rows(grad_recept, rights.at[4], recept_in)
-    units_over_x.wait_recv()
     both_over_core = remote(x_units, core_units.at[1], unit_send.at[2], unit_recv.at[2], links.core)
-    both_over_core.start()
     grads = ((grad_key, MIX_KEY), (grad_value, MIX_VALUE), (grad_recept, MIX_RECEPT))
 
     def shift_one(rows_at, at, keeping):
@@ -1397,6 +1424,9 @@
     halo.start()
     pass_second(2)
     pass_z(0)
+    pass_second(3)
+    pass_z(1)
+    pass_second(4)
     loads[3].wait()
     halo.wait_recv()
     row = lax.broadcasted_iota(jnp.int32, (length, 128), 0)
@@ -1415,14 +1445,12 @@
             return carry
 
         lax.fori_loop(0, width // 128, shift_pass, 0)
-    pass_second(3)
-    pass_z(1)
+    pass_z(2)
     loads[4].wait()
     norm_back_tiles(
         token_grads, grad_z, unit_in, inverse, vectors[GAIN_ONE : GAIN_ONE + 1, :], grad_residual, sums, GAIN_ONE
     )
     sums[DECAY : DECAY + 1, :] = -sums[DECAY : DECAY + 1, :] * rates[0:1, :] * vectors[DECAY : DECAY + 1, :]
-    pass_second(4)
 
     stages = [[links.core], [links.over_x], [links.over_y], links.along_z]
     pending = []
@@ -1446,17 +1474,19 @@
 
     copies = begin(stages[0], sums, 0)
     pending += copies
-    pass_z(2)
+    pass_z(3)
+    finish(0)
     collect(copies, sums, 0, held.at[6])
     copies = begin(stages[1], held.at[6], 1)
     pending += copies
-    pass_z(3)
-    finish(0)
+    pass_z(4)
+    finish(1)
     collect(copies, held.at[6], 1, held.at[7])
     copies = begin(stages[2], held.at[7], 2)
     pending += copies
-    pass_z(4)
-    finish(1)
+    units_over_x.wait_recv()
+    both_over_core.start()
+    finish(2)
     collect(copies, held.at[7], 2, held.at[8])
     copies = begin(stages[3], held.at[8], 3)
     pending += copies
@@ -1470,9 +1500,8 @@
                 pick = jnp.where(links.dp == d ^ 2, x_units[side, at], pick)
                 pick = jnp.where(links.dp == d, own_units[side, at], pick)
                 target[d, at] = pick.astype(F32)
+    finish(3)
     collect(copies, held.at[8], 3, vector_grads)
-    finish(2)
-    finish(3)
     finish(4)
     for n in range(count):
         to_core(n).wait_send()
@@ -1480,13 +1509,13 @@
         to_second(n).wait_send()
         for o in (1, 2, 3):
             to_z(n, o).wait_send()
-    for copy in pending + list(feed_copies.values()) + [units_over_x, units_over_core, both_over_core, halo]:
+    for copy in pending + [units_over_x, units_over_core, both_over_core, halo]:
         copy.wait_send()
 
 
 def front_backward(near, far):
-    feed_part, lefts = near[:2]
-    rows = feed_part.shape[2]
+    own_units, lefts = near[:2]
+    rows = own_units.shape[1]
     count, tokens, width = lefts.shape
     own = width // 32
     dma = pltpu.SemaphoreType.DMA
@@ -1506,15 +1535,14 @@
         + [
             pltpu.VMEM((count, 4, 4, own, width), BF), pltpu.VMEM((count, 4, 4, own, width), BF),
             pltpu.VMEM((count, 2, 4, own, width), BF), pltpu.VMEM((count, 4, own, width), BF),
-            pltpu.VMEM((count, 3, own, width), BF), pltpu.VMEM((2, 3, rows, width), BF),
-            pltpu.VMEM((2, rows, width), BF), pltpu.VMEM((2, rows, width), BF), pltpu.VMEM((2, 2, rows, width), BF),
+            pltpu.VMEM((count, 3, own, width), BF), pltpu.VMEM((2, rows, width), BF), pltpu.VMEM((2, 2, rows, width), BF),
         ]
         + [big] * 4
         + [
             pltpu.VMEM((16, width), F32), pltpu.VMEM((9, 16, width), F32), pltpu.VMEM((8, width), F32),
             pltpu.VMEM((8, width), F32),
             dma((5,)), dma((count,)), dma((count,)), dma((count,)), dma((count,)), dma((count,)), dma((count,)),
-            dma((count, 3)), dma((count, 3)), dma((2, 3)), dma((2, 3)), dma((3,)), dma((3,)), dma((1,)), dma((1,)),
+            dma((count, 3)), dma((count, 3)), dma((3,)), dma((3,)), dma((1,)), dma((1,)),
             dma((6,)), dma((6,)),
         ],
         compiler_params=pltpu.CompilerParams(
@@ -1554,8 +1582,8 @@
     ]
     near = [feed_in, grad_value, grad_gate, table, keep_lanes, inverse_two, cotangent]
     far = [feed, positive, w_feedr, w_output, spread_two, unit_two, keys, values, denom, mixed, prior_a, prior_b, recept]
-    feed_part, rights, grad_residual, sums = channel_backward(near, far, size)
-    near = [feed_part, lefts, rights, table, keep_lanes, inverse_one, grad_residual, sums, rates]
+    own_units, rights, grad_residual, sums = channel_backward(near, far, size)
+    near = [own_units, lefts, rights, table, keep_lanes, inverse_one, grad_residual, sums, rates]
     far = [w_key, w_value, w_recept, spread_one, unit_one]
     square_grads, unit_key, unit_value, token_grads, vector_grads = front_backward(near, far)
     mine = lax.dynamic_slice_in_dim(vector_grads, (dp * size + t) * share, share, 1)

time: 375 us -> 347 us (0.925)
  Pallas kernels: 357 us -> 331 us
    pallas_call x1, Pallas kernels: 93 us -> 77.9 us  [front_backward(): pl.pallas_call(front_backward_kernel, out_shape=[jax.ShapeDtypeStruct((co...]
    pallas_call x1, Pallas kernels: 118 us -> 107 us  [channel_backward(): pl.pallas_call(channel_backward_kernel, out_shape=[jax.ShapeDtypeStruct((...]
where the time goes in v5:
time: 347 us; the launch traced here: 345 us
  Pallas kernels  331 us (95%)
  local copies, waits for them, and re-layouts  12 us (3%)
    pallas_call x1, Pallas kernels, forward(): pl.pallas_call(forward_kernel, out_shape=[jax.ShapeDtypeStruct((2, 2, 4,...  146 us
    pallas_call x1, Pallas kernels, channel_backward(): pl.pallas_call(channel_backward_kernel, out_shape=[jax.ShapeDtypeStruct((...  107 us
    pallas_call x1, Pallas kernels, front_backward(): pl.pallas_call(front_backward_kernel, out_shape=[jax.ShapeDtypeStruct((co...  77.9 us

profile of v5, /device:TPU:0, one launch (start us, length us, event | category | flops | bytes accessed | tf_op | source)
XLA Modules:
  0.0 344.6 jit_solution(1037073171836136020)
XLA Ops:
  0.7 0.0 copy-start.4
  0.7 0.0 copy-start.12
  0.7 0.0 copy-start.13
  0.7 0.0 copy-start.14
  0.7 0.0 copy-start.15
  0.7 0.0 copy-start.5
  0.7 0.0 copy-start.6
  0.7 0.0 copy-start.7
  0.8 1.1 constant_dynamic-slice_fusion.1
  1.9 0.8 pad_maximum_fusion.own_feed
  2.8 0.8 broadcast_in_dim.2.keep
  3.6 0.1 stack.47
  3.7 0.6 pad.4.own_vectors
  4.3 145.9 %forward.1 = (bf16[2,2,4,2,16,128]{5,4,3,2,1,0:T(8,128)(2,1)}, bf16[2,2,4,2,32,1024]{5,4,3,2,1,0:T(8,128)(2,1)}, bf16[2,2,4,2,32,1024]{5,4,3,2,1,0:T(8,128)(2,1)...) custom-call(bf16[256,1024]{1,0:T(8,128)(2,1)} %bitcast.79, ...), custom_call_target="tpu_custom_call" | custom-call | flops 5905580032 | bytes 60000000 | tf_op jit(solution)/shard_map/forward/pallas_call | solution.py:951
  150.1 107.1 %channel_backward.1 = (bf16[2,128,1024]{2,1,0:T(8,128)(2,1)}, bf16[5,256,1024]{2,1,0:T(8,128)(2,1)}, f32[256,1024]{1,0:T(8,128)}, f32[16,1024]{1,0:T(8,128)}) custom-call(bf16[256,1024]{1,0:T(8,128)(2,1)} %get-tuple-element.57.feed_in, bf16[256,1024]{1,0:T(8,128)(2,1)} %get-tuple-element.58.grad_value, bf16[256,1024]{1,0:T(8,128)(2,1)} %get-tuple-element.59.grad_gate, ...), custom_call_target="tpu_custom_call" | custom-call | flops 8589934592 | bytes 67108864 | tf_op jit(solution)/shard_map/channel_backward/pallas_call | solution.py:1277
  257.3 77.9 %front_backward.1 = (f32[5,32,1024]{2,1,0:T(8,128)}, f32[4,128,1024]{2,1,0:T(8,128)}, f32[4,128,1024]{2,1,0:T(8,128)}, f32[256,1024]{1,0:T(8,128)}, f32[16,1024]{1,0:T(8,128)}) custom-call(bf16[2,128,1024]{2,1,0:T(8,128)(2,1)} %get-tuple-element.75.own_units, bf16[5,256,1024]{2,1,0:T(8,128)(2,1)} %get-tuple-element.76.lefts, ...), custom_call_target="tpu_custom_call" | custom-call | flops 5368709120 | bytes 41943040 | tf_op jit(solution)/shard_map/front_backward/pallas_call | solution.py:1524
  335.2 2.1 slice_bitcast_fusion
  337.4 1.6 dynamic-slice_bitcast_fusion
  339.0 1.0 copy.47
  339.9 1.0 copy.48
  340.9 0.0 copy-done.1
  341.0 1.3 copy.49
  342.3 1.0 copy-done
  343.3 1.3 copy.50
  (23 shorter events, 0.0 us)
Async XLA Ops:
  0.7 2.1 copy-start.4
  0.7 2.8 copy-start.12
  0.7 2.8 copy-start.13
  0.7 2.8 copy-start.14
  0.7 2.8 copy-start.15
  0.7 2.8 copy-start.5
  0.7 2.8 copy-start.6
  0.7 2.8 copy-start.7
  0.7 2.8 copy-start.8
  0.8 2.8 copy-start.9
  0.8 2.8 copy-start.10
  0.8 2.8 copy-start.11
  335.2 3.8 %copy-start.2 = (f32[256,1024]{1,0:T(8,128)S(1)}, f32[256,1024]{1,0:T(8,128)}, u32[]{:S(2)}) copy-start(f32[256,1024]{1,0:T(8,128)} %get-tuple-element.56) | copy-start | bytes 3145732
  335.2 4.7 %copy-start.3 = (f32[256,1024]{1,0:T(8,128)S(1)}, f32[256,1024]{1,0:T(8,128)}, u32[]{:S(2)}) copy-start(f32[256,1024]{1,0:T(8,128)} %get-tuple-element.87) | copy-start | bytes 3145732
  339.0 2.0 copy-start.1
  341.0 2.3 copy-start

commit v6 on v5

--- a/solution.py
+++ b/solution.py
@@ -575,15 +575,16 @@
 
 def forward_kernel(
     tokens, cotangent, keep,
-    own_vectors, own_key, own_value, own_recept, own_output, own_feedr, own_feed,
+    own_vectors, own_key, own_value, own_recept, own_output, own_feedr,
+    feed_key, feed_value,
     all_vectors, all_key, all_value, all_recept, all_output, all_feedr, all_feed,
     result, table_out, rates_out, lefts, feed_in_out, grad_value_out, grad_gate_out, positive, spread_one_out,
     unit_one_out, inverse_one_out, spread_two_out, unit_two_out, inverse_two_out, keys_out, values_out, denom_out,
     mixed_out, prior_a_out, prior_b_out, recept_out,
-    packed, table, rates, squares, feed_slot, positive_slot, left_parts, feed_in, grad_value, grad_gate, spread_one,
+    own_feed, packed, table, rates, squares, feed_slot, positive_slot, left_parts, feed_in, grad_value, grad_gate, spread_one,
     unit_one, inverse_one, spread_two, unit_two, inverse_two, keys, values, gates, denom, mixed, prior_a, prior_b,
     cum, up, low, residual, total, halo_tokens, halo_unit, halo_inverse, summary, arrived, entering_rows, halo_out, halo_in,
-    send, recv, own_sem, load_sem, out_sem, slot_sem, scan_send, scan_recv, halo_send, halo_recv,
+    send, recv, own_sem, feed_sem, load_sem, out_sem, slot_sem, scan_send, scan_recv, halo_send, halo_recv,
 ):
     size = arrived.shape[0]
     links = Links(size)
@@ -675,8 +676,16 @@
         written.append(copy)
 
     owns = [pltpu.make_async_copy(ins[i], outs[i].at[x, c, z, y], own_sem.at[i]) for i in range(7)]
-    for own in owns:
+    for own in owns[:6]:
         own.start()
+    share_rows = own_feed.shape[0]
+    mine = pl.ds(pl.multiple_of(dp * share_rows, share_rows), share_rows)
+    feed_loads = [
+        pltpu.make_async_copy(feed_key.at[mine], own_feed.at[:, :width], feed_sem.at[0]),
+        pltpu.make_async_copy(feed_value.at[mine], own_feed.at[:, width:], feed_sem.at[1]),
+    ]
+    for copy in feed_loads:
+        copy.start()
     links.greet(True)
     halo_copies = [
         remote(
@@ -692,12 +701,15 @@
     summary[...] = jnp.zeros_like(summary)
     halo_out[...] = jnp.zeros_like(halo_out)
     total[...] = jnp.zeros_like(total)
-    for own in owns:
+    for own in owns[:6]:
         own.wait()
     advance(0)
     norm_tiles(tokens, unit_one, inverse_one)
     write(unit_one, unit_one_out)
     write(inverse_one, inverse_one_out)
+    for copy in feed_loads:
+        copy.wait()
+    owns[6].start()
     advance(1, 2)
     for halo in halo_copies:
         halo.wait_recv()
@@ -707,6 +719,7 @@
     vector_load = pltpu.make_async_copy(all_vectors, packed, load_sem.at[5])
     vector_load.start()
     advance(3)
+    owns[6].wait()
     vector_load.wait()
     share = width // 32
     per = 128 // share
@@ -803,7 +816,7 @@
 
     dot_columns(finish_gate, left_parts.at[4], squares.at[2])
     write(gates, recept_out)
-    advance(10, 11)
+    advance(10, 11, 12)
     for copy in scan_copies:
         copy.wait_recv()
     for m in range(micro):
@@ -842,7 +855,6 @@
     write(prior_a, prior_a_out)
     write(prior_b, prior_b_out)
     ready(3)
-    advance(12)
     load(3).wait()
 
     def finish_residual(at, value):
@@ -858,7 +870,7 @@
     halo_two = remote(halo_out, halo_in, halo_send.at[micro], halo_recv.at[micro], links.row(1))
     halo_two.start()
     ready(4)
-    advance(13)
+    advance(13, 14)
     halo_two.wait_recv()
     mixes = [(feed_in, BLEND_KEY), (left_parts.at[0], BLEND_RECEPT)]
     for m in range(micro):
@@ -870,7 +882,6 @@
     write(spread_two, spread_two_out)
     write(feed_in, feed_in_out)
     write(left_parts.at[0], lefts.at[0])
-    advance(14)
     load(4).wait()
 
     def finish_second_gate(at, value):
@@ -938,28 +949,30 @@
         copy.wait()
 
 
-def forward(near, parts, size):
+def forward(near, parts, far, size):
     count, width = near[0].shape
-    rows = parts[6].shape[0]
+    rows = far[0].shape[0] // 4
+    whole_parts = [(p.shape, p.dtype) for p in parts] + [((rows, 2 * width), BF)]
     flat = lambda kind: jax.ShapeDtypeStruct((count, width), kind)
     narrow = jax.ShapeDtypeStruct((count, 128), F32)
     dma = pltpu.SemaphoreType.DMA
     big, low = pltpu.VMEM((count, width), F32), pltpu.VMEM((count, width), BF)
     lines = pltpu.VMEM((count, 128), F32)
-    steps = sum(p.shape[0] // 16 for p in parts)
+    steps = sum(shape[0] // 16 for shape, _ in whole_parts)
     eight = pltpu.VMEM((8, width), F32)
     return pl.pallas_call(
         forward_kernel,
-        out_shape=[jax.ShapeDtypeStruct((2, 2, 4, 2) + p.shape, p.dtype) for p in parts]
+        out_shape=[jax.ShapeDtypeStruct((2, 2, 4, 2) + shape, kind) for shape, kind in whole_parts]
         + [
             flat(F32), jax.ShapeDtypeStruct((16, width), F32), jax.ShapeDtypeStruct((8, width), F32),
             jax.ShapeDtypeStruct((5, count, width), BF), flat(BF), flat(BF), flat(BF),
             jax.ShapeDtypeStruct((2, 2, 4, 2, rows, count), F32), flat(F32), flat(F32), narrow, flat(F32), flat(F32), narrow,
         ]
         + [flat(F32)] * 7,
-        in_specs=[whole()] * (len(near) + len(parts)),
+        in_specs=[whole()] * (len(near) + len(parts)) + [anywhere()] * 2,
         out_specs=[anywhere()] * 28,
         scratch_shapes=[
+            pltpu.VMEM((rows, 2 * width), BF),
             pltpu.VMEM((2, 2, 4, 2, 16, 128), BF), pltpu.VMEM((16, width), F32), eight,
             pltpu.VMEM((5, 2, 2, 4, 2, width // 32, width), BF), pltpu.VMEM((2, 2, 4, 2, 16, 2 * width), BF),
             pltpu.VMEM((2, 2, 2, 4, 2, 16, count), F32), pltpu.VMEM((5, count, width), BF), low, low, low, big,
@@ -969,13 +982,13 @@
         + [
             pltpu.VMEM((32, width), BF), pltpu.VMEM((32, width), F32), pltpu.VMEM((32, 128), F32), eight,
             pltpu.VMEM((size, 8, width), F32), eight, eight, eight,
-            dma((steps, 7)), dma((steps, 7)), dma((7,)), dma((6,)), dma((24,)), dma((3,)), dma((size,)), dma((size,)),
+            dma((steps, 7)), dma((steps, 7)), dma((7,)), dma((2,)), dma((6,)), dma((24,)), dma((3,)), dma((size,)), dma((size,)),
             dma((3,)), dma((3,)),
         ],
         compiler_params=pltpu.CompilerParams(collective_id=0, has_side_effects=True, vmem_limit_bytes=66_000_000),
         cost_estimate=cost(6 * count * width * width + 4 * count * 32 * rows * width, 60_000_000),
         name="forward",
-    )(*near, *parts)
+    )(*near, *parts, *far)
 
 
 def channel_backward_kernel(
@@ -995,7 +1008,7 @@
     micro, length = keep.shape[:2]
 
     def which(s):
-        return lax.rem(s // 2, 2), 3 - 2 * (s // 4) - lax.rem(s, 2)
+        return lax.rem(s, 2), 3 - s // 2
 
     def fetches(s, slot):
         own, i = which(s)
@@ -1027,15 +1040,53 @@
     def to_core(i, slot):
         return remote(outgoing.at[slot], gathered.at[i], core_send.at[i], core_recv.at[i], links.core)
 
-    half = rows // 2
+    spans = [(0, rows // 2), (rows // 2, rows)] * 2
 
     def piece(ref, u, *first):
-        return ref.at[(*first, u // 2, slice(None), slice((u % 2) * half, (u % 2 + 1) * half))]
+        return ref.at[(*first, u // 2, slice(None), slice(*spans[u]))]
 
     def to_first(q, u):
         return remote(
             piece(gathered, u, 2 + q), piece(from_first, u, q), first_send.at[q, u], first_recv.at[q, u], links.first
         )
+
+    def to_second(u):
+        return remote(
+            piece(gathered, u, 1), piece(from_second, u), second_send.at[u], second_recv.at[u], links.second
+        )
+
+    def to_z(u, o):
+        at = slice(*spans[u])
+        return remote(
+            feed_part.at[u // 2, o, at], feed_z.at[u // 2, o - 1, at], feed_send.at[u, o - 1], feed_recv.at[u, o - 1],
+            links.along_z[o - 1],
+        )
+
+    def pass_first(u):
+        to_first(1, u).start()
+        to_first(0, u).start()
+
+    def pass_second(u):
+        to_first(1, u).wait_recv()
+        add_blocks(piece(gathered, u, 1), [piece(gathered, u, 1), piece(from_first, u, 1)])
+        to_second(u).start()
+
+    def pass_z(u):
+        to_first(0, u).wait_recv()
+        to_second(u).wait_recv()
+        add_blocks(piece(feed_part, u), [piece(gathered, u, 0), piece(from_first, u, 0), piece(from_second, u)])
+        for o in (1, 2, 3):
+            to_z(u, o).start()
+
+    def finish(u):
+        for o in (1, 2, 3):
+            to_z(u, o).wait_recv()
+        for r in range(*spans[u], 32):
+            at = slice(r, r + 32)
+            value = feed_part[u // 2, 0, at].astype(F32)
+            for o in range(3):
+                value = value + feed_z[u // 2, o, at].astype(F32)
+            own_units[u // 2, at] = value.astype(BF)
 
     def column(s, carry):
         slot = lax.rem(s, 2)
@@ -1057,77 +1108,43 @@
         key_part[...] = matmul(grad_pre, feed_in[...])
         grad_in[...] += matmul_lead(grad_pre, key_rows)
 
+        turn_slot = lax.rem(s // 2, 2)
+
         @pl.when(own == 0)
         def _():
             @pl.when(s >= 4)
             def _():
-                to_core(i + 2, slot).wait_send()
+                to_core(i + 2, turn_slot).wait_send()
 
             for k in range(4):
                 at = lax.rem(k + 4 - z, 4)
-                outgoing[slot, 0, at] = value_part[k * rows : (k + 1) * rows].astype(BF)
-                outgoing[slot, 1, at] = key_part[k * rows : (k + 1) * rows].astype(BF)
-            to_core(i, slot).start()
+                outgoing[turn_slot, 0, at] = value_part[k * rows : (k + 1) * rows].astype(BF)
+                outgoing[turn_slot, 1, at] = key_part[k * rows : (k + 1) * rows].astype(BF)
+            to_core(i, turn_slot).start()
 
         @pl.when(own == 1)
         def _():
-            to_core(i, slot).wait_recv()
+            to_core(i, turn_slot).wait_recv()
             for side, part in ((0, value_part), (1, key_part)):
                 for k in range(4):
                     at = lax.rem(k + 4 - z, 4)
                     total = gathered[i, side, at].astype(F32) + part[k * rows : (k + 1) * rows]
                     gathered[i, side, at] = total.astype(BF)
 
-        for turn, q in ((2, 1), (3, 0)):
+        for turn, q in ((1, 1), (3, 0)):
 
             @pl.when(s == turn)
             def _(q=q):
                 to_first(q, 0).start()
                 to_first(q, 1).start()
 
+        pl.when(s == 5)(lambda: pass_second(0))
+        pl.when(s == 6)(lambda: pass_second(1))
         return carry
 
     lax.fori_loop(0, 8, column, 0)
     to_core(1, 0).wait_send()
     to_core(0, 1).wait_send()
-
-    def to_second(u):
-        return remote(
-            piece(gathered, u, 1), piece(from_second, u), second_send.at[u], second_recv.at[u], links.second
-        )
-
-    def to_z(u, o):
-        at = slice((u % 2) * half, (u % 2 + 1) * half)
-        return remote(
-            feed_part.at[u // 2, o, at], feed_z.at[u // 2, o - 1, at], feed_send.at[u, o - 1], feed_recv.at[u, o - 1],
-            links.along_z[o - 1],
-        )
-
-    def pass_first(u):
-        to_first(1, u).start()
-        to_first(0, u).start()
-
-    def pass_second(u):
-        to_first(1, u).wait_recv()
-        add_blocks(piece(gathered, u, 1), [piece(gathered, u, 1), piece(from_first, u, 1)])
-        to_second(u).start()
-
-    def pass_z(u):
-        to_first(0, u).wait_recv()
-        to_second(u).wait_recv()
-        add_blocks(piece(feed_part, u), [piece(gathered, u, 0), piece(from_first, u, 0), piece(from_second, u)])
-        for o in (1, 2, 3):
-            to_z(u, o).start()
-
-    def finish(u):
-        for o in (1, 2, 3):
-            to_z(u, o).wait_recv()
-        for r in range((u % 2) * half, (u % 2 + 1) * half, 32):
-            at = slice(r, r + 32)
-            value = feed_part[u // 2, 0, at].astype(F32)
-            for o in range(3):
-                value = value + feed_z[u // 2, o, at].astype(F32)
-            own_units[u // 2, at] = value.astype(BF)
 
     row = lax.broadcasted_iota(jnp.int32, (length, 128), 0)
     loads[0].wait()
@@ -1144,10 +1161,9 @@
         halo_out[m : m + 1] = shift_two(m, slice(start, start + 1), slice(None), keep[m, 0:1, 0:1])
     halo = remote(halo_out, halo_in, halo_send.at[0], halo_recv.at[0], links.row(size - 1))
     halo.start()
-    pass_second(0)
     pass_first(2)
-    pass_second(1)
     loads[1].wait()
+    pass_z(0)
     halo.wait_recv()
     for m in range(micro):
         rows_at = slice(m * length, (m + 1) * length)
@@ -1177,7 +1193,7 @@
     dot_rows(grad_w, grad_att, output)
     for load in loads[4:]:
         load.wait()
-    pass_z(0)
+    pass_z(1)
 
     def quotient_grads(rows_at, at):
         gate = recept_in[rows_at, at]
@@ -1209,7 +1225,7 @@
         copy.start()
     pass_first(3)
     pass_second(2)
-    pass_z(1)
+    pass_second(3)
     for copy in copies:
         copy.wait_recv()
     for m in range(micro):
@@ -1246,9 +1262,8 @@
 
         lax.fori_loop(0, width // 128, second_pass, 0)
         if m == 0:
-            pass_second(3)
-
-    pass_z(2)
+            pass_z(2)
+
     finish(0)
     finish(1)
     pass_z(3)
@@ -1277,7 +1292,8 @@
     return pl.pallas_call(
         channel_backward_kernel,
         out_shape=[
-            jax.ShapeDtypeStruct((2, rows, width), BF), jax.ShapeDtypeStruct((5, tokens, width), BF),
+            jax.ShapeDtypeStruct((2, rows, width), BF),
+            jax.ShapeDtypeStruct((5, tokens, width), BF),
             jax.ShapeDtypeStruct(flat_f32, F32), jax.ShapeDtypeStruct((16, width), F32),
         ],
         in_specs=[whole()] * len(near) + [anywhere()] * len(far),
@@ -1310,13 +1326,13 @@
 
 
 def front_backward_kernel(
-    own_units, lefts, rights, vectors, keep, inverse, grad_residual, sums_in, rates,
-    w_key, w_value, w_recept, spread, unit,
-    square_grads, unit_key, unit_value, token_grads, vector_grads,
-    key_in, value_in, recept_in, spread_in, unit_in, outgoing, gathered, from_first, from_second, from_z,
-    x_units, core_units, grad_key, grad_value, grad_recept, grad_z, sums, held, halo_out, halo_in,
+    own_units, vectors, keep, inverse, sums_in, rates,
+    lefts_far, rights_far, grad_residual_far, w_key, w_value, w_recept, spread, unit,
+    square_grads, units, token_grads, vector_grads,
+    lefts, rights, grad_residual, key_in, value_in, recept_in, spread_in, unit_in, outgoing, gathered, from_first, from_second, from_z,
+    grad_key, grad_value, grad_recept, grad_z, sums, held, halo_out, halo_in,
     load_sem, core_send, core_recv, first_send, first_recv, second_send, second_recv, z_send, z_recv,
-    unit_send, unit_recv, halo_send, halo_recv, sum_send, sum_recv,
+    unit_send, unit_recv, halo_send, halo_recv, sum_send, sum_recv, keep_sem, pair_sem,
 ):
     links = Links(8)
     x, c, z, y, t, size = links.x, links.c, links.z, links.y, links.t, links.size
@@ -1325,13 +1341,28 @@
     rows = width // 32
     micro, length = keep.shape[:2]
     late = [(w_key, key_in), (w_value, value_in), (w_recept, recept_in), (spread, spread_in), (unit, unit_in)]
+    late += [(grad_residual_far, grad_residual)]
     loads = [pltpu.make_async_copy(source, target, load_sem.at[k]) for k, (source, target) in enumerate(late)]
+
+    def pair(n):
+        return (
+            pltpu.make_async_copy(lefts_far.at[n], lefts.at[n], pair_sem.at[0, n]),
+            pltpu.make_async_copy(rights_far.at[n], rights.at[n], pair_sem.at[1, n]),
+        )
+
+    for n in range(count):
+        for copy in pair(n):
+            copy.start()
     for load in loads:
         load.start()
     links.greet(True)
-    units_over_x = remote(own_units, x_units, unit_send.at[0], unit_recv.at[0], links.over_x)
+    dp = links.dp
+    over = (1 - x) * 2 + c
+    kept = pltpu.make_async_copy(own_units, units.at[dp], keep_sem.at[0])
+    kept.start()
+    units_over_x = remote(own_units, units.at[dp], unit_send.at[0], unit_recv.at[0], links.over_x)
     pl.when(c == 0)(units_over_x.start)
-    units_over_core = remote(own_units, core_units.at[0], unit_send.at[1], unit_recv.at[1], links.core)
+    units_over_core = remote(own_units, units.at[dp], unit_send.at[1], unit_recv.at[1], links.core)
     units_over_core.start()
     halo_out[...] = jnp.zeros_like(halo_out)
     sums[...] = sums_in[...]
@@ -1362,6 +1393,8 @@
         )
 
     def other(n, carry):
+        for copy in pair(n):
+            copy.wait()
         for xx in range(2):
             value = part(n, 1 - c, xx)
             for zz, yy, at in blocks():
@@ -1411,7 +1444,7 @@
     pass_second(1)
     loads[2].wait()
     dot_rows(grad_recept, rights.at[4], recept_in)
-    both_over_core = remote(x_units, core_units.at[1], unit_send.at[2], unit_recv.at[2], links.core)
+    last_over_core = remote(units.at[over], units.at[over], unit_send.at[2], unit_recv.at[2], links.core)
     grads = ((grad_key, MIX_KEY), (grad_value, MIX_VALUE), (grad_recept, MIX_RECEPT))
 
     def shift_one(rows_at, at, keeping):
@@ -1447,6 +1480,7 @@
         lax.fori_loop(0, width // 128, shift_pass, 0)
     pass_z(2)
     loads[4].wait()
+    loads[5].wait()
     norm_back_tiles(
         token_grads, grad_z, unit_in, inverse, vectors[GAIN_ONE : GAIN_ONE + 1, :], grad_residual, sums, GAIN_ONE
     )
@@ -1485,36 +1519,29 @@
     copies = begin(stages[2], held.at[7], 2)
     pending += copies
     units_over_x.wait_recv()
-    both_over_core.start()
+    last_over_core.start()
     finish(2)
     collect(copies, held.at[7], 2, held.at[8])
     copies = begin(stages[3], held.at[8], 3)
     pending += copies
-    units_over_core.wait_recv()
-    both_over_core.wait_recv()
-    for side, target in ((1, unit_key), (0, unit_value)):
-        for d in range(4):
-            for r in range(0, own_units.shape[1], 32):
-                at = slice(r, r + 32)
-                pick = jnp.where(links.dp == d ^ 1, core_units[0, side, at], core_units[1, side, at])
-                pick = jnp.where(links.dp == d ^ 2, x_units[side, at], pick)
-                pick = jnp.where(links.dp == d, own_units[side, at], pick)
-                target[d, at] = pick.astype(F32)
     finish(3)
     collect(copies, held.at[8], 3, vector_grads)
     finish(4)
+    for copy in (units_over_core, last_over_core):
+        copy.wait_recv()
+    kept.wait()
     for n in range(count):
         to_core(n).wait_send()
         to_first(n).wait_send()
         to_second(n).wait_send()
         for o in (1, 2, 3):
             to_z(n, o).wait_send()
-    for copy in pending + [units_over_x, units_over_core, both_over_core, halo]:
+    for copy in pending + [units_over_x, units_over_core, last_over_core, halo]:
         copy.wait_send()
 
 
 def front_backward(near, far):
-    own_units, lefts = near[:2]
+    own_units, lefts = near[0], far[0]
     rows = own_units.shape[1]
     count, tokens, width = lefts.shape
     own = width // 32
@@ -1525,25 +1552,26 @@
         front_backward_kernel,
         out_shape=[
             jax.ShapeDtypeStruct((count, own, width), F32),
-            jax.ShapeDtypeStruct((4, rows, width), F32), jax.ShapeDtypeStruct((4, rows, width), F32),
+            jax.ShapeDtypeStruct((4, 2, rows, width), BF),
             jax.ShapeDtypeStruct((tokens, width), F32), jax.ShapeDtypeStruct((16, width), F32),
         ],
         in_specs=[whole()] * len(near) + [anywhere()] * len(far),
-        out_specs=[whole()] * 5,
-        scratch_shapes=[square] * 3
+        out_specs=[whole(), anywhere(), whole(), whole()],
+        scratch_shapes=[pltpu.VMEM(lefts.shape, BF), pltpu.VMEM(lefts.shape, BF), big]
+        + [square] * 3
         + [big] * 2
         + [
             pltpu.VMEM((count, 4, 4, own, width), BF), pltpu.VMEM((count, 4, 4, own, width), BF),
             pltpu.VMEM((count, 2, 4, own, width), BF), pltpu.VMEM((count, 4, own, width), BF),
-            pltpu.VMEM((count, 3, own, width), BF), pltpu.VMEM((2, rows, width), BF), pltpu.VMEM((2, 2, rows, width), BF),
+            pltpu.VMEM((count, 3, own, width), BF),
         ]
         + [big] * 4
         + [
             pltpu.VMEM((16, width), F32), pltpu.VMEM((9, 16, width), F32), pltpu.VMEM((8, width), F32),
             pltpu.VMEM((8, width), F32),
-            dma((5,)), dma((count,)), dma((count,)), dma((count,)), dma((count,)), dma((count,)), dma((count,)),
+            dma((6,)), dma((count,)), dma((count,)), dma((count,)), dma((count,)), dma((count,)), dma((count,)),
             dma((count, 3)), dma((count, 3)), dma((3,)), dma((3,)), dma((1,)), dma((1,)),
-            dma((6,)), dma((6,)),
+            dma((6,)), dma((6,)), dma((1,)), dma((2, count)),
         ],
         compiler_params=pltpu.CompilerParams(
             collective_id=3, has_side_effects=True, vmem_limit_bytes=66_000_000
@@ -1561,36 +1589,32 @@
     dp, t = lax.axis_index("dp"), lax.axis_index("tensor")
     micro, _, length, width = tokens.shape
     count = micro * length
-    unit_rows = feed_key.shape[0] // 4
-    feed_shard = jnp.concatenate(
-        [lax.dynamic_slice_in_dim(w, dp * unit_rows, unit_rows, 0) for w in (feed_key, feed_value)], axis=1
-    )
     share = vector_shards[0].shape[0]
     vector_pack = jnp.pad(jnp.stack(vector_shards), ((0, 16 - len(vector_shards)), (0, 128 - share)))
     keep = (1 - resets[:, 0]).astype(F32)[:, :, None]
     keep_lanes = jnp.broadcast_to(keep, (micro, length, 128))
     cotangent = out_grads.reshape(count, width)
     near = [tokens.reshape(count, width), cotangent, keep_lanes]
-    parts = [vector_pack, mixer_key, mixer_value, mixer_recept, mixer_output, feed_recept, feed_shard]
+    parts = [vector_pack, mixer_key, mixer_value, mixer_recept, mixer_output, feed_recept]
     (
         _, all_key, all_value, all_recept, all_output, all_feedr, feed,
         result, table, rates, lefts, feed_in, grad_value, grad_gate, positive, spread_one, unit_one, inverse_one,
         spread_two, unit_two, inverse_two, keys, values, denom, mixed, prior_a, prior_b, recept,
-    ) = forward(near, parts, size)
+    ) = forward(near, parts, [feed_key, feed_value], size)
     w_key, w_value, w_recept, w_output, w_feedr = [
         w.reshape(width, width) for w in (all_key, all_value, all_recept, all_output, all_feedr)
     ]
     near = [feed_in, grad_value, grad_gate, table, keep_lanes, inverse_two, cotangent]
     far = [feed, positive, w_feedr, w_output, spread_two, unit_two, keys, values, denom, mixed, prior_a, prior_b, recept]
     own_units, rights, grad_residual, sums = channel_backward(near, far, size)
-    near = [own_units, lefts, rights, table, keep_lanes, inverse_one, grad_residual, sums, rates]
-    far = [w_key, w_value, w_recept, spread_one, unit_one]
-    square_grads, unit_key, unit_value, token_grads, vector_grads = front_backward(near, far)
+    near = [own_units, table, keep_lanes, inverse_one, sums, rates]
+    far = [lefts, rights, grad_residual, w_key, w_value, w_recept, spread_one, unit_one]
+    square_grads, units, token_grads, vector_grads = front_backward(near, far)
     mine = lax.dynamic_slice_in_dim(vector_grads, (dp * size + t) * share, share, 1)
     return (
         result.reshape(tokens.shape), token_grads.reshape(tokens.shape),
         square_grads[2], square_grads[3], square_grads[4], square_grads[1], square_grads[0],
-        unit_key.reshape(feed_key.shape), unit_value.reshape(feed_value.shape),
+        units[:, 1].reshape(feed_key.shape).astype(F32), units[:, 0].reshape(feed_value.shape).astype(F32),
     ) + tuple(mine[i] for i in range(len(vector_shards)))
 
 

time: 347 us -> 340 us (0.980)
  Pallas kernels: 331 us -> 324 us
    pallas_call x1, Pallas kernels: 107 us -> 98.8 us  [channel_backward(): pl.pallas_call(channel_backward_kernel, out_shape=[jax.ShapeDtypeStruct((...]
    unnamed x36 -> x8, local copies, waits for them, and re-layouts: 5.71 us -> 1.95 us
where the time goes in v6:
time: 340 us; the launch traced here: 337 us
  Pallas kernels  324 us (95%)
  local copies, waits for them, and re-layouts  8.97 us (3%)
    pallas_call x1, Pallas kernels, forward(): pl.pallas_call(forward_kernel, out_shape=[jax.ShapeDtypeStruct((2, 2, 4,...  149 us
    pallas_call x1, Pallas kernels, channel_backward(): pl.pallas_call(channel_backward_kernel, out_shape=[jax.ShapeDtypeStruct((...  98.8 us
    pallas_call x1, Pallas kernels, front_backward(): pl.pallas_call(front_backward_kernel, out_shape=[jax.ShapeDtypeStruct((co...  76.7 us

profile of v6, /device:TPU:0, one launch (start us, length us, event | category | flops | bytes accessed | tf_op | source)
XLA Modules:
  0.0 337.1 jit_solution(15336132095035291758)
XLA Ops:
  0.7 0.7 subtract_convert_fusion
  1.3 0.8 broadcast_in_dim.2.keep
  2.1 1.5 stack.47
  3.6 0.6 pad.4.own_vectors
  4.2 148.6 %forward.1 = (bf16[2,2,4,2,16,128]{5,4,3,2,1,0:T(8,128)(2,1)}, bf16[2,2,4,2,32,1024]{5,4,3,2,1,0:T(8,128)(2,1)}, bf16[2,2,4,2,32,1024]{5,4,3,2,1,0:T(8,128)(2,1)...) custom-call(bf16[256,1024]{1,0:T(8,128)(2,1)} %bitcast.81, ...), custom_call_target="tpu_custom_call" | custom-call | flops 5905580032 | bytes 60000000 | tf_op jit(solution)/shard_map/forward/pallas_call | solution.py:963
  152.8 98.8 %channel_backward.1 = (bf16[2,128,1024]{2,1,0:T(8,128)(2,1)}, bf16[5,256,1024]{2,1,0:T(8,128)(2,1)}, f32[256,1024]{1,0:T(8,128)}, f32[16,1024]{1,0:T(8,128)}) custom-call(bf16[256,1024]{1,0:T(8,128)(2,1)} %get-tuple-element.56.feed_in, bf16[256,1024]{1,0:T(8,128)(2,1)} %get-tuple-element.57.grad_value, bf16[256,1024]{1,0:T(8,128)(2,1)} %get-tuple-element.58.grad_gate, ...), custom_call_target="tpu_custom_call" | custom-call | flops 8589934592 | bytes 67108864 | tf_op jit(solution)/shard_map/channel_backward/pallas_call | solution.py:1292
  251.6 76.7 %front_backward.1 = (f32[5,32,1024]{2,1,0:T(8,128)}, bf16[4,2,128,1024]{3,2,1,0:T(8,128)(2,1)}, f32[256,1024]{1,0:T(8,128)}, f32[16,1024]{1,0:T(8,128)}) custom-call(bf16[2,128,1024]{2,1,0:T(8,128)(2,1)} %get-tuple-element.74.own_units, f32[16,1024]{1,0:T(8,128)} %get-tuple-element.59.vectors, f32[2,128,128]{2,1,0:T(8,128)} %broadcast_in_dim.2.keep, ...), custom_call_target="tpu_custom_call" | custom-call | flops 5368709120 | bytes 41943040 | tf_op jit(solution)/shard_map/front_backward/pallas_call | solution.py:1551
  328.4 1.7 fusion
  330.1 0.0 copy-start.2
  330.1 2.6 bitcast_convert_fusion
  332.7 0.0 copy-start
  332.7 0.0 copy-start.1
  332.7 0.0 copy-done.2
  332.8 0.8 slice_bitcast_fusion
  333.6 1.6 dynamic-slice_bitcast_fusion
  335.2 0.0 copy-done
  335.2 1.0 copy.45
  336.2 0.0 copy-done.1
  336.2 1.0 copy.46
Async XLA Ops:
  330.1 2.6 copy-start.2
  332.7 2.4 copy-start
  332.7 3.4 %copy-start.1 = (f32[256,1024]{1,0:T(8,128)S(1)}, f32[256,1024]{1,0:T(8,128)}, u32[]{:S(2)}) copy-start(f32[256,1024]{1,0:T(8,128)} %get-tuple-element.86) | copy-start | bytes 3145732

commit v7 on v6

--- a/solution.py
+++ b/solution.py
@@ -994,12 +994,13 @@
 def channel_backward_kernel(
     feed_in, grad_value, grad_gate, vectors, keep, inverse, cotangent,
     weights, positive, w_feedr, w_output, spread, unit, keys, values, denom, mixed, prior_a, prior_b, recept,
-    own_units, rights, grad_residual, sums,
+    own_units, sums, rights_far, grad_residual_far,
+    rights, grad_residual,
     weight_slots, positive_slots, feedr, output, spread_in, unit_in, keys_in, values_in, denom_in, mixed_in,
     prior_a_in, prior_b_in, recept_in, value_part, key_part, outgoing, gathered, from_first, from_second, feed_part, feed_z,
     grad_in, grad_rin, grad_z, grad_w, cum, up, low, summary, arrived, entering_rows, halo_out, halo_in,
     slot_sem, load_sem, core_send, core_recv, first_send, first_recv, second_send, second_recv, feed_send, feed_recv,
-    scan_send, scan_recv, halo_send, halo_recv,
+    scan_send, scan_recv, halo_send, halo_recv, out_sem,
 ):
     size = arrived.shape[0]
     links = Links(size)
@@ -1032,6 +1033,9 @@
     links.greet(True)
     grad_att, grad_keys, grad_values, grad_recept = [rights.at[n] for n in range(1, 5)]
     rights[0] = grad_gate[...]
+    puts = [pltpu.make_async_copy(rights.at[n], rights_far.at[n], out_sem.at[n]) for n in range(5)]
+    puts.append(pltpu.make_async_copy(grad_residual, grad_residual_far, out_sem.at[5]))
+    puts[0].start()
     grad_in[...] = jnp.zeros_like(grad_in)
     sums[...] = jnp.zeros_like(sums)
     summary[...] = jnp.zeros_like(summary)
@@ -1188,6 +1192,8 @@
         grad_residual, grad_z, unit_in, inverse, vectors[GAIN_TWO : GAIN_TWO + 1, :], cotangent, sums, GAIN_TWO
     )
     grad_att[...] = grad_residual[...].astype(BF)
+    puts[1].start()
+    puts[5].start()
 
     loads[3].wait()
     dot_rows(grad_w, grad_att, output)
@@ -1263,6 +1269,8 @@
         lax.fori_loop(0, width // 128, second_pass, 0)
         if m == 0:
             pass_z(2)
+    for n in (2, 3, 4):
+        puts[n].start()
 
     finish(0)
     finish(1)
@@ -1278,6 +1286,8 @@
     halo.wait_send()
     for copy in copies:
         copy.wait_send()
+    for copy in puts:
+        copy.wait()
 
 
 def channel_backward(near, far, size):
@@ -1292,13 +1302,13 @@
     return pl.pallas_call(
         channel_backward_kernel,
         out_shape=[
-            jax.ShapeDtypeStruct((2, rows, width), BF),
-            jax.ShapeDtypeStruct((5, tokens, width), BF),
-            jax.ShapeDtypeStruct(flat_f32, F32), jax.ShapeDtypeStruct((16, width), F32),
+            jax.ShapeDtypeStruct((2, rows, width), BF), jax.ShapeDtypeStruct((16, width), F32),
+            jax.ShapeDtypeStruct((5, tokens, width), BF), jax.ShapeDtypeStruct(flat_f32, F32),
         ],
         in_specs=[whole()] * len(near) + [anywhere()] * len(far),
-        out_specs=[whole()] * 4,
+        out_specs=[whole()] * 2 + [anywhere()] * 2,
         scratch_shapes=[
+            pltpu.VMEM((5, tokens, width), BF), big,
             pltpu.VMEM((2, 4, rows, 2 * width), BF), pltpu.VMEM((2, 4, rows, tokens), F32),
             pltpu.VMEM((width, width), BF), pltpu.VMEM((width, width), BF),
         ]
@@ -1315,7 +1325,7 @@
             pltpu.VMEM((8, width), F32), pltpu.VMEM((8, width), F32),
             dma((2, 2)), dma((11,)), dma((4,)), dma((4,)), dma((2, 4)), dma((2, 4)), dma((4,)), dma((4,)),
             dma((4, 3)), dma((4, 3)),
-            dma((size,)), dma((size,)), dma((1,)), dma((1,)),
+            dma((size,)), dma((size,)), dma((1,)), dma((1,)), dma((6,)),
         ],
         compiler_params=pltpu.CompilerParams(
             collective_id=2, has_side_effects=True, vmem_limit_bytes=66_000_000
@@ -1486,7 +1496,7 @@
     )
     sums[DECAY : DECAY + 1, :] = -sums[DECAY : DECAY + 1, :] * rates[0:1, :] * vectors[DECAY : DECAY + 1, :]
 
-    stages = [[links.core], [links.over_x], [links.over_y], links.along_z]
+    stages = [[links.core], [links.over_x], [links.over_y]]
     pending = []
     source, slot = sums, 0
 
@@ -1522,10 +1532,26 @@
     last_over_core.start()
     finish(2)
     collect(copies, held.at[7], 2, held.at[8])
-    copies = begin(stages[3], held.at[8], 3)
+
+    def block(zz):
+        return pl.ds(pl.multiple_of((dp * 2 + zz // 2) * 128, 128), 128)
+
+    copies = []
+    for k, peer in enumerate(links.along_z):
+        at = block(lax.rem(z + k + 1, 4))
+        copies.append(
+            remote(held.at[8, :, at], held.at[3 + k, :, at], sum_send.at[3 + k], sum_recv.at[3 + k], peer)
+        )
+        copies[-1].start()
     pending += copies
     finish(3)
-    collect(copies, held.at[8], 3, vector_grads)
+    own_lanes = block(z)
+    value = held[8, :, own_lanes]
+    for k, copy in enumerate(copies):
+        copy.wait_recv()
+        value = value + held[3 + k, :, own_lanes]
+    vector_grads[...] = jnp.zeros_like(vector_grads)
+    vector_grads[:, own_lanes] = value
     finish(4)
     for copy in (units_over_core, last_over_core):
         copy.wait_recv()
@@ -1606,7 +1632,7 @@
     ]
     near = [feed_in, grad_value, grad_gate, table, keep_lanes, inverse_two, cotangent]
     far = [feed, positive, w_feedr, w_output, spread_two, unit_two, keys, values, denom, mixed, prior_a, prior_b, recept]
-    own_units, rights, grad_residual, sums = channel_backward(near, far, size)
+    own_units, sums, rights, grad_residual = channel_backward(near, far, size)
     near = [own_units, table, keep_lanes, inverse_one, sums, rates]
     far = [lefts, rights, grad_residual, w_key, w_value, w_recept, spread_one, unit_one]
     square_grads, units, token_grads, vector_grads = front_backward(near, far)

time: 340 us -> 335 us (0.985)
  Pallas kernels: 324 us -> 320 us
where the time goes in v7:
time: 335 us; the launch traced here: 333 us
  Pallas kernels  320 us (96%)
  local copies, waits for them, and re-layouts  8.97 us (3%)
    pallas_call x1, Pallas kernels, forward(): pl.pallas_call(forward_kernel, out_shape=[jax.ShapeDtypeStruct((2, 2, 4,...  149 us
    pallas_call x1, Pallas kernels, channel_backward(): pl.pallas_call(channel_backward_kernel, out_shape=[jax.ShapeDtypeStruct((...  97.9 us
    pallas_call x1, Pallas kernels, front_backward(): pl.pallas_call(front_backward_kernel, out_shape=[jax.ShapeDtypeStruct((co...  73.7 us

profile of v7, /device:TPU:0, one launch (start us, length us, event | category | flops | bytes accessed | tf_op | source)
XLA Modules:
  0.0 333.1 jit_solution(1997301248176726410)
XLA Ops:
  0.7 0.7 subtract_convert_fusion
  1.3 0.8 broadcast_in_dim.2.keep
  2.1 1.5 stack.47
  3.6 0.6 pad.4.own_vectors
  4.2 148.6 %forward.1 = (bf16[2,2,4,2,16,128]{5,4,3,2,1,0:T(8,128)(2,1)}, bf16[2,2,4,2,32,1024]{5,4,3,2,1,0:T(8,128)(2,1)}, bf16[2,2,4,2,32,1024]{5,4,3,2,1,0:T(8,128)(2,1)...) custom-call(bf16[256,1024]{1,0:T(8,128)(2,1)} %bitcast.81, ...), custom_call_target="tpu_custom_call" | custom-call | flops 5905580032 | bytes 60000000 | tf_op jit(solution)/shard_map/forward/pallas_call | solution.py:963
  152.8 97.9 %channel_backward.1 = (bf16[2,128,1024]{2,1,0:T(8,128)(2,1)}, f32[16,1024]{1,0:T(8,128)}, bf16[5,256,1024]{2,1,0:T(8,128)(2,1)}, f32[256,1024]{1,0:T(8,128)}) custom-call(bf16[256,1024]{1,0:T(8,128)(2,1)} %get-tuple-element.56.feed_in, bf16[256,1024]{1,0:T(8,128)(2,1)} %get-tuple-element.57.grad_value, bf16[256,1024]{1,0:T(8,128)(2,1)} %get-tuple-element.58.grad_gate, ...), custom_call_target="tpu_custom_call" | custom-call | flops 8589934592 | bytes 67108864 | tf_op jit(solution)/shard_map/channel_backward/pallas_call | solution.py:1302
  250.7 73.7 %front_backward.1 = (f32[5,32,1024]{2,1,0:T(8,128)}, bf16[4,2,128,1024]{3,2,1,0:T(8,128)(2,1)}, f32[256,1024]{1,0:T(8,128)}, f32[16,1024]{1,0:T(8,128)}) custom-call(bf16[2,128,1024]{2,1,0:T(8,128)(2,1)} %get-tuple-element.74.own_units, f32[16,1024]{1,0:T(8,128)} %get-tuple-element.59.vectors, f32[2,128,128]{2,1,0:T(8,128)} %broadcast_in_dim.2.keep, ...), custom_call_target="tpu_custom_call" | custom-call | flops 5368709120 | bytes 41943040 | tf_op jit(solution)/shard_map/front_backward/pallas_call | solution.py:1577
  324.4 1.7 fusion
  326.1 0.0 copy-start.2
  326.1 2.6 bitcast_convert_fusion
  328.7 0.0 copy-start
  328.7 0.0 copy-start.1
  328.7 0.0 copy-done.2
  328.7 0.8 slice_bitcast_fusion
  329.6 1.6 dynamic-slice_bitcast_fusion
  331.2 0.0 copy-done
  331.2 1.0 copy.45
  332.2 0.0 copy-done.1
  332.2 1.0 copy.46
Async XLA Ops:
  326.1 2.6 copy-start.2
  328.7 2.4 copy-start
  328.7 3.4 %copy-start.1 = (f32[256,1024]{1,0:T(8,128)S(1)}, f32[256,1024]{1,0:T(8,128)}, u32[]{:S(2)}) copy-start(f32[256,1024]{1,0:T(8,128)} %get-tuple-element.86) | copy-start | bytes 3145732
